TPU v7x, 32 devices: a whole 2x2x4 slice. The times are simulated.
32 devices in a mesh: gx: 16 (over z, y, core), gy: 2 (over x).
Axes of the slice: x: 2, y: 2, z: 4, core: 2. Of those that a mesh axis runs over, the one named last changes fastest.
Arguments:
- signal: float32 [45, 16, 16, 128], P(None, 'gx', 'gy'), may hold values from -6 to 6
- response: float32 [45], replicated, may hold values from 0.2 to 2
- basis: float32 [362, 45], replicated, may hold values from -0.875 to 0.875
- mask: int32 [16, 16, 128], P('gx', 'gy'), may hold values 0 or 1
- coefficients: float32 [45, 16, 16, 128], P(None, 'gx', 'gy'), may hold values from -6 to 6
- extrapolated: float32 [45, 16, 16, 128], P(None, 'gx', 'gy'), may hold values from -6 to 6
- dual_grad: float32 [3, 362, 16, 16, 128], P(None, None, 'gx', 'gy'), may hold values from -2 to 2
- dual_sign: float32 [362, 16, 16, 128], P(None, 'gx', 'gy'), may hold values from -1 to 0
Outputs:
- coefficients_out: float32 [45, 16, 16, 128], P(None, 'gx', 'gy')
- extrapolated_out: float32 [45, 16, 16, 128], P(None, 'gx', 'gy')
- dual_grad_out: float32 [3, 362, 16, 16, 128], P(None, None, 'gx', 'gy')
- dual_sign_out: float32 [362, 16, 16, 128], P(None, 'gx', 'gy')
Inputs may be any that keep to these rules, and one draw needn't show every extreme that they name: `mask`: 1 marks a voxel inside the brain.
All inputs are finite; a program needn't handle non-finite values. No bound on the sum of `mask` on one device may be relied on, other than what follows from the above.
Results may differ from a plain program's by a relative error of at most 0.0001.
Values sent between devices are 32-bit elements; how exact they have to be, the bound alone decides.
No kernel may reach another device: no remote copies, remote signals or barrier semaphores. Data moves between devices by JAX's collectives and lax.ppermute only.
A program may use at most 64 MiB of HBM per device.

v0:
```python
import jax
import jax.numpy as jnp
from jax import lax
from jax.sharding import PartitionSpec as P

ITERS = 2


STEP_PRIMAL = 0.25
STEP_DUAL = 0.02
TV_WEIGHT = 0.5


def from_behind(value, axis, steps):
    count = lax.axis_size(axis)
    leading, last = (max(0, -steps), min(count, count - steps))
    return lax.ppermute(value, axis, [(source, source + steps) for source in range(leading, last)])


def to_sphere(basis, coef_rows):
    count = coef_rows.shape[0]
    result = jnp.dot(
        basis,
        coef_rows.reshape(count, -1),
        precision=lax.Precision.HIGHEST,
        preferred_element_type=jnp.float32,
    )
    return result.reshape((basis.shape[0],) + coef_rows.shape[1:])


def to_harmonics(basis, amp_rows):
    count = amp_rows.shape[0]
    result = jnp.dot(
        basis.T,
        amp_rows.reshape(count, -1),
        precision=lax.Precision.HIGHEST,
        preferred_element_type=jnp.float32,
    )
    return result.reshape((basis.shape[1],) + amp_rows.shape[1:])


def forward_diff(field, along):
    length = field.shape[along]
    upper_part = lax.slice_in_dim(field, 1, length, axis=along)
    lower_part = lax.slice_in_dim(field, 0, length - 1, axis=along)
    zero_face = jnp.zeros_like(lax.slice_in_dim(field, 0, 1, axis=along))
    return jnp.concatenate([upper_part - lower_part, zero_face], along)


def backward_diff(dual_part, along):
    length = dual_part.shape[along]
    kept_rows = lax.slice_in_dim(dual_part, 0, length - 1, axis=along)
    zero_face = jnp.zeros_like(lax.slice_in_dim(dual_part, 0, 1, axis=along))
    masked = jnp.concatenate([kept_rows, zero_face], along)
    before = jnp.concatenate([zero_face, kept_rows], along)
    return masked - before


def keep_factor(field, is_last, along):
    length = field.shape[along]
    shape_now = [1] * field.ndim
    shape_now[along] = length
    position = lax.broadcasted_iota(jnp.int32, tuple(shape_now), along)
    dropped = jnp.logical_and(is_last, position == length - 1)
    return jnp.where(dropped, 0.0, 1.0).astype(jnp.float32)


def edge_diff(field, after_rows, is_last, along):
    length = field.shape[along]
    upper_part = jnp.concatenate(
        [lax.slice_in_dim(field, 1, length, axis=along), after_rows], along
    )
    return (upper_part - field) * keep_factor(field, is_last, along)


def zero_last(dual_part, is_last, along):
    return dual_part * keep_factor(dual_part, is_last, along)


def inner_div(masked, along):
    length = masked.shape[along]
    zero_face = jnp.zeros_like(lax.slice_in_dim(masked, 0, 1, axis=along))
    before = jnp.concatenate(
        [zero_face, lax.slice_in_dim(masked, 0, length - 1, axis=along)], along
    )
    return masked - before


def add_first(field, face_rows, along):
    length = field.shape[along]
    first_rows = lax.slice_in_dim(field, 0, 1, axis=along) + face_rows
    return jnp.concatenate([first_rows, lax.slice_in_dim(field, 1, length, axis=along)], along)


def last_face(field, along):
    length = field.shape[along]
    return lax.slice_in_dim(field, length - 1, length, axis=along)


def per_device(signal, response, basis, mask, coefficients, extrapolated, dual_grad, dual_sign):
    last_x = lax.axis_index("gx") == lax.axis_size("gx") - 1
    last_y = lax.axis_index("gy") == lax.axis_size("gy") - 1
    weight = mask.astype(jnp.float32)[None] * response[:, None, None, None]
    target = STEP_PRIMAL * weight * signal
    divisor = 1.0 + STEP_PRIMAL * weight * response[:, None, None, None]
    for iteration in range(ITERS):
        sphere_now = to_sphere(basis, extrapolated)
        after_x = to_sphere(basis, from_behind(extrapolated, "gx", -1))
        after_y = to_sphere(basis, from_behind(extrapolated[:, :, :1], "gy", -1))
        stepped_x = dual_grad[0] + STEP_DUAL * edge_diff(sphere_now, after_x, last_x, 1)
        stepped_y = dual_grad[1] + STEP_DUAL * edge_diff(sphere_now, after_y, last_y, 2)
        stepped_z = dual_grad[2] + STEP_DUAL * forward_diff(sphere_now, 3)
        magnitude = jnp.sqrt(stepped_x * stepped_x + stepped_y * stepped_y + stepped_z * stepped_z)
        shrink = jnp.maximum(1.0, magnitude / TV_WEIGHT)
        dual_grad = jnp.stack([stepped_x / shrink, stepped_y / shrink, stepped_z / shrink])
        dual_sign = jnp.minimum(0.0, dual_sign + STEP_DUAL * sphere_now)
        masked_x = zero_last(dual_grad[0], last_x, 1)
        masked_y = zero_last(dual_grad[1], last_y, 2)
        backward = dual_sign - (
            inner_div(masked_x, 1) + inner_div(masked_y, 2) + backward_diff(dual_grad[2], 3)
        )
        harmonic = to_harmonics(basis, backward)
        before_x = from_behind(to_harmonics(basis, last_face(masked_x, 1)), "gx", 1)
        before_y = from_behind(to_harmonics(basis, last_face(masked_y, 2)), "gy", 1)
        harmonic = add_first(add_first(harmonic, before_x, 1), before_y, 2)
        trial_step = coefficients - STEP_PRIMAL * harmonic
        updated = (trial_step + target) / divisor
        extrapolated = 2.0 * updated - coefficients
        coefficients = updated
    return (coefficients, extrapolated, dual_grad, dual_sign)


def solution(mesh):
    in_specs = (
        P(None, "gx", "gy", None),
        P(),
        P(),
        P("gx", "gy", None),
        P(None, "gx", "gy", None),
        P(None, "gx", "gy", None),
        P(None, None, "gx", "gy", None),
        P(None, "gx", "gy", None),
    )
    out_specs = (
        P(None, "gx", "gy", None),
        P(None, "gx", "gy", None),
        P(None, None, "gx", "gy", None),
        P(None, "gx", "gy", None),
    )
    return jax.shard_map(
        per_device, mesh=mesh, in_specs=in_specs, out_specs=out_specs, check_vma=False
    )
```

profile of v0, /device:TPU:8, one launch (start us, length us, event | category | flops | bytes accessed | tf_op | source)
XLA Modules:
  0.0 77.5 jit_solution(15770361541857060999)
XLA Ops:
  0.6 2.9 %collective-permute-start = (f32[45,1,8,128]{3,2,1,0:T(8,128)}, f32[45,1,8,128]{3,2,1,0:T(8,128)S(1)}, u32[]{:S(2)}, u32[]{:S(2)}) collective-permute-start(f32[45,1,8,128]{3,2,1,0:T(8,128)} %param.13), channel_id=1, source_target_pairs={{2,0},{4,2},{6,4},{8,6},{10,8},{12,10},{14,12},{16,14},{18,16},{20... | collective-permute-start | bytes 552968 | tf_op jit(solution)/shard_map/ppermute | solution.py:17
  3.5 0.9 %slice.68 = f32[45,1,1,128]{3,2,1,0:T(1,128)S(1)} slice(f32[45,1,8,128]{3,2,1,0:T(8,128)} %param.13), slice={[0:45], [0:1], [0:1], [0:128]} | slice | bytes 46080 | tf_op jit(solution)/shard_map/slice | solution.py:109
  4.5 1.3 %collective-permute-start.1 = (f32[45,1,1,128]{3,0,2,1:T(8,128)S(1)}, f32[45,1,1,128]{3,0,2,1:T(8,128)S(1)}, u32[]{:S(2)}, u32[]{:S(2)}) collective-permute-start(f32[45,1,1,128]{3,0,2,1:T(8,128)S(1)} %copy.71), channel_id=1, source_target_pairs={{1,0},{3,2},{5,4},{7,6},{9,8},{11,10},{13,12},{15,14},{17,16},{19,... | collective-permute-start | bytes 69128 | tf_op jit(solution)/shard_map/ppermute | solution.py:17
  5.8 0.9 %pad.21 = f32[48,8,128]{2,1,0:T(8,128)S(1)} pad(f32[45,8,128]{2,1,0:T(8,128)} %bitcast.243, f32[]{:T(128)} %constant.12.clone.1), padding=0_3x0_0x0_0 | pad | bytes 380932
  6.8 1.4 %fusion.46 = f32[362,1024]{1,0:T(8,128)S(1)} fusion(f32[362,45]{0,1:T(8,128)S(1)} %copy-done, f32[45,1024]{1,0:T(8,128)S(1)} %bitcast.227), kind=kOutput, calls=%fused_computation.95 | convolution fusion | flops 200171520 | bytes 1732232 | tf_op jit(solution)/shard_map/dot_general | solution.py:22
  8.2 0.3 copy.74
  8.5 1.3 %fusion.45 = (f32[362,8,128]{2,1,0:T(8,128)}, f32[362,1,8,128]{3,2,0,1:T(8,128)S(1)}) fusion(f32[368,8,128]{2,1,0:T(8,128)S(1)} %bitcast.220), kind=kLoop, calls=%fused_computation.94 | loop fusion | bytes 4448256
  10.1 0.5 slice_subtract_fusion.1
  10.6 1.7 %slice_bitcast_fusion.11 = (f32[362,7,128]{2,0,1:T(8,128)}, f32[362,1,7,128]{3,0,2,1:T(8,128)}) fusion(f32[362,1,8,128]{3,0,2,1:T(8,128)S(1)} %copy.32), kind=kLoop, calls=%fused_computation.89 | loop fusion | bytes 3892224 | tf_op jit(solution)/shard_map/concatenate | solution.py:70
  12.3 4.4 %fusion.44 = (f32[1,362,1,8,128]{4,3,2,1,0:T(8,128)}, f32[1,362,1,8,128]{4,3,2,1,0:T(8,128)}, f32[1,362,1,8,128]{4,3,2,1,0:T(8,128)}) fusion(f32[3,362,1,8,128]{4,3,2,1,0:T(8,128)} %param.14), kind=kLoop, calls=%fused_computation.93 | loop fusion | bytes 8896512 | tf_op jit(solution)/shard_map/slice | solution.py:110
  16.8 0.5 fusion.36
  17.3 6.8 %broadcast_multiply_fusion.1 = (f32[362,1,8,128]{3,0,2,1:T(8,128)S(1)}, f32[362,1,8,128]{3,0,2,1:T(8,128)S(1)}, f32[362,1,8,128]{3,0,2,1:T(8,128)S(1)}, f32[362,8,128]{2,0,1:T(8,128)S(1)}) fusion(f32[8]{0:T(128)S(1)} %and_select_fusion, f32[362,1,8,128]{3,2,0,1:T(8,128)S(1)} %get-tuple-element.37, f32[362,1,1,128]{3,0,2,1:T(8,128)S(1)} %bitcast.225, ...), kind=kOutput, calls=%fused_computation.49 | convolution fusion | flops 209438720 | bytes 18030956 | tf_op jit(solution)/shard_map/dot_general | solution.py:22
  24.4 1.0 %copy-done.2 = f32[1,362,1,8,128]{4,3,2,1,0:T(8,128)S(1)} copy-done((f32[1,362,1,8,128]{4,3,2,1,0:T(8,128)S(1)}, f32[1,362,1,8,128]{4,3,2,1,0:T(8,128)}, u32[]{:S(2)}) %copy-start.2) | copy-done | bytes 1482776
  25.5 0.5 fusion.24
  26.0 4.5 %collective-permute-start.3 = (f32[45,1,1,128]{3,0,2,1:T(8,128)S(1)}, f32[45,1,1,128]{3,0,2,1:T(8,128)S(1)}, u32[]{:S(2)}, u32[]{:S(2)}) collective-permute-start(f32[45,1,1,128]{3,0,2,1:T(8,128)S(1)} %convolution_bitcast_fusion.2), channel_id=1, source_target_pairs={{0,1},{2,3},{4,5},{6,7},{8,9},{10,11},{12,13},{14,15},{16,17},{18,... | collective-permute-start | bytes 69128 | tf_op jit(solution)/shard_map/ppermute | solution.py:17
  30.6 1.4 %add_subtract_fusion.1 = (f32[362,1,8,128]{3,0,2,1:T(8,128)S(1)}, f32[362,1,8,128]{3,0,2,1:T(8,128)S(1)}) fusion(f32[362,1,8,127]{3,0,2,1:T(8,128)S(1)} %bitcast.206, f32[362,1,8,128]{3,0,2,1:T(8,128)S(1)} %fusion.24, f32[362,1,8,128]{3,0,2,1:T(8,128)S(1)} %get-tuple-element.25, f32[362,1,7,128]{3,0,2,1:T(8,128)S(1)} %slice.89, ...), kind=kLoop, calls=%fused_computation.38 | loop fusion | flops 4077568 | bytes 14630724 | tf_op jit(solution)/shard_map/sub | solution.py:119
  31.9 0.9 %copy_bitcast_fusion.4 = (f32[362,8,128]{2,1,0:T(8,128)S(1)}, f32[362,8,128]{2,1,0:T(8,128)S(1)}) fusion(f32[362,1,8,128]{3,0,2,1:T(8,128)S(1)} %get-tuple-element.24, f32[362,1,8,128]{3,0,2,1:T(8,128)S(1)} %get-tuple-element.23), kind=kLoop, calls=%fused_computation.43 | loop fusion | bytes 5931008
  32.9 0.3 copy.80
  33.2 1.1 %fusion.48 = f32[1024,45]{0,1:T(8,128)S(1)} fusion(f32[362,1024]{1,0:T(8,128)S(1)} %bitcast.212, f32[362,45]{0,1:T(8,128)S(1)} %copy-done), kind=kOutput, calls=%fused_computation.97 | convolution fusion | flops 200171520 | bytes 1732232 | tf_op jit(solution)/shard_map/dot_general | solution.py:33
  34.5 2.1 %collective-permute-start.2 = (f32[45,1,8,128]{3,0,2,1:T(8,128)S(1)}, f32[45,1,8,128]{3,0,2,1:T(8,128)S(1)}, u32[]{:S(2)}, u32[]{:S(2)}) collective-permute-start(f32[45,1,8,128]{3,0,2,1:T(8,128)S(1)} %copy.47), channel_id=1, source_target_pairs={{0,2},{2,4},{4,6},{6,8},{8,10},{10,12},{12,14},{14,16},{16,18},{18... | collective-permute-start | bytes 552968 | tf_op jit(solution)/shard_map/ppermute | solution.py:17
  36.7 0.3 copy.78
  37.1 1.1 %fusion.47 = f32[1024,45]{0,1:T(8,128)S(1)} fusion(f32[362,1024]{1,0:T(8,128)S(1)} %bitcast.214, f32[362,45]{0,1:T(8,128)S(1)} %copy-done), kind=kOutput, calls=%fused_computation.96 | convolution fusion | flops 200171520 | bytes 1732232 | tf_op jit(solution)/shard_map/dot_general | solution.py:33
  38.3 4.1 %collective-permute-done.2 = f32[45,1,8,128]{3,0,2,1:T(8,128)S(1)} collective-permute-done((f32[45,1,8,128]{3,0,2,1:T(8,128)S(1)}, f32[45,1,8,128]{3,0,2,1:T(8,128)S(1)}, u32[]{:S(2)}, u32[]{:S(2)}) %collective-permute-start.2) | collective-permute-done | bytes 184352 | tf_op jit(solution)/shard_map/ppermute | solution.py:17
  42.8 1.9 %collective-permute-start.4 = (f32[45,1,8,128]{3,0,2,1:T(8,128)S(1)}, f32[45,1,8,128]{3,0,2,1:T(8,128)S(1)}, u32[]{:S(2)}, u32[]{:S(2)}) collective-permute-start(f32[45,1,8,128]{3,0,2,1:T(8,128)S(1)} %get-tuple-element.21), channel_id=1, source_target_pairs={{2,0},{4,2},{6,4},{8,6},{10,8},{12,10},{14,12},{16,14},{18,16},{20... | collective-permute-start | bytes 552968 | tf_op jit(solution)/shard_map/ppermute | solution.py:17
  44.7 1.3 %collective-permute-start.5 = (f32[45,1,1,128]{3,0,2,1:T(8,128)S(1)}, f32[45,1,1,128]{3,0,2,1:T(8,128)S(1)}, u32[]{:S(2)}, u32[]{:S(2)}) collective-permute-start(f32[45,1,1,128]{3,0,2,1:T(8,128)S(1)} %slice.95), channel_id=1, source_target_pairs={{1,0},{3,2},{5,4},{7,6},{9,8},{11,10},{13,12},{15,14},{17,16},{19,... | collective-permute-start | bytes 69128 | tf_op jit(solution)/shard_map/ppermute | solution.py:17
  46.1 1.4 %fusion.49 = f32[1024,362]{0,1:T(8,128)S(1)} fusion(f32[45,1024]{1,0:T(8,128)S(1)} %bitcast.230, f32[362,45]{0,1:T(8,128)S(1)} %copy-done), kind=kOutput, calls=%fused_computation.98 | convolution fusion | flops 200171520 | bytes 1732232 | tf_op jit(solution)/shard_map/dot_general | solution.py:22
  48.2 0.5 slice_subtract_fusion
  48.7 0.7 copy-done.1
  49.3 1.1 %collective-permute-done.5 = f32[45,1,1,128]{3,0,2,1:T(8,128)S(1)} collective-permute-done((f32[45,1,1,128]{3,0,2,1:T(8,128)S(1)}, f32[45,1,1,128]{3,0,2,1:T(8,128)S(1)}, u32[]{:S(2)}, u32[]{:S(2)}) %collective-permute-start.5) | collective-permute-done | bytes 23072 | tf_op jit(solution)/shard_map/ppermute | solution.py:17
  50.4 0.5 convolution_bitcast_fusion
  51.1 1.4 %fusion.50 = f32[1024,362]{0,1:T(8,128)S(1)} fusion(f32[45,1024]{1,0:T(8,128)S(1)} %bitcast.231, f32[362,45]{0,1:T(8,128)S(1)} %copy-done), kind=kOutput, calls=%fused_computation.99 | convolution fusion | flops 200171520 | bytes 1732232 | tf_op jit(solution)/shard_map/dot_general | solution.py:22
  52.4 0.3 copy.85
  52.9 1.2 %slice-done = f32[362,1,7,128]{3,0,2,1:T(8,128)S(1)} async-done(((f32[362,1,8,128]{3,0,2,1:T(8,128)}), f32[362,1,7,128]{3,0,2,1:T(8,128)S(1)}, s32[]{:S(2)}) %slice-start) | async-done | bytes 1297432 | tf_op jit(solution)/shard_map/slice | solution.py:71
  54.1 1.7 %divide_bitcast_fusion.1 = (f32[1,362,1,8,128]{4,1,3,2,0:T(8,128)S(1)}, f32[362,1,8,128]{3,0,2,1:T(8,128)S(1)}, f32[362,1,8,128]{3,0,2,1:T(8,128)S(1)}, f32[362,1,8,128]{3,0,2,1:T(8,128)S(1)}) fusion(f32[362,1,8,128]{3,0,2,1:T(8,128)S(1)} %fusion.24, f32[362,1,8,127]{3,0,2,1:T(8,128)S(1)} %slice_subtract_fusion, ...), kind=kLoop, calls=%fused_computation.92 | loop fusion | flops 7413760 | bytes 17781476 | tf_op jit(solution)/shard_map/stack | solution.py:115
  55.8 0.5 divide_bitcast_fusion
  56.6 3.8 %collective-permute-start.7 = (f32[45,1,1,128]{3,0,2,1:T(8,128)S(1)}, f32[45,1,1,128]{3,0,2,1:T(8,128)S(1)}, u32[]{:S(2)}, u32[]{:S(2)}) collective-permute-start(f32[45,1,1,128]{3,0,2,1:T(8,128)S(1)} %convolution_bitcast_fusion.1), channel_id=1, source_target_pairs={{0,1},{2,3},{4,5},{6,7},{8,9},{10,11},{12,13},{14,15},{16,17},{18,... | collective-permute-start | bytes 69128 | tf_op jit(solution)/shard_map/ppermute | solution.py:17
  60.4 1.7 %add_subtract_fusion = (f32[362,1,8,128]{3,0,2,1:T(8,128)S(1)}, f32[362,1,8,128]{3,0,2,1:T(8,128)S(1)}, f32[362,1,8,128]{3,0,2,1:T(8,128)S(1)}) fusion(f32[362,1,8,127]{3,0,2,1:T(8,128)S(1)} %bitcast.207, f32[362,1,8,128]{3,0,2,1:T(8,128)S(1)} %get-tuple-element.33, f32[362,1,8,128]{3,0,2,1:T(8,128)S(1)} %get-tuple-element.32, ...), kind=kLoop, calls=%fused_computation.34 | loop fusion | flops 5189632 | bytes 17596228 | tf_op jit(solution)/shard_map/sub | solution.py:119
  62.1 0.5 copy.158
  63.0 1.1 %fusion.51 = f32[1024,45]{0,1:T(8,128)S(1)} fusion(f32[362,1024]{1,0:T(8,128)S(1)} %bitcast.218, f32[362,45]{0,1:T(8,128)S(1)} %copy-done), kind=kOutput, calls=%fused_computation.100 | convolution fusion | flops 200171520 | bytes 1732232 | tf_op jit(solution)/shard_map/dot_general | solution.py:33
  64.2 1.6 %copy.68 = f32[362,1,8,128]{3,2,1,0:T(8,128)} copy(f32[362,1,8,128]{3,0,2,1:T(8,128)S(1)} %get-tuple-element.19) | data formatting | bytes 2965504
  65.7 0.5 copy.157
  66.6 1.1 %fusion.52 = f32[1024,45]{0,1:T(8,128)S(1)} fusion(f32[362,1024]{1,0:T(8,128)S(1)} %bitcast.219, f32[362,45]{0,1:T(8,128)S(1)} %copy-done), kind=kOutput, calls=%fused_computation.101 | convolution fusion | flops 200171520 | bytes 1732232 | tf_op jit(solution)/shard_map/dot_general | solution.py:33
  67.9 1.9 %collective-permute-start.6 = (f32[45,1,8,128]{3,0,2,1:T(8,128)S(1)}, f32[45,1,8,128]{3,0,2,1:T(8,128)S(1)}, u32[]{:S(2)}, u32[]{:S(2)}) collective-permute-start(f32[45,1,8,128]{3,0,2,1:T(8,128)S(1)} %copy.63), channel_id=1, source_target_pairs={{0,2},{2,4},{4,6},{6,8},{8,10},{10,12},{12,14},{14,16},{16,18},{18... | collective-permute-start | bytes 552968 | tf_op jit(solution)/shard_map/ppermute | solution.py:17
  69.8 0.5 pad_maximum_fusion
  70.3 3.4 %copy.67 = f32[3,362,1,8,128]{4,3,2,1,0:T(8,128)} copy(f32[3,362,1,8,128]{4,1,3,2,0:T(8,128)S(1)} %pad_maximum_fusion) | data formatting | bytes 8896512
  73.7 2.0 %collective-permute-done.6 = f32[45,1,8,128]{3,0,2,1:T(8,128)S(1)} collective-permute-done((f32[45,1,8,128]{3,0,2,1:T(8,128)S(1)}, f32[45,1,8,128]{3,0,2,1:T(8,128)S(1)}, u32[]{:S(2)}, u32[]{:S(2)}) %collective-permute-start.6) | collective-permute-done | bytes 184352 | tf_op jit(solution)/shard_map/ppermute | solution.py:17
  76.1 0.7 copy.66
  76.8 0.7 copy.65
  (70 shorter events, 3.9 us)
Async XLA Ops:
  0.6 6.2 %copy-start = (f32[362,45]{0,1:T(8,128)S(1)}, f32[362,45]{0,1:T(8,128)}, u32[]{:S(2)}) copy-start(f32[362,45]{0,1:T(8,128)} %param.10) | copy-start | bytes 195484
  0.6 16.6 %collective-permute-start = (f32[45,1,8,128]{3,2,1,0:T(8,128)}, f32[45,1,8,128]{3,2,1,0:T(8,128)S(1)}, u32[]{:S(2)}, u32[]{:S(2)}) collective-permute-start(f32[45,1,8,128]{3,2,1,0:T(8,128)} %param.13), channel_id=1, source_target_pairs={{2,0},{4,2},{6,4},{8,6},{10,8},{12,10},{14,12},{16,14},{18,16},{20... | collective-permute-start | bytes 552968 | tf_op jit(solution)/shard_map/ppermute | solution.py:17
  4.5 12.3 %collective-permute-start.1 = (f32[45,1,1,128]{3,0,2,1:T(8,128)S(1)}, f32[45,1,1,128]{3,0,2,1:T(8,128)S(1)}, u32[]{:S(2)}, u32[]{:S(2)}) collective-permute-start(f32[45,1,1,128]{3,0,2,1:T(8,128)S(1)} %copy.71), channel_id=1, source_target_pairs={{1,0},{3,2},{5,4},{7,6},{9,8},{11,10},{13,12},{15,14},{17,16},{19,... | collective-permute-start | bytes 69128 | tf_op jit(solution)/shard_map/ppermute | solution.py:17
  10.6 1.7 %copy-start.8 = (f32[45]{0:T(128)S(1)}, f32[45]{0:T(128)}, u32[]{:S(2)}) copy-start(f32[45]{0:T(128)} %param.9) | copy-start | bytes 544
  10.6 1.7 %copy-start.7 = (s32[1,8,128]{2,1,0:T(8,128)S(1)}, s32[1,8,128]{2,1,0:T(8,128)}, u32[]{:S(2)}) copy-start(s32[1,8,128]{2,1,0:T(8,128)} %param.11) | copy-start | bytes 12292
  24.1 1.4 %copy-start.2 = (f32[1,362,1,8,128]{4,3,2,1,0:T(8,128)S(1)}, f32[1,362,1,8,128]{4,3,2,1,0:T(8,128)}, u32[]{:S(2)}) copy-start(f32[1,362,1,8,128]{4,3,2,1,0:T(8,128)} %get-tuple-element.30) | copy-start | bytes 4448260
  25.5 5.1 %copy-start.3 = (f32[362,1,8,128]{3,2,1,0:T(8,128)S(1)}, f32[362,1,8,128]{3,2,1,0:T(8,128)}, u32[]{:S(2)}) copy-start(f32[362,1,8,128]{3,2,1,0:T(8,128)} %param.15) | copy-start | bytes 4448260
  25.5 5.1 %copy-start.9 = (pred[128]{0:T(512)(128)(4,1)S(1)}, pred[128]{0:T(512)(128)(4,1)}, u32[]{:S(2)}) copy-start(pred[128]{0:T(512)(128)(4,1)} %constant.37.clone.1) | copy-start | bytes 388
  26.0 16.5 %collective-permute-start.3 = (f32[45,1,1,128]{3,0,2,1:T(8,128)S(1)}, f32[45,1,1,128]{3,0,2,1:T(8,128)S(1)}, u32[]{:S(2)}, u32[]{:S(2)}) collective-permute-start(f32[45,1,1,128]{3,0,2,1:T(8,128)S(1)} %convolution_bitcast_fusion.2), channel_id=1, source_target_pairs={{0,1},{2,3},{4,5},{6,7},{8,9},{10,11},{12,13},{14,15},{16,17},{18,... | collective-permute-start | bytes 69128 | tf_op jit(solution)/shard_map/ppermute | solution.py:17
  34.5 7.9 %collective-permute-start.2 = (f32[45,1,8,128]{3,0,2,1:T(8,128)S(1)}, f32[45,1,8,128]{3,0,2,1:T(8,128)S(1)}, u32[]{:S(2)}, u32[]{:S(2)}) collective-permute-start(f32[45,1,8,128]{3,0,2,1:T(8,128)S(1)} %copy.47), channel_id=1, source_target_pairs={{0,2},{2,4},{4,6},{6,8},{8,10},{10,12},{12,14},{14,16},{16,18},{18... | collective-permute-start | bytes 552968 | tf_op jit(solution)/shard_map/ppermute | solution.py:17
  37.0 5.4 %copy-start.5 = (f32[45,1,8,128]{3,2,1,0:T(8,128)S(1)}, f32[45,1,8,128]{3,2,1,0:T(8,128)}, u32[]{:S(2)}) copy-start(f32[45,1,8,128]{3,2,1,0:T(8,128)} %param.8) | copy-start | bytes 552964
  37.0 5.4 %copy-start.6 = (f32[45,1,8,128]{3,2,1,0:T(8,128)S(1)}, f32[45,1,8,128]{3,2,1,0:T(8,128)}, u32[]{:S(2)}) copy-start(f32[45,1,8,128]{3,2,1,0:T(8,128)} %param.12) | copy-start | bytes 552964
  42.8 8.1 %collective-permute-start.4 = (f32[45,1,8,128]{3,0,2,1:T(8,128)S(1)}, f32[45,1,8,128]{3,0,2,1:T(8,128)S(1)}, u32[]{:S(2)}, u32[]{:S(2)}) collective-permute-start(f32[45,1,8,128]{3,0,2,1:T(8,128)S(1)} %get-tuple-element.21), channel_id=1, source_target_pairs={{2,0},{4,2},{6,4},{8,6},{10,8},{12,10},{14,12},{16,14},{18,16},{20... | collective-permute-start | bytes 552968 | tf_op jit(solution)/shard_map/ppermute | solution.py:17
  44.7 5.7 %collective-permute-start.5 = (f32[45,1,1,128]{3,0,2,1:T(8,128)S(1)}, f32[45,1,1,128]{3,0,2,1:T(8,128)S(1)}, u32[]{:S(2)}, u32[]{:S(2)}) collective-permute-start(f32[45,1,1,128]{3,0,2,1:T(8,128)S(1)} %slice.95), channel_id=1, source_target_pairs={{1,0},{3,2},{5,4},{7,6},{9,8},{11,10},{13,12},{15,14},{17,16},{19,... | collective-permute-start | bytes 69128 | tf_op jit(solution)/shard_map/ppermute | solution.py:17
  48.2 1.1 %copy-start.1 = (f32[362,1,8,128]{3,0,2,1:T(8,128)}, f32[362,1,8,128]{3,0,2,1:T(8,128)S(1)}, u32[]{:S(2)}) copy-start(f32[362,1,8,128]{3,0,2,1:T(8,128)S(1)} %copy.53) | copy-start | bytes 4448260
  52.8 1.3 %slice-start = ((f32[362,1,8,128]{3,0,2,1:T(8,128)}), f32[362,1,7,128]{3,0,2,1:T(8,128)S(1)}, s32[]{:S(2)}) async-start(f32[362,1,8,128]{3,0,2,1:T(8,128)} %copy-done.1), calls=%async_computation | async-start | bytes 2637824 | tf_op jit(solution)/shard_map/slice | solution.py:71
  56.2 4.2 %copy-start.4 = (f32[362,1,8,128]{3,2,1,0:T(8,128)S(1)}, f32[362,1,8,128]{3,2,1,0:T(8,128)}, u32[]{:S(2)}) copy-start(f32[362,1,8,128]{3,2,1,0:T(8,128)} %param.15) | copy-start | bytes 4448260
  56.6 19.3 %collective-permute-start.7 = (f32[45,1,1,128]{3,0,2,1:T(8,128)S(1)}, f32[45,1,1,128]{3,0,2,1:T(8,128)S(1)}, u32[]{:S(2)}, u32[]{:S(2)}) collective-permute-start(f32[45,1,1,128]{3,0,2,1:T(8,128)S(1)} %convolution_bitcast_fusion.1), channel_id=1, source_target_pairs={{0,1},{2,3},{4,5},{6,7},{8,9},{10,11},{12,13},{14,15},{16,17},{18,... | collective-permute-start | bytes 69128 | tf_op jit(solution)/shard_map/ppermute | solution.py:17
  67.9 7.9 %collective-permute-start.6 = (f32[45,1,8,128]{3,0,2,1:T(8,128)S(1)}, f32[45,1,8,128]{3,0,2,1:T(8,128)S(1)}, u32[]{:S(2)}, u32[]{:S(2)}) collective-permute-start(f32[45,1,8,128]{3,0,2,1:T(8,128)S(1)} %copy.63), channel_id=1, source_target_pairs={{0,2},{2,4},{4,6},{6,8},{8,10},{10,12},{12,14},{14,16},{16,18},{18... | collective-permute-start | bytes 552968 | tf_op jit(solution)/shard_map/ppermute | solution.py:17
where the time goes:
time: 77.9 us; the launch traced here: 77.5 us
  local copies, waits for them, and re-layouts  24.8 us (32%)
  starting transfers between devices  19.7 us (25%)
  matrix products  16.9 us (22%)
  other arithmetic  7.52 us (10%)
  waiting for transfers between devices  7.3 us (9%)
  between operations  1.29 us (2%)
    ppermute x8, starting transfers between devices, from_behind(): lax.ppermute(value, axis, [(source, source + steps) for source in range(l...  19.7 us
    unnamed x48, local copies, waits for them, and re-layouts  14.2 us
    dot_general x6, matrix products, to_sphere(): jnp.dot(basis, coef_rows.reshape(count, -1), precision=lax.Precision.HIGH...  11.9 us
    ppermute x8, waiting for transfers between devices, from_behind(): lax.ppermute(value, axis, [(source, source + steps) for source in range(l...  7.3 us
    dot_general x6, matrix products, to_harmonics(): jnp.dot(basis.T, amp_rows.reshape(count, -1), precision=lax.Precision.HIG...  5.04 us
    slice x1, local copies, waits for them, and re-layouts, per_device(): dual_grad[0] + STEP_DUAL * edge_diff(sphere_now, after_x, last_x, 1)  4.45 us
    sub x2, other arithmetic, per_device(): dual_sign - (inner_div(masked_x, 1) + inner_div(masked_y, 2) + backward_d...  3.02 us
    another operation x3, other arithmetic, per_device(): jnp.stack([stepped_x / shrink, stepped_y / shrink, stepped_z / shrink])  2.6 us
  transfers between devices with their start and end apart: 8, of which 3 were waited for; matrix products, arithmetic and copies ran while one was open for 42% of the time, Pallas kernels for 0%

commit v1 on v0

v1 whole, which is shorter than its diff:
```python
import functools

import jax
import jax.numpy as jnp
from jax import lax
from jax.experimental import pallas as pl
from jax.experimental.pallas import tpu as pltpu
from jax.sharding import PartitionSpec as P

STEP_PRIMAL = 0.25
STEP_DUAL = 0.02
TV_WEIGHT = 0.5

F32 = jnp.float32
BF16 = jnp.bfloat16
VMEM_LIMIT = 24 * 1024 * 1024
GROUP = 16
LANES = 128


def round_up(value, unit):
    return -(-value // unit) * unit


def split_two(value):
    high = value.astype(BF16)
    low = (value - high.astype(F32)).astype(BF16)
    return high, low


def put_cat(cat_ref, value, low_row):
    rows, width = value.shape
    high, low = split_two(value)
    cat_ref[0:rows, 0:width] = high
    cat_ref[rows : 2 * rows, 0:width] = high
    cat_ref[low_row : low_row + rows, 0:width] = low


def planes_of(ref, count, rows, padded):
    parts = []
    for row in range(rows):
        part = ref[pl.ds(row, count, stride=rows), :]
        parts.append(jnp.concatenate([part, jnp.zeros((padded - count, part.shape[1]), F32)], 0))
    return jnp.concatenate(parts, 1)


def matmul(left, right):
    return jnp.dot(left, right, preferred_element_type=F32)


def wide_matmul(left_ref, right_ref, out_ref, width):
    for start in range(0, width, 256):
        size = min(256, width - start)
        out_ref[:, start : start + size] = matmul(left_ref[...], right_ref[:, start : start + size])


def harmonics(adjoint_ref, high_ref, low_ref, start, size, padded):
    first = matmul(adjoint_ref[...], high_ref[:, start : start + size])
    second = matmul(adjoint_ref[0:padded, :], low_ref[:, start : start + size])
    return first[0:padded] + first[padded : 2 * padded] + second


def all_harmonics(adjoint_ref, high_ref, low_ref, width, padded):
    parts = [
        harmonics(adjoint_ref, high_ref, low_ref, start, min(256, width - start), padded)
        for start in range(0, width, 256)
    ]
    return jnp.concatenate(parts, 1)


def last_flags():
    last_x = lax.axis_index("gx") == lax.axis_size("gx") - 1
    last_y = lax.axis_index("gy") == lax.axis_size("gy") - 1
    keep_x = jnp.where(last_x, 0.0, 1.0).astype(F32)
    keep_y = jnp.where(last_y, 0.0, 1.0).astype(F32)
    return keep_x, keep_y


def lane_edge():
    lane = lax.broadcasted_iota(jnp.int32, (GROUP, LANES), 1)
    return jnp.where(lane == LANES - 1, 0.0, 1.0).astype(F32)


def shrunk(step_x, step_y, step_z):
    square = step_x * step_x + step_y * step_y + step_z * step_z
    factor = TV_WEIGHT * lax.rsqrt(jnp.maximum(square, TV_WEIGHT * TV_WEIGHT))
    return step_x * factor, step_y * factor, step_z * factor


def next_lane(value):
    return pltpu.roll(value, LANES - 1, 1)


def previous_lane(value):
    return pltpu.roll(value, 1, 1)


class Shape:
    def __init__(self, directions, count, rows, lanes):
        assert lanes == LANES
        self.directions, self.count, self.rows = directions, count, rows
        self.padded_dirs = round_up(directions, GROUP)
        self.padded = round_up(count + 1, GROUP)
        self.width = rows * lanes
        self.low_row = round_up(2 * self.padded, LANES)
        self.depth = self.low_row + self.padded


def load_kernel(s, e_ref, basis_ref, response_ref, grad_ref, sign_ref,
                dual_ref, own_ref, cat_ref, adjoint_ref, column_ref,
                basis_in, response_in, padded_ref, e_cat, amp, sems):
    first = [
        pltpu.make_async_copy(basis_ref, basis_in, sems.at[4 * s.rows]),
        pltpu.make_async_copy(response_ref, response_in, sems.at[4 * s.rows + 1]),
        pltpu.make_async_copy(e_ref, own_ref, sems.at[4 * s.rows + 2]),
    ]
    for copy in first:
        copy.start()
    copies = []
    pad_rows = s.padded_dirs - s.directions
    for part in range(4):
        if pad_rows:
            dual_ref[part, :, s.directions :, :] = jnp.zeros((s.rows, pad_rows, LANES), F32)
    for row in range(s.rows):
        for part in (3, 1, 2, 0):
            source = sign_ref.at[:, 0, row] if part == 3 else grad_ref.at[part, :, 0, row]
            copies.append(pltpu.make_async_copy(
                source, dual_ref.at[part, row, pl.ds(0, s.directions)],
                sems.at[part * s.rows + row]))
    for copy in copies:
        copy.start()

    padded_ref[...] = jnp.zeros_like(padded_ref)
    for copy in first:
        copy.wait()
    padded_ref[0 : s.count, 0 : s.directions] = basis_in[...]
    whole = padded_ref[...]
    high, low = split_two(whole)
    adjoint_ref[0 : s.padded, :] = high[0 : s.padded, 0 : s.padded_dirs]
    adjoint_ref[s.padded : 2 * s.padded, :] = low[0 : s.padded, 0 : s.padded_dirs]
    high = high.astype(F32).T[0 : s.padded_dirs]
    low = low.astype(F32).T[0 : s.padded_dirs]
    cat_ref[:, 0:LANES] = (high + pltpu.roll(low, s.padded, 1)).astype(BF16)
    cat_ref[:, s.low_row : s.low_row + s.padded] = high[:, 0 : s.padded].astype(BF16)
    row_index = lax.broadcasted_iota(jnp.int32, (s.padded, LANES), 0)
    lane_index = lax.broadcasted_iota(jnp.int32, (s.padded, LANES), 1)
    spread = jnp.concatenate([response_in[...], jnp.zeros((1, LANES - s.count), F32)], 1)
    picked = jnp.where(row_index == lane_index, spread, 0.0)
    column_ref[...] = jnp.broadcast_to(jnp.sum(picked, 1, keepdims=True), (s.padded, LANES))

    e_cat[...] = jnp.zeros_like(e_cat)
    put_cat(e_cat, planes_of(own_ref, s.count, s.rows, s.padded) * STEP_DUAL, s.low_row)
    wide_matmul(cat_ref, e_cat, amp, s.width)
    for copy in copies:
        copy.wait()
    edge = lane_edge()

    def step(index, carry):
        here = pl.ds(pl.multiple_of(index * GROUP, GROUP), GROUP)
        values = [amp[here, row * LANES : (row + 1) * LANES] for row in range(s.rows)]
        for row in range(s.rows):
            if row + 1 < s.rows:
                dual_ref[1, row, here, :] += values[row + 1] - values[row]
            dual_ref[2, row, here, :] += (next_lane(values[row]) - values[row]) * edge
            dual_ref[3, row, here, :] = jnp.minimum(0.0, dual_ref[3, row, here, :] + values[row])
        return carry

    lax.fori_loop(0, s.padded_dirs // GROUP, step, 0)


def dual_pass(s, dual_in, dual_out, diff, amp, keep_y, highs):
    edge = lane_edge()
    back_high, back_low, x_high, x_low, y_high, y_low = highs

    def step(index, carry):
        here = pl.ds(pl.multiple_of(index * GROUP, GROUP), GROUP)
        before = None
        if amp is not None:
            value = amp[here, 0:LANES]
        for row in range(s.rows):
            at = slice(row * LANES, (row + 1) * LANES)
            step_x = dual_in[0, row, here, :] + diff[here, at]
            step_y, step_z, sign = dual_in[1, row, here, :], dual_in[2, row, here, :], dual_in[3, row, here, :]
            if row + 1 == s.rows:
                step_y = step_y + diff[here, s.width : s.width + LANES]
            if amp is not None:
                step_z = step_z + (next_lane(value) - value) * edge
                sign = jnp.minimum(0.0, sign + value)
                dual_out[3, row, here, :] = sign
                if row + 1 < s.rows:
                    after = amp[here, (row + 1) * LANES : (row + 2) * LANES]
                    step_y = step_y + (after - value)
                    value = after
            new_x, new_y, new_z = shrunk(step_x, step_y, step_z)
            dual_out[0, row, here, :] = new_x
            dual_out[1, row, here, :] = new_y
            dual_out[2, row, here, :] = new_z
            inner_z = new_z * edge
            inner_y = new_y
            if row + 1 == s.rows:
                inner_y = new_y * keep_y
                high, low = split_two(inner_y)
                y_high[here, :] = high
                y_low[here, :] = low
            back = sign - (inner_z - previous_lane(inner_z)) - inner_y
            if before is not None:
                back = back + before
            before = inner_y
            high, low = split_two(back)
            back_high[here, at] = high
            back_low[here, at] = low
            high, low = split_two(new_x)
            x_high[here, at] = high
            x_low[here, at] = low
        return carry

    lax.fori_loop(0, s.padded_dirs // GROUP, step, 0)


def weights(s, mask_ref, response_ref):
    mask = jnp.concatenate(
        [mask_ref[row : row + 1, :].astype(F32) for row in range(s.rows)], 1)
    return mask, jnp.concatenate([response_ref[...]] * s.rows, 1)


def is_odd(axis):
    return lax.rem(lax.axis_index(axis), 2) == 1


def to_partners(axis, upward, downward):
    odd = jnp.broadcast_to(is_odd(axis), upward.shape)
    return jnp.where(odd, downward, upward), jnp.where(odd, upward, downward)


def from_partners(axis, over_even, over_odd):
    odd = jnp.broadcast_to(is_odd(axis), over_even.shape)
    return jnp.where(odd, over_even, over_odd), jnp.where(odd, over_odd, over_even)


def first_kernel(s, dual_in, cat_ref, adjoint_ref, e_ref, ex_ref, ey_ref, coef_ref, signal_ref,
                 mask_ref, response_ref, dual_ref, base_ref, inverse_ref, coef_out, target_ref,
                 x_ref, v_ref, y_ref, even_ref, odd_ref,
                 e_cat, diff, back_high, back_low, x_high, x_low, y_high, y_low):
    keep_x, keep_y = last_flags()
    here = planes_of(e_ref, s.count, s.rows, s.padded)
    there = planes_of(ex_ref, s.count, s.rows, s.padded)
    edge_row = jnp.concatenate([ey_ref[...], jnp.zeros((s.padded - s.count, LANES), F32)], 0)
    e_cat[2 * s.padded : s.low_row, :] = jnp.zeros((s.low_row - 2 * s.padded, s.width + LANES), BF16)
    put_cat(e_cat, jnp.concatenate(
        [(there - here) * (STEP_DUAL * keep_x),
         (edge_row - here[:, s.width - LANES :]) * (STEP_DUAL * keep_y)], 1), s.low_row)
    wide_matmul(cat_ref, e_cat, diff, s.width + LANES)
    dual_pass(s, dual_in, dual_ref, diff, None, keep_y,
              (back_high, back_low, x_high, x_low, y_high, y_low))
    from_back = all_harmonics(adjoint_ref, back_high, back_low, s.width, s.padded)
    from_x = all_harmonics(adjoint_ref, x_high, x_low, s.width, s.padded)
    from_y = all_harmonics(adjoint_ref, y_high, y_low, LANES, s.padded)
    mask, response = weights(s, mask_ref, response_ref)
    weight = mask * response
    coef = planes_of(coef_ref, s.count, s.rows, s.padded)
    signal = planes_of(signal_ref, s.count, s.rows, s.padded)
    target = STEP_PRIMAL * weight * signal
    inverse = 1.0 / (1.0 + STEP_PRIMAL * weight * response)
    base = coef + target - STEP_PRIMAL * (from_back - keep_x * from_x)
    row_index = lax.broadcasted_iota(jnp.int32, (s.padded, s.width), 0)
    ahead = jnp.where(row_index == s.count, mask, 2.0 * base * inverse - coef)
    base_ref[...] = base
    inverse_ref[...] = inverse
    coef_out[...] = coef
    target_ref[...] = target
    x_ref[...] = from_x
    v_ref[...] = ahead
    y_ref[...] = from_y
    even_ref[...], odd_ref[...] = to_partners(
        "gy", jnp.concatenate([from_y, from_y], 0),
        jnp.concatenate([ahead[:, 0:LANES], from_x[:, 0:LANES]], 0))


def middle_kernel(s, base_in, inverse_ref, x_ref, v_ref, *refs):
    *received, base_ref, even_ref, odd_ref, side_ref = refs
    over_even = received[0][...]
    over_odd = received[1][...] if len(received) > 1 else jnp.zeros_like(over_even)
    below, above = from_partners("gy", over_even, over_odd)
    base_ref[...] = base_in[...]
    base_ref[:, 0:LANES] -= STEP_PRIMAL * below[0 : s.padded]
    side_ref[...] = above[0 : s.padded]
    ahead = v_ref[...]
    row_index = lax.broadcasted_iota(jnp.int32, (s.padded, LANES), 0)
    change = (2.0 * STEP_PRIMAL) * below[0 : s.padded] * inverse_ref[:, 0:LANES]
    change = jnp.where(row_index < s.count, change, 0.0)
    down = jnp.concatenate([ahead[:, 0:LANES] - change, ahead[:, LANES:], change], 1)
    up = jnp.concatenate([x_ref[...], above[s.padded :]], 1)
    even_ref[...], odd_ref[...] = to_partners("gx", up, down)


def ahead_of(s, message, own, response):
    row_index = lax.broadcasted_iota(jnp.int32, message.shape, 0)
    mask = message[s.count : s.count + 1, :]
    inverse = 1.0 / (1.0 + STEP_PRIMAL * (mask * response) * response)
    return jnp.where(row_index < s.count, message - (2.0 * STEP_PRIMAL) * inverse * own, 0.0)


def second_kernel(s, dual_in, cat_ref, adjoint_ref, base_ref, inverse_ref, coef_ref, target_ref,
                  x_ref, y_ref, over_even_ref, over_odd_ref, side_ref, response_ref,
                  dual_ref, base_out, coef_out, x_out, y_out,
                  e_cat, d_cat, amp, diff, back_high, back_low, x_high, x_low, y_high, y_low):
    keep_x, keep_y = last_flags()
    below, above = from_partners("gx", over_even_ref[...], over_odd_ref[...])
    response = response_ref[...]
    inverse = inverse_ref[...]
    coef = coef_ref[...]
    updated = (base_ref[...] - STEP_PRIMAL * below[:, 0 : s.width]) * inverse
    here = 2.0 * updated - coef
    wide = jnp.concatenate([response] * s.rows, 1)
    there = ahead_of(s, above[:, 0 : s.width], x_ref[...], wide)
    edge_row = ahead_of(s, side_ref[...], y_ref[...] + below[:, s.width :], response)
    zeros = jnp.zeros((s.low_row - 2 * s.padded, s.width + LANES), BF16)
    e_cat[2 * s.padded : s.low_row, :] = zeros[:, 0 : s.width]
    d_cat[2 * s.padded : s.low_row, :] = zeros
    put_cat(e_cat, here * STEP_DUAL, s.low_row)
    put_cat(d_cat, jnp.concatenate(
        [(there - here) * (STEP_DUAL * keep_x),
         (edge_row - here[:, s.width - LANES :]) * (STEP_DUAL * keep_y)], 1), s.low_row)
    wide_matmul(cat_ref, e_cat, amp, s.width)
    wide_matmul(cat_ref, d_cat, diff, s.width + LANES)
    dual_pass(s, dual_in, dual_ref, diff, amp, keep_y,
              (back_high, back_low, x_high, x_low, y_high, y_low))
    from_back = all_harmonics(adjoint_ref, back_high, back_low, s.width, s.padded)
    from_x = all_harmonics(adjoint_ref, x_high, x_low, s.width, s.padded)
    from_y = all_harmonics(adjoint_ref, y_high, y_low, LANES, s.padded)
    base_out[...] = updated + target_ref[...] - STEP_PRIMAL * (from_back - keep_x * from_x)
    coef_out[...] = updated
    x_out[...] = from_x
    y_out[...] = from_y


def store_kernel(s, dual_ref, grad_ref, sign_ref, sems):
    copies = []
    for row in range(s.rows):
        for part in range(3):
            copies.append(pltpu.make_async_copy(
                dual_ref.at[part, row, pl.ds(0, s.directions)], grad_ref.at[part, :, 0, row],
                sems.at[part * s.rows + row]))
        copies.append(pltpu.make_async_copy(
            dual_ref.at[3, row, pl.ds(0, s.directions)], sign_ref.at[:, 0, row],
            sems.at[3 * s.rows + row]))
    for copy in copies:
        copy.start()
    for copy in copies:
        copy.wait()


def last_kernel(s, base_ref, inverse_ref, coef_ref, x_ref, y_ref, coef_out, extra_out):
    total = jnp.concatenate(
        [x_ref[:, 0:LANES] + y_ref[...], x_ref[:, LANES:]], 1)
    updated = (base_ref[...] - STEP_PRIMAL * total) * inverse_ref[...]
    extra = 2.0 * updated - coef_ref[...]
    for row in range(s.rows):
        at = slice(row * LANES, (row + 1) * LANES)
        coef_out[pl.ds(row, s.count, stride=s.rows), :] = updated[0 : s.count, at]
        extra_out[pl.ds(row, s.count, stride=s.rows), :] = extra[0 : s.count, at]


def call(kernel, outs, ins, scratch, name, flops, in_specs=None, out_specs=None, aliases=None):
    vmem = pl.BlockSpec(memory_space=pltpu.VMEM)
    count = len(outs) if isinstance(outs, (tuple, list)) else 1
    size = lambda arrays: sum(a.size * a.dtype.itemsize for a in jax.tree.leaves(arrays))
    return pl.pallas_call(
        kernel,
        out_shape=outs,
        in_specs=in_specs or [vmem] * len(ins),
        out_specs=out_specs or ([vmem] * count if isinstance(outs, (tuple, list)) else vmem),
        scratch_shapes=scratch,
        input_output_aliases=aliases or {},
        compiler_params=pltpu.CompilerParams(vmem_limit_bytes=VMEM_LIMIT),
        cost_estimate=pl.CostEstimate(
            flops=flops, bytes_accessed=size(outs) + size(list(ins)), transcendentals=0),
        name=name,
    )(*ins)


def pair_lists(count):
    even = [pair for low in range(0, count - 1, 2) for pair in ((low, low + 1), (low + 1, low))]
    odd = [pair for low in range(1, count - 1, 2) for pair in ((low, low + 1), (low + 1, low))]
    return even, odd


def exchange(axis, to_even, to_odd):
    even, odd = pair_lists(lax.axis_size(axis))
    received = [lax.ppermute(to_odd, axis, odd)] if odd else []
    return [lax.ppermute(to_even, axis, even)] + received


def shift(value, axis, steps):
    count = lax.axis_size(axis)
    pairs = [(i, i + steps) for i in range(count) if 0 <= i + steps < count]
    return lax.ppermute(value, axis, pairs)


def per_device(signal, response, basis, mask, coefficients, extrapolated, dual_grad, dual_sign):
    count, layers, rows, lanes = signal.shape
    assert layers == 1
    s = Shape(basis.shape[0], count, rows, lanes)
    flat = lambda a: a.reshape(count * rows, lanes)
    f32 = lambda *shape: jax.ShapeDtypeStruct(shape, F32)
    bf16 = lambda *shape: jax.ShapeDtypeStruct(shape, BF16)
    vmem = pl.BlockSpec(memory_space=pltpu.VMEM)
    hbm = pl.BlockSpec(memory_space=pltpu.HBM)
    dirs, padded, width = s.padded_dirs, s.padded, s.width
    splits = [pltpu.VMEM((dirs, width), BF16)] * 4 + [pltpu.VMEM((dirs, LANES), BF16)] * 2
    dual = f32(4, rows, dirs, lanes)
    plane = f32(padded, width)

    after_x = shift(extrapolated, "gx", -1)
    after_y = shift(extrapolated[:, 0, 0], "gy", -1)
    in_hbm = lambda a: pltpu.with_memory_space_constraint(a, pltpu.HBM)
    line = f32(padded, lanes)
    duals, own, cat, adjoint, column = call(
        functools.partial(load_kernel, s),
        (dual, f32(count * rows, lanes), bf16(dirs, s.depth), bf16(2 * padded, dirs), line),
        [in_hbm(a) for a in
         (flat(extrapolated), basis.T, response[None], dual_grad, dual_sign)],
        [pltpu.VMEM((count, s.directions), F32), pltpu.VMEM((1, count), F32),
         pltpu.VMEM((LANES, round_up(dirs, LANES)), F32), pltpu.VMEM((s.depth, width), BF16),
         pltpu.VMEM((dirs, width), F32), pltpu.SemaphoreType.DMA((4 * rows + 3,))],
        "load", 2_000_000_000, in_specs=[hbm] * 5)
    duals, base, inverse, coef, target, from_x, ahead, from_y, to_even, to_odd = call(
        functools.partial(first_kernel, s),
        (dual,) + (plane,) * 6 + (line, f32(2 * padded, lanes), f32(2 * padded, lanes)),
        (duals, cat, adjoint, own, flat(after_x), after_y, flat(coefficients), flat(signal),
         mask[0], column),
        [pltpu.VMEM((s.depth, width + LANES), BF16), pltpu.VMEM((dirs, width + LANES), F32)] + splits,
        "first", 2_000_000_000, aliases={0: 0})
    message = f32(padded, width + lanes)
    base, to_even, to_odd, side = call(
        functools.partial(middle_kernel, s),
        (plane, message, message, line),
        [base, inverse, from_x, ahead] + exchange("gy", to_even, to_odd), [], "middle", 1_000_000)
    over_even, over_odd = exchange("gx", to_even, to_odd)
    duals, base, coef, from_x, from_y = call(
        functools.partial(second_kernel, s),
        (dual, plane, plane, plane, line),
        (duals, cat, adjoint, base, inverse, coef, target, from_x, from_y, over_even, over_odd,
         side, column),
        [pltpu.VMEM((s.depth, width), BF16), pltpu.VMEM((s.depth, width + LANES), BF16),
         pltpu.VMEM((dirs, width), F32), pltpu.VMEM((dirs, width + LANES), F32)] + splits,
        "second", 2_000_000_000, aliases={0: 0})
    below_x = shift(from_x, "gx", 1)
    below_y = shift(from_y, "gy", 1)
    grad_out, sign_out = call(
        functools.partial(store_kernel, s),
        (f32(*dual_grad.shape), f32(*dual_sign.shape)), (duals,),
        [pltpu.SemaphoreType.DMA((4 * rows,))], "store", 2_000_000_000, out_specs=[hbm, hbm])
    coef_out, extra_out = call(
        functools.partial(last_kernel, s),
        (f32(count * rows, lanes), f32(count * rows, lanes)),
        (base, inverse, coef, below_x, below_y), [], "last", 1_000_000)
    return (coef_out.reshape(signal.shape), extra_out.reshape(signal.shape), grad_out, sign_out)


def solution(mesh):
    cube = P(None, "gx", "gy", None)
    in_specs = (cube, P(), P(), P("gx", "gy", None), cube, cube, P(None, None, "gx", "gy", None), cube)
    out_specs = (cube, cube, P(None, None, "gx", "gy", None), cube)
    return jax.shard_map(per_device, mesh=mesh, in_specs=in_specs, out_specs=out_specs, check_vma=False)
```

time: 77.9 us -> 52.2 us (0.67)
  the two profiles are of different devices: /device:TPU:8 before, /device:TPU:1 now
where the time goes in v1:
time: 52.2 us; the launch traced here: 51.9 us
  Pallas kernels  24.2 us (46%)
  starting transfers between devices  19.2 us (37%)
  waiting for transfers between devices  6.78 us (13%)
  local copies, waits for them, and re-layouts  0.95 us (2%)
  between operations  0.8 us (2%)
    pallas_call x6, Pallas kernels, call(): pl.pallas_call(kernel, out_shape=outs, in_specs=in_specs or [vmem] * len(...  24.2 us
    ppermute x4, starting transfers between devices, shift(): return lax.ppermute(value, axis, pairs)  11.3 us
    ppermute x1, waiting for transfers between devices, exchange(): received = [lax.ppermute(to_odd, axis, odd)] if odd else []  5.22 us
    ppermute x1, starting transfers between devices, exchange(): received = [lax.ppermute(to_odd, axis, odd)] if odd else []  4.81 us
    ppermute x2, starting transfers between devices, exchange(): return [lax.ppermute(to_even, axis, even)] + received  3 us
    ppermute x2, waiting for transfers between devices, exchange(): return [lax.ppermute(to_even, axis, even)] + received  1.56 us
  transfers between devices with their start and end apart: 7, of which 2 were waited for; matrix products, arithmetic and copies ran while one was open for 2% of the time, Pallas kernels for 16%

profile of v1, /device:TPU:1, one launch (start us, length us, event | category | flops | bytes accessed | tf_op | source)
XLA Modules:
  0.0 51.9 jit_solution(7546929755862556983)
XLA Ops:
  0.6 0.0 copy-start
  0.6 0.0 copy-start.2
  0.7 0.0 copy-start.1
  0.7 2.1 %collective-permute-start = (f32[45,1,8,128]{3,2,1,0:T(8,128)}, f32[45,1,8,128]{3,2,1,0:T(8,128)S(1)}, u32[]{:S(2)}, u32[]{:S(2)}) collective-permute-start(f32[45,1,8,128]{3,2,1,0:T(8,128)} %param.13), channel_id=1, source_target_pairs={{2,0},{4,2},{6,4},{8,6},{10,8},{12,10},{14,12},{16,14},{18,16},{20... | collective-permute-start | bytes 552968 | tf_op jit(solution)/shard_map/ppermute | solution.py:397
  2.7 0.9 %slice.3 = f32[45,1,1,128]{3,2,1,0:T(1,128)S(1)} slice(f32[45,1,8,128]{3,2,1,0:T(8,128)} %param.13), slice={[0:45], [0:1], [0:1], [0:128]} | slice | bytes 46080 | tf_op jit(solution)/shard_map/slice | solution.py:415
  3.7 1.3 %collective-permute-start.1 = (f32[45,128]{1,0:T(8,128)S(1)}, f32[45,128]{1,0:T(8,128)S(1)}, u32[]{:S(2)}, u32[]{:S(2)}) collective-permute-start(f32[45,128]{1,0:T(8,128)S(1)} %bitcast.20), channel_id=1, source_target_pairs={{1,0},{3,2},{5,4},{7,6},{9,8},{11,10},{13,12},{15,14},{17,16},{19,... | collective-permute-start | bytes 69128 | tf_op jit(solution)/shard_map/ppermute | solution.py:397
  5.0 5.3 %load.1 = (f32[4,8,368,128]{3,2,1,0:T(8,128)S(1)}, f32[360,128]{1,0:T(8,128)S(1)}, bf16[368,176]{1,0:T(8,128)(2,1)S(1)}, bf16[96,368]{1,0:T(8,128)(2,1)S(1)}, f32[48,128]{1,0:T(8,128)S(1)}) custom-call(f32[360,128]{1,0:T(8,128)} %bitcast.21, f32[45,362]{1,0:T(8,128)} %bitcast.24, f32[1,45]{1,0:T(1,128)} %bitcast.25, f32[3,362,1,8,128]{4,3,2,1,0:T(8,128)} %grad_ref.1, ...), custom_call_target="tpu_custom_call" | custom-call | flops 2000000000 | bytes 12619068 | tf_op jit(solution)/shard_map/load/pallas_call | solution.py:368
  10.3 0.0 collective-permute-done.1.ey_ref
  10.3 0.0 collective-permute-done
  10.3 0.0 copy-done
  10.3 0.0 copy-done.2
  10.3 0.0 copy-done.1
  10.3 6.9 %first.1 = (f32[4,8,368,128]{3,2,1,0:T(8,128)S(1)}, f32[48,1024]{1,0:T(8,128)S(1)}, f32[48,1024]{1,0:T(8,128)S(1)}, f32[48,1024]{1,0:T(8,128)S(1)}, f32[48,1024]...) custom-call(f32[4,8,368,128]{3,2,1,0:T(8,128)S(1)} %get-tuple-elemen, ...), custom_call_target="tpu_custom_call", output_to_operand_aliasing={{0}: (0, {})} | custom-call | flops 2000000000 | bytes 14350336 | tf_op jit(solution)/shard_map/first/pallas_call | solution.py:368
  17.3 2.7 %collective-permute-start.2 = (f32[96,128]{1,0:T(8,128)S(1)}, f32[96,128]{1,0:T(8,128)S(1)}, u32[]{:S(2)}, u32[]{:S(2)}) collective-permute-start(f32[96,128]{1,0:T(8,128)S(1)} %get-tuple-element.41), channel_id=1, source_target_pairs={{0,1},{1,0},{2,3},{3,2},{4,5},{5,4},{6,7},{7,6},{8,9},{9,8},{10,11... | collective-permute-start | bytes 147464 | tf_op jit(solution)/shard_map/ppermute | solution.py:391
  20.0 1.6 %collective-permute-done.2.refs_0_ = f32[96,128]{1,0:T(8,128)S(1)} collective-permute-done((f32[96,128]{1,0:T(8,128)S(1)}, f32[96,128]{1,0:T(8,128)S(1)}, u32[]{:S(2)}, u32[]{:S(2)}) %collective-permute-start.2) | collective-permute-done | bytes 49184 | tf_op jit(solution)/shard_map/ppermute | solution.py:391
  21.5 0.1 middle.1
  21.6 0.3 collective-permute-start.3
  21.9 4.8 %collective-permute-start.4 = (f32[48,1152]{1,0:T(8,128)S(1)}, f32[48,1152]{1,0:T(8,128)S(1)}, u32[]{:S(2)}, u32[]{:S(2)}) collective-permute-start(f32[48,1152]{1,0:T(8,128)S(1)} %get-tuple-element.47), channel_id=1, source_target_pairs={{2,4},{4,2},{6,8},{8,6},{10,12},{12,10},{14,16},{16,14},{18,20},{2... | collective-permute-start | bytes 663560 | tf_op jit(solution)/shard_map/ppermute | solution.py:390
  26.7 0.0 collective-permute-done.3.over_even_ref
  26.7 5.2 %collective-permute-done.4.over_odd_ref = f32[48,1152]{1,0:T(8,128)S(1)} collective-permute-done((f32[48,1152]{1,0:T(8,128)S(1)}, f32[48,1152]{1,0:T(8,128)S(1)}, u32[]{:S(2)}, u32[]{:S(2)}) %collective-permute-start.4) | collective-permute-done | bytes 221216 | tf_op jit(solution)/shard_map/ppermute | solution.py:390
  31.9 8.3 %second.1 = (f32[4,8,368,128]{3,2,1,0:T(8,128)S(1)}, f32[48,1024]{1,0:T(8,128)S(1)}, f32[48,1024]{1,0:T(8,128)S(1)}, f32[48,1024]{1,0:T(8,128)S(1)}, f32[48,128]{1,0:T(8,128)S(1)}) custom-call(f32[4,8,368,128]{3,2,1,0:T(8,128)S(1)} %get-tuple-element.36.dual_in, bf16[368,176]{1,0:T(8,128)(2,1)S(1)} %get-tuple-element.32.cat_ref, ...), custom_call_target="tpu_custom_call", output_to_operand_aliasing={{0}: (0, {})} | custom-call | flops 2000000000 | bytes 14372352 | tf_op jit(solution)/shard_map/second/pallas_call | solution.py:368
  40.3 4.4 %collective-permute-start.5 = (f32[48,1024]{1,0:T(8,128)S(1)}, f32[48,1024]{1,0:T(8,128)S(1)}, u32[]{:S(2)}, u32[]{:S(2)}) collective-permute-start(f32[48,1024]{1,0:T(8,128)S(1)} %get-tuple-element.51), channel_id=1, source_target_pairs={{0,2},{2,4},{4,6},{6,8},{8,10},{10,12},{12,14},{14,16},{16,18},{18... | collective-permute-start | bytes 589832 | tf_op jit(solution)/shard_map/ppermute | solution.py:397
  44.6 3.6 %collective-permute-start.6 = (f32[48,128]{1,0:T(8,128)S(1)}, f32[48,128]{1,0:T(8,128)S(1)}, u32[]{:S(2)}, u32[]{:S(2)}) collective-permute-start(f32[48,128]{1,0:T(8,128)S(1)} %get-tuple-element.52), channel_id=1, source_target_pairs={{0,1},{2,3},{4,5},{6,7},{8,9},{10,11},{12,13},{14,15},{16,17},{18,... | collective-permute-start | bytes 73736 | tf_op jit(solution)/shard_map/ppermute | solution.py:397
  48.3 2.8 %store.1 = (f32[3,362,1,8,128]{4,3,2,1,0:T(8,128)}, f32[362,1,8,128]{3,2,1,0:T(8,128)}) custom-call(f32[4,8,368,128]{3,2,1,0:T(8,128)S(1)} %get-tuple-element.55.dual_ref), custom_call_target="tpu_custom_call" | custom-call | flops 2000000000 | bytes 11960320 | tf_op jit(solution)/shard_map/store/pallas_call | solution.py:368
  51.1 0.0 collective-permute-done.6.y_ref
  51.1 0.0 collective-permute-done.5.x_ref
  51.1 0.8 %last.1 = (f32[360,128]{1,0:T(8,128)}, f32[360,128]{1,0:T(8,128)}) custom-call(f32[48,1024]{1,0:T(8,128)S(1)} %get-tuple-element.49.base_ref, f32[48,1024]{1,0:T(8,128)S(1)} %get-tuple-element.38.inverse_ref, f32[48,1024]{1,0:T(8,128)S(1)} %get-tuple-element.50.coef_ref, f32[48,1024]{1,0:T(8,128)S(1)} %collective-permute-done.5.x_ref, ...), custom_call_target="tpu_custom_call" | custom-call | flops 1000000 | bytes 1179648 | tf_op jit(solution)/shard_map/last/pallas_call | solution.py:368
  (1 shorter events, 0.0 us)
Async XLA Ops:
  0.6 9.7 %copy-start = (f32[45,1,8,128]{3,2,1,0:T(8,128)S(1)}, f32[45,1,8,128]{3,2,1,0:T(8,128)}, u32[]{:S(2)}) copy-start(f32[45,1,8,128]{3,2,1,0:T(8,128)} %param.12) | copy-start | bytes 552964
  0.6 9.7 %copy-start.2 = (s32[1,8,128]{2,1,0:T(8,128)S(1)}, s32[1,8,128]{2,1,0:T(8,128)}, u32[]{:S(2)}) copy-start(s32[1,8,128]{2,1,0:T(8,128)} %param.11) | copy-start | bytes 12292
  0.7 9.7 %copy-start.1 = (f32[45,1,8,128]{3,2,1,0:T(8,128)S(1)}, f32[45,1,8,128]{3,2,1,0:T(8,128)}, u32[]{:S(2)}) copy-start(f32[45,1,8,128]{3,2,1,0:T(8,128)} %param.8) | copy-start | bytes 552964
  0.7 9.6 %collective-permute-start = (f32[45,1,8,128]{3,2,1,0:T(8,128)}, f32[45,1,8,128]{3,2,1,0:T(8,128)S(1)}, u32[]{:S(2)}, u32[]{:S(2)}) collective-permute-start(f32[45,1,8,128]{3,2,1,0:T(8,128)} %param.13), channel_id=1, source_target_pairs={{2,0},{4,2},{6,4},{8,6},{10,8},{12,10},{14,12},{16,14},{18,16},{20... | collective-permute-start | bytes 552968 | tf_op jit(solution)/shard_map/ppermute | solution.py:397
  3.7 6.6 %collective-permute-start.1 = (f32[45,128]{1,0:T(8,128)S(1)}, f32[45,128]{1,0:T(8,128)S(1)}, u32[]{:S(2)}, u32[]{:S(2)}) collective-permute-start(f32[45,128]{1,0:T(8,128)S(1)} %bitcast.20), channel_id=1, source_target_pairs={{1,0},{3,2},{5,4},{7,6},{9,8},{11,10},{13,12},{15,14},{17,16},{19,... | collective-permute-start | bytes 69128 | tf_op jit(solution)/shard_map/ppermute | solution.py:397
  17.3 4.3 %collective-permute-start.2 = (f32[96,128]{1,0:T(8,128)S(1)}, f32[96,128]{1,0:T(8,128)S(1)}, u32[]{:S(2)}, u32[]{:S(2)}) collective-permute-start(f32[96,128]{1,0:T(8,128)S(1)} %get-tuple-element.41), channel_id=1, source_target_pairs={{0,1},{1,0},{2,3},{3,2},{4,5},{5,4},{6,7},{7,6},{8,9},{9,8},{10,11... | collective-permute-start | bytes 147464 | tf_op jit(solution)/shard_map/ppermute | solution.py:391
  21.6 5.1 %collective-permute-start.3 = (f32[48,1152]{1,0:T(8,128)S(1)}, f32[48,1152]{1,0:T(8,128)S(1)}, u32[]{:S(2)}, u32[]{:S(2)}) collective-permute-start(f32[48,1152]{1,0:T(8,128)S(1)} %get-tuple-element.46), channel_id=1, source_target_pairs={{0,2},{2,0},{4,6},{6,4},{8,10},{10,8},{12,14},{14,12},{16,18},{18,... | collective-permute-start | bytes 663560 | tf_op jit(solution)/shard_map/ppermute | solution.py:391
  21.9 10.0 %collective-permute-start.4 = (f32[48,1152]{1,0:T(8,128)S(1)}, f32[48,1152]{1,0:T(8,128)S(1)}, u32[]{:S(2)}, u32[]{:S(2)}) collective-permute-start(f32[48,1152]{1,0:T(8,128)S(1)} %get-tuple-element.47), channel_id=1, source_target_pairs={{2,4},{4,2},{6,8},{8,6},{10,12},{12,10},{14,16},{16,14},{18,20},{2... | collective-permute-start | bytes 663560 | tf_op jit(solution)/shard_map/ppermute | solution.py:390
  40.3 10.8 %collective-permute-start.5 = (f32[48,1024]{1,0:T(8,128)S(1)}, f32[48,1024]{1,0:T(8,128)S(1)}, u32[]{:S(2)}, u32[]{:S(2)}) collective-permute-start(f32[48,1024]{1,0:T(8,128)S(1)} %get-tuple-element.51), channel_id=1, source_target_pairs={{0,2},{2,4},{4,6},{6,8},{8,10},{10,12},{12,14},{14,16},{16,18},{18... | collective-permute-start | bytes 589832 | tf_op jit(solution)/shard_map/ppermute | solution.py:397
  44.6 6.4 %collective-permute-start.6 = (f32[48,128]{1,0:T(8,128)S(1)}, f32[48,128]{1,0:T(8,128)S(1)}, u32[]{:S(2)}, u32[]{:S(2)}) collective-permute-start(f32[48,128]{1,0:T(8,128)S(1)} %get-tuple-element.52), channel_id=1, source_target_pairs={{0,1},{2,3},{4,5},{6,7},{8,9},{10,11},{12,13},{14,15},{16,17},{18,... | collective-permute-start | bytes 73736 | tf_op jit(solution)/shard_map/ppermute | solution.py:397

commit v2 on v1

--- a/solution.py
+++ b/solution.py
@@ -104,10 +104,21 @@
         self.width = rows * lanes
         self.low_row = round_up(2 * self.padded, LANES)
         self.depth = self.low_row + self.padded
+        self.groups = self.padded_dirs // GROUP
+        self.part_rows = (rows + 1) * self.padded_dirs + 8
+
+    def start(self, part, row):
+        return part * self.part_rows + (row + 1) * self.padded_dirs
+
+    def at(self, part, row, index):
+        return pl.ds(pl.multiple_of(self.start(part, row) + index * GROUP, 8), GROUP)
+
+    def lanes(self, row):
+        return pl.ds(pl.multiple_of(row * LANES, LANES), LANES)
 
 
 def load_kernel(s, e_ref, basis_ref, response_ref, grad_ref, sign_ref,
-                dual_ref, own_ref, cat_ref, adjoint_ref, column_ref,
+                dual_ref, sign_out, own_ref, cat_ref, adjoint_ref, column_ref,
                 basis_in, response_in, padded_ref, e_cat, amp, sems):
     first = [
         pltpu.make_async_copy(basis_ref, basis_in, sems.at[4 * s.rows]),
@@ -116,19 +127,25 @@
     ]
     for copy in first:
         copy.start()
-    copies = []
     pad_rows = s.padded_dirs - s.directions
     for part in range(4):
-        if pad_rows:
-            dual_ref[part, :, s.directions :, :] = jnp.zeros((s.rows, pad_rows, LANES), F32)
+        for row in range(s.rows):
+            if pad_rows:
+                end = s.start(part % 3, row) + s.padded_dirs
+                place = sign_out if part == 3 else dual_ref
+                place[end - pad_rows : end, :] = jnp.zeros((pad_rows, LANES), F32)
+
+    def copy_of(part, row):
+        source = sign_ref.at[:, 0, row] if part == 3 else grad_ref.at[part, :, 0, row]
+        place = sign_out if part == 3 else dual_ref
+        target = place.at[pl.ds(s.start(part % 3, row), s.directions)]
+        return pltpu.make_async_copy(source, target, sems.at[part * s.rows + row])
+
     for row in range(s.rows):
-        for part in (3, 1, 2, 0):
-            source = sign_ref.at[:, 0, row] if part == 3 else grad_ref.at[part, :, 0, row]
-            copies.append(pltpu.make_async_copy(
-                source, dual_ref.at[part, row, pl.ds(0, s.directions)],
-                sems.at[part * s.rows + row]))
-    for copy in copies:
-        copy.start()
+        for part in (1, 2, 3):
+            copy_of(part, row).start()
+    for row in range(s.rows):
+        copy_of(0, row).start()
 
     padded_ref[...] = jnp.zeros_like(padded_ref)
     for copy in first:
@@ -151,70 +168,91 @@
     e_cat[...] = jnp.zeros_like(e_cat)
     put_cat(e_cat, planes_of(own_ref, s.count, s.rows, s.padded) * STEP_DUAL, s.low_row)
     wide_matmul(cat_ref, e_cat, amp, s.width)
-    for copy in copies:
-        copy.wait()
     edge = lane_edge()
 
-    def step(index, carry):
-        here = pl.ds(pl.multiple_of(index * GROUP, GROUP), GROUP)
-        values = [amp[here, row * LANES : (row + 1) * LANES] for row in range(s.rows)]
-        for row in range(s.rows):
-            if row + 1 < s.rows:
-                dual_ref[1, row, here, :] += values[row + 1] - values[row]
-            dual_ref[2, row, here, :] += (next_lane(values[row]) - values[row]) * edge
-            dual_ref[3, row, here, :] = jnp.minimum(0.0, dual_ref[3, row, here, :] + values[row])
+    def update_row(row):
+        for part in (1, 2, 3):
+            copy_of(part, row).wait()
+        for index in range(s.groups):
+            here = slice(index * GROUP, (index + 1) * GROUP)
+            value = amp[here, s.lanes(row)]
+            if not isinstance(row, int):
+                dual_ref[s.at(1, row, index), :] += amp[here, s.lanes(row + 1)] - value
+            dual_ref[s.at(2, row, index), :] += (next_lane(value) - value) * edge
+            sign = sign_out[s.at(0, row, index), :] + value
+            sign_out[s.at(0, row, index), :] = jnp.minimum(0.0, sign)
+
+    def step(row, carry):
+        update_row(row)
         return carry
 
-    lax.fori_loop(0, s.padded_dirs // GROUP, step, 0)
-
-
-def dual_pass(s, dual_in, dual_out, diff, amp, keep_y, highs):
+    lax.fori_loop(0, s.rows - 1, step, 0)
+    update_row(s.rows - 1)
+    for row in range(s.rows):
+        copy_of(0, row).wait()
+
+
+def dual_pass(s, dual_in, sign_in, dual_out, sign_out, change, highs):
     edge = lane_edge()
     back_high, back_low, x_high, x_low, y_high, y_low = highs
-
-    def step(index, carry):
-        here = pl.ds(pl.multiple_of(index * GROUP, GROUP), GROUP)
-        before = None
-        if amp is not None:
-            value = amp[here, 0:LANES]
-        for row in range(s.rows):
-            at = slice(row * LANES, (row + 1) * LANES)
-            step_x = dual_in[0, row, here, :] + diff[here, at]
-            step_y, step_z, sign = dual_in[1, row, here, :], dual_in[2, row, here, :], dual_in[3, row, here, :]
-            if row + 1 == s.rows:
-                step_y = step_y + diff[here, s.width : s.width + LANES]
-            if amp is not None:
-                step_z = step_z + (next_lane(value) - value) * edge
-                sign = jnp.minimum(0.0, sign + value)
-                dual_out[3, row, here, :] = sign
-                if row + 1 < s.rows:
-                    after = amp[here, (row + 1) * LANES : (row + 2) * LANES]
-                    step_y = step_y + (after - value)
-                    value = after
+    full = sign_out is not None
+    signs = sign_out if full else sign_in
+    dual_out[s.start(1, -1) : s.start(1, 0), :] = jnp.zeros((s.padded_dirs, LANES), F32)
+
+    def part_lanes(part, row):
+        return pl.ds(pl.multiple_of(part * s.width + row * LANES, LANES), LANES)
+
+    def shrink_row(row):
+        for index in range(s.groups):
+            here = slice(index * GROUP, (index + 1) * GROUP)
+            step_x = dual_in[s.at(0, row, index), :] + change[here, part_lanes(0, row)]
+            step_y, step_z = dual_in[s.at(1, row, index), :], dual_in[s.at(2, row, index), :]
+            if full:
+                step_y = step_y + change[here, part_lanes(1, row)]
+                step_z = step_z + change[here, part_lanes(2, row)]
+                sign_out[s.at(0, row, index), :] = jnp.minimum(
+                    0.0, sign_in[s.at(0, row, index), :] + change[here, part_lanes(3, row)])
+            elif isinstance(row, int):
+                step_y = step_y + change[here, part_lanes(1, 0)]
             new_x, new_y, new_z = shrunk(step_x, step_y, step_z)
-            dual_out[0, row, here, :] = new_x
-            dual_out[1, row, here, :] = new_y
-            dual_out[2, row, here, :] = new_z
-            inner_z = new_z * edge
-            inner_y = new_y
-            if row + 1 == s.rows:
-                inner_y = new_y * keep_y
-                high, low = split_two(inner_y)
-                y_high[here, :] = high
-                y_low[here, :] = low
-            back = sign - (inner_z - previous_lane(inner_z)) - inner_y
-            if before is not None:
-                back = back + before
-            before = inner_y
-            high, low = split_two(back)
-            back_high[here, at] = high
-            back_low[here, at] = low
-            high, low = split_two(new_x)
-            x_high[here, at] = high
-            x_low[here, at] = low
+            dual_out[s.at(0, row, index), :] = new_x
+            dual_out[s.at(1, row, index), :] = new_y
+            dual_out[s.at(2, row, index), :] = new_z
+
+    def split_row(row, carry):
+        for index in range(s.groups):
+            here = slice(index * GROUP, (index + 1) * GROUP)
+            inner_z = dual_out[s.at(2, row, index), :] * edge
+            back = signs[s.at(0, row, index), :] - (inner_z - previous_lane(inner_z))
+            back = back - (dual_out[s.at(1, row, index), :] - dual_out[s.at(1, row - 1, index), :])
+            back_high[here, s.lanes(row)], back_low[here, s.lanes(row)] = split_two(back)
+            x_high[here, s.lanes(row)], x_low[here, s.lanes(row)] = split_two(
+                dual_out[s.at(0, row, index), :])
         return carry
 
-    lax.fori_loop(0, s.padded_dirs // GROUP, step, 0)
+    def step(row, carry):
+        shrink_row(row)
+        return carry
+
+    if full:
+        lax.fori_loop(0, s.rows, step, 0)
+    else:
+        lax.fori_loop(0, s.rows - 1, step, 0)
+        shrink_row(s.rows - 1)
+    lax.fori_loop(0, s.rows, split_row, 0)
+    for index in range(s.groups):
+        here = slice(index * GROUP, (index + 1) * GROUP)
+        y_high[here, :], y_low[here, :] = split_two(dual_out[s.at(1, s.rows - 1, index), :])
+
+
+def all_adjoints(s, adjoint_ref, splits, keep_x, keep_y):
+    back_high, back_low, x_high, x_low, y_high, y_low = splits
+    from_back = all_harmonics(adjoint_ref, back_high, back_low, s.width, s.padded)
+    from_x = all_harmonics(adjoint_ref, x_high, x_low, s.width, s.padded)
+    from_y = all_harmonics(adjoint_ref, y_high, y_low, LANES, s.padded)
+    last = from_back[:, s.width - LANES :] + (1.0 - keep_y) * from_y
+    total = jnp.concatenate([from_back[:, : s.width - LANES], last], 1) - keep_x * from_x
+    return total, from_x, from_y
 
 
 def weights(s, mask_ref, response_ref):
@@ -237,10 +275,11 @@
     return jnp.where(odd, over_even, over_odd), jnp.where(odd, over_odd, over_even)
 
 
-def first_kernel(s, dual_in, cat_ref, adjoint_ref, e_ref, ex_ref, ey_ref, coef_ref, signal_ref,
+def first_kernel(s, dual_in, sign_in, cat_ref, adjoint_ref, e_ref, ex_ref, ey_ref, coef_ref, signal_ref,
                  mask_ref, response_ref, dual_ref, base_ref, inverse_ref, coef_out, target_ref,
-                 x_ref, v_ref, y_ref, even_ref, odd_ref,
-                 e_cat, diff, back_high, back_low, x_high, x_low, y_high, y_low):
+                 x_ref, v_ref, y_ref, *refs):
+    e_cat, diff = refs[-8:-6]
+    send_refs = refs[:-8]
     keep_x, keep_y = last_flags()
     here = planes_of(e_ref, s.count, s.rows, s.padded)
     there = planes_of(ex_ref, s.count, s.rows, s.padded)
@@ -250,18 +289,15 @@
         [(there - here) * (STEP_DUAL * keep_x),
          (edge_row - here[:, s.width - LANES :]) * (STEP_DUAL * keep_y)], 1), s.low_row)
     wide_matmul(cat_ref, e_cat, diff, s.width + LANES)
-    dual_pass(s, dual_in, dual_ref, diff, None, keep_y,
-              (back_high, back_low, x_high, x_low, y_high, y_low))
-    from_back = all_harmonics(adjoint_ref, back_high, back_low, s.width, s.padded)
-    from_x = all_harmonics(adjoint_ref, x_high, x_low, s.width, s.padded)
-    from_y = all_harmonics(adjoint_ref, y_high, y_low, LANES, s.padded)
+    dual_pass(s, dual_in, sign_in, dual_ref, None, diff, refs[-6:])
+    total, from_x, from_y = all_adjoints(s, adjoint_ref, refs[-6:], keep_x, keep_y)
     mask, response = weights(s, mask_ref, response_ref)
     weight = mask * response
     coef = planes_of(coef_ref, s.count, s.rows, s.padded)
     signal = planes_of(signal_ref, s.count, s.rows, s.padded)
     target = STEP_PRIMAL * weight * signal
     inverse = 1.0 / (1.0 + STEP_PRIMAL * weight * response)
-    base = coef + target - STEP_PRIMAL * (from_back - keep_x * from_x)
+    base = coef + target - STEP_PRIMAL * total
     row_index = lax.broadcasted_iota(jnp.int32, (s.padded, s.width), 0)
     ahead = jnp.where(row_index == s.count, mask, 2.0 * base * inverse - coef)
     base_ref[...] = base
@@ -271,9 +307,11 @@
     x_ref[...] = from_x
     v_ref[...] = ahead
     y_ref[...] = from_y
-    even_ref[...], odd_ref[...] = to_partners(
+    sends = to_partners(
         "gy", jnp.concatenate([from_y, from_y], 0),
         jnp.concatenate([ahead[:, 0:LANES], from_x[:, 0:LANES]], 0))
+    for send_ref, send in zip(send_refs, sends):
+        send_ref[...] = send
 
 
 def middle_kernel(s, base_in, inverse_ref, x_ref, v_ref, *refs):
@@ -300,10 +338,10 @@
     return jnp.where(row_index < s.count, message - (2.0 * STEP_PRIMAL) * inverse * own, 0.0)
 
 
-def second_kernel(s, dual_in, cat_ref, adjoint_ref, base_ref, inverse_ref, coef_ref, target_ref,
+def second_kernel(s, dual_in, sign_in, cat_ref, adjoint_ref, base_ref, inverse_ref, coef_ref, target_ref,
                   x_ref, y_ref, over_even_ref, over_odd_ref, side_ref, response_ref,
-                  dual_ref, base_out, coef_out, x_out, y_out,
-                  e_cat, d_cat, amp, diff, back_high, back_low, x_high, x_low, y_high, y_low):
+                  dual_ref, sign_ref, base_out, coef_out, x_out, y_out,
+                  e_cat, change, *splits):
     keep_x, keep_y = last_flags()
     below, above = from_partners("gx", over_even_ref[...], over_odd_ref[...])
     response = response_ref[...]
@@ -314,35 +352,33 @@
     wide = jnp.concatenate([response] * s.rows, 1)
     there = ahead_of(s, above[:, 0 : s.width], x_ref[...], wide)
     edge_row = ahead_of(s, side_ref[...], y_ref[...] + below[:, s.width :], response)
-    zeros = jnp.zeros((s.low_row - 2 * s.padded, s.width + LANES), BF16)
-    e_cat[2 * s.padded : s.low_row, :] = zeros[:, 0 : s.width]
-    d_cat[2 * s.padded : s.low_row, :] = zeros
-    put_cat(e_cat, here * STEP_DUAL, s.low_row)
-    put_cat(d_cat, jnp.concatenate(
-        [(there - here) * (STEP_DUAL * keep_x),
-         (edge_row - here[:, s.width - LANES :]) * (STEP_DUAL * keep_y)], 1), s.low_row)
-    wide_matmul(cat_ref, e_cat, amp, s.width)
-    wide_matmul(cat_ref, d_cat, diff, s.width + LANES)
-    dual_pass(s, dual_in, dual_ref, diff, amp, keep_y,
-              (back_high, back_low, x_high, x_low, y_high, y_low))
-    from_back = all_harmonics(adjoint_ref, back_high, back_low, s.width, s.padded)
-    from_x = all_harmonics(adjoint_ref, x_high, x_low, s.width, s.padded)
-    from_y = all_harmonics(adjoint_ref, y_high, y_low, LANES, s.padded)
-    base_out[...] = updated + target_ref[...] - STEP_PRIMAL * (from_back - keep_x * from_x)
+    e_cat[2 * s.padded : s.low_row, :] = jnp.zeros((s.low_row - 2 * s.padded, 4 * s.width), BF16)
+    edge = lane_edge()[0:1]
+    planes = [here[:, row * LANES : (row + 1) * LANES] for row in range(s.rows)]
+    along_y = jnp.concatenate([here[:, LANES:], edge_row], 1) - here
+    along_y = jnp.concatenate(
+        [along_y[:, : s.width - LANES], keep_y * along_y[:, s.width - LANES :]], 1)
+    along_z = jnp.concatenate([(next_lane(plane) - plane) * edge for plane in planes], 1)
+    put_cat(e_cat, STEP_DUAL * jnp.concatenate(
+        [(there - here) * keep_x, along_y, along_z, here], 1), s.low_row)
+    wide_matmul(cat_ref, e_cat, change, 4 * s.width)
+    dual_pass(s, dual_in, sign_in, dual_ref, sign_ref, change, splits)
+    total, from_x, from_y = all_adjoints(s, adjoint_ref, splits, keep_x, keep_y)
+    base_out[...] = updated + target_ref[...] - STEP_PRIMAL * total
     coef_out[...] = updated
     x_out[...] = from_x
     y_out[...] = from_y
 
 
-def store_kernel(s, dual_ref, grad_ref, sign_ref, sems):
+def store_kernel(s, dual_ref, sign_in, grad_ref, sign_ref, sems):
     copies = []
     for row in range(s.rows):
         for part in range(3):
             copies.append(pltpu.make_async_copy(
-                dual_ref.at[part, row, pl.ds(0, s.directions)], grad_ref.at[part, :, 0, row],
+                dual_ref.at[pl.ds(s.start(part, row), s.directions)], grad_ref.at[part, :, 0, row],
                 sems.at[part * s.rows + row]))
         copies.append(pltpu.make_async_copy(
-            dual_ref.at[3, row, pl.ds(0, s.directions)], sign_ref.at[:, 0, row],
+            sign_in.at[pl.ds(s.start(0, row), s.directions)], sign_ref.at[:, 0, row],
             sems.at[3 * s.rows + row]))
     for copy in copies:
         copy.start()
@@ -382,13 +418,12 @@
 def pair_lists(count):
     even = [pair for low in range(0, count - 1, 2) for pair in ((low, low + 1), (low + 1, low))]
     odd = [pair for low in range(1, count - 1, 2) for pair in ((low, low + 1), (low + 1, low))]
-    return even, odd
-
-
-def exchange(axis, to_even, to_odd):
-    even, odd = pair_lists(lax.axis_size(axis))
-    received = [lax.ppermute(to_odd, axis, odd)] if odd else []
-    return [lax.ppermute(to_even, axis, even)] + received
+    return [even, odd] if odd else [even]
+
+
+def exchange(axis, sends):
+    lists = pair_lists(lax.axis_size(axis))
+    return [lax.ppermute(send, axis, pairs) for send, pairs in zip(sends, lists)]
 
 
 def shift(value, axis, steps):
@@ -408,48 +443,49 @@
     hbm = pl.BlockSpec(memory_space=pltpu.HBM)
     dirs, padded, width = s.padded_dirs, s.padded, s.width
     splits = [pltpu.VMEM((dirs, width), BF16)] * 4 + [pltpu.VMEM((dirs, LANES), BF16)] * 2
-    dual = f32(4, rows, dirs, lanes)
+    dual = f32(3 * s.part_rows, lanes)
+    signs = f32(s.part_rows, lanes)
     plane = f32(padded, width)
 
     after_x = shift(extrapolated, "gx", -1)
     after_y = shift(extrapolated[:, 0, 0], "gy", -1)
     in_hbm = lambda a: pltpu.with_memory_space_constraint(a, pltpu.HBM)
     line = f32(padded, lanes)
-    duals, own, cat, adjoint, column = call(
+    duals, sign, own, cat, adjoint, column = call(
         functools.partial(load_kernel, s),
-        (dual, f32(count * rows, lanes), bf16(dirs, s.depth), bf16(2 * padded, dirs), line),
+        (dual, signs, f32(count * rows, lanes), bf16(dirs, s.depth), bf16(2 * padded, dirs), line),
         [in_hbm(a) for a in
          (flat(extrapolated), basis.T, response[None], dual_grad, dual_sign)],
         [pltpu.VMEM((count, s.directions), F32), pltpu.VMEM((1, count), F32),
          pltpu.VMEM((LANES, round_up(dirs, LANES)), F32), pltpu.VMEM((s.depth, width), BF16),
          pltpu.VMEM((dirs, width), F32), pltpu.SemaphoreType.DMA((4 * rows + 3,))],
         "load", 2_000_000_000, in_specs=[hbm] * 5)
-    duals, base, inverse, coef, target, from_x, ahead, from_y, to_even, to_odd = call(
+    pairs_y = len(pair_lists(lax.axis_size("gy")))
+    duals, base, inverse, coef, target, from_x, ahead, from_y, *sends = call(
         functools.partial(first_kernel, s),
-        (dual,) + (plane,) * 6 + (line, f32(2 * padded, lanes), f32(2 * padded, lanes)),
-        (duals, cat, adjoint, own, flat(after_x), after_y, flat(coefficients), flat(signal),
+        (dual,) + (plane,) * 6 + (line,) + (f32(2 * padded, lanes),) * pairs_y,
+        (duals, sign, cat, adjoint, own, flat(after_x), after_y, flat(coefficients), flat(signal),
          mask[0], column),
         [pltpu.VMEM((s.depth, width + LANES), BF16), pltpu.VMEM((dirs, width + LANES), F32)] + splits,
-        "first", 2_000_000_000, aliases={0: 0})
+        "first", 2_000_000_000)
     message = f32(padded, width + lanes)
     base, to_even, to_odd, side = call(
         functools.partial(middle_kernel, s),
         (plane, message, message, line),
-        [base, inverse, from_x, ahead] + exchange("gy", to_even, to_odd), [], "middle", 1_000_000)
-    over_even, over_odd = exchange("gx", to_even, to_odd)
-    duals, base, coef, from_x, from_y = call(
+        [base, inverse, from_x, ahead] + exchange("gy", sends), [], "middle", 1_000_000)
+    over_even, over_odd = exchange("gx", [to_even, to_odd])
+    duals, sign, base, coef, from_x, from_y = call(
         functools.partial(second_kernel, s),
-        (dual, plane, plane, plane, line),
-        (duals, cat, adjoint, base, inverse, coef, target, from_x, from_y, over_even, over_odd,
+        (dual, signs, plane, plane, plane, line),
+        (duals, sign, cat, adjoint, base, inverse, coef, target, from_x, from_y, over_even, over_odd,
          side, column),
-        [pltpu.VMEM((s.depth, width), BF16), pltpu.VMEM((s.depth, width + LANES), BF16),
-         pltpu.VMEM((dirs, width), F32), pltpu.VMEM((dirs, width + LANES), F32)] + splits,
-        "second", 2_000_000_000, aliases={0: 0})
+        [pltpu.VMEM((s.depth, 4 * width), BF16), pltpu.VMEM((dirs, 4 * width), F32)] + splits,
+        "second", 2_000_000_000)
     below_x = shift(from_x, "gx", 1)
     below_y = shift(from_y, "gy", 1)
     grad_out, sign_out = call(
         functools.partial(store_kernel, s),
-        (f32(*dual_grad.shape), f32(*dual_sign.shape)), (duals,),
+        (f32(*dual_grad.shape), f32(*dual_sign.shape)), (duals, sign),
         [pltpu.SemaphoreType.DMA((4 * rows,))], "store", 2_000_000_000, out_specs=[hbm, hbm])
     coef_out, extra_out = call(
         functools.partial(last_kernel, s),

time: 52.2 us -> 42.4 us (0.81)
  Pallas kernels: 24.2 us -> 14.4 us
  waiting for transfers between devices: 6.78 us -> 8.07 us
  starting transfers between devices: 19.2 us -> 18 us
    pallas_call x6, Pallas kernels: 24.2 us -> 14.4 us  [call(): pl.pallas_call(kernel, out_shape=outs, in_specs=in_specs or [vmem] * len(...]
    ppermute x4, waiting for transfers between devices: 0.01 us -> 0.71 us  [shift(): return lax.ppermute(value, axis, pairs)]
    ppermute x3, starting transfers between devices: 7.81 us -> 7.16 us  [exchange(): lax.ppermute(send, axis, pairs)]
    ppermute x3, waiting for transfers between devices: 6.77 us -> 7.36 us  [exchange(): lax.ppermute(send, axis, pairs)]
    ppermute x4, starting transfers between devices: 11.3 us -> 10.8 us  [shift(): return lax.ppermute(value, axis, pairs)]
  transfers between devices with their start and end apart: 7 -> 7, of which waited for: 2 -> 3; matrix products, arithmetic and copies ran while one was open for 2% -> 2% of each run, Pallas kernels for 16% -> 14%
where the time goes in v2:
time: 42.4 us; the launch traced here: 42.2 us
  starting transfers between devices  18 us (42%)
  Pallas kernels  14.4 us (34%)
  waiting for transfers between devices  8.07 us (19%)
  local copies, waits for them, and re-layouts  0.95 us (2%)
  between operations  0.78 us (2%)
    pallas_call x6, Pallas kernels, call(): pl.pallas_call(kernel, out_shape=outs, in_specs=in_specs or [vmem] * len(...  14.4 us
    ppermute x4, starting transfers between devices, shift(): return lax.ppermute(value, axis, pairs)  10.8 us
    ppermute x3, waiting for transfers between devices, exchange(): lax.ppermute(send, axis, pairs)  7.36 us
    ppermute x3, starting transfers between devices, exchange(): lax.ppermute(send, axis, pairs)  7.16 us
    slice x1, local copies, waits for them, and re-layouts, per_device(): after_y = shift(extrapolated[:, 0, 0], 'gy', -1)  0.94 us
  transfers between devices with their start and end apart: 7, of which 3 were waited for; matrix products, arithmetic and copies ran while one was open for 2% of the time, Pallas kernels for 14%

profile of v2, /device:TPU:1, one launch (start us, length us, event | category | flops | bytes accessed | tf_op | source)
XLA Modules:
  0.0 42.2 jit_solution(9364327966098117049)
XLA Ops:
  0.6 0.0 copy-start
  0.6 0.0 copy-start.2
  0.7 0.0 copy-start.1
  0.7 2.1 %collective-permute-start = (f32[45,1,8,128]{3,2,1,0:T(8,128)}, f32[45,1,8,128]{3,2,1,0:T(8,128)S(1)}, u32[]{:S(2)}, u32[]{:S(2)}) collective-permute-start(f32[45,1,8,128]{3,2,1,0:T(8,128)} %param.13), channel_id=1, source_target_pairs={{2,0},{4,2},{6,4},{8,6},{10,8},{12,10},{14,12},{16,14},{18,16},{20... | collective-permute-start | bytes 552968 | tf_op jit(solution)/shard_map/ppermute | solution.py:432
  2.7 0.9 %slice.3 = f32[45,1,1,128]{3,2,1,0:T(1,128)S(1)} slice(f32[45,1,8,128]{3,2,1,0:T(8,128)} %param.13), slice={[0:45], [0:1], [0:1], [0:128]} | slice | bytes 46080 | tf_op jit(solution)/shard_map/slice | solution.py:451
  3.7 1.3 %collective-permute-start.1 = (f32[45,128]{1,0:T(8,128)S(1)}, f32[45,128]{1,0:T(8,128)S(1)}, u32[]{:S(2)}, u32[]{:S(2)}) collective-permute-start(f32[45,128]{1,0:T(8,128)S(1)} %bitcast.20), channel_id=1, source_target_pairs={{1,0},{3,2},{5,4},{7,6},{9,8},{11,10},{13,12},{15,14},{17,16},{19,... | collective-permute-start | bytes 69128 | tf_op jit(solution)/shard_map/ppermute | solution.py:432
  5.0 3.2 %load.1 = (f32[9960,128]{1,0:T(8,128)S(1)}, f32[3320,128]{1,0:T(8,128)S(1)}, f32[360,128]{1,0:T(8,128)S(1)}, bf16[368,176]{1,0:T(8,128)(2,1)S(1)}, bf16[96,368]{1,0:T(8,128)(2,1)S(1)}, /*index=5*/f32[48,128]{1,0:T(8,128)S(1)}) custom-call(f32[360,128]{1,0:T(8,128)} %bitcast.21, f32[45,362]{1,0:T(8,128)} %bitcast.24, f32[1,45]{1,0:T(1,128)} %bitcast.25, ...), custom_call_target="tpu_custom_call" | custom-call | flops 2000000000 | bytes 13389116 | tf_op jit(solution)/shard_map/load/pallas_call | solution.py:404
  8.2 0.7 %collective-permute-done.1.ey_ref = f32[45,128]{1,0:T(8,128)S(1)} collective-permute-done((f32[45,128]{1,0:T(8,128)S(1)}, f32[45,128]{1,0:T(8,128)S(1)}, u32[]{:S(2)}, u32[]{:S(2)}) %collective-permute-start.1) | collective-permute-done | bytes 23072 | tf_op jit(solution)/shard_map/ppermute | solution.py:432
  8.9 0.0 collective-permute-done
  8.9 0.0 copy-done
  8.9 0.0 copy-done.2
  8.9 0.0 copy-done.1
  8.9 3.3 %first.1 = (f32[9960,128]{1,0:T(8,128)S(1)}, f32[48,1024]{1,0:T(8,128)S(1)}, f32[48,1024]{1,0:T(8,128)S(1)}, f32[48,1024]{1,0:T(8,128)S(1)}, f32[48,1024]{1,0:T(...) custom-call(f32[9960,128]{1,0:T(8,128)S(1)} %get-tuple-element.33.du, ...), custom_call_target="tpu_custom_call" | custom-call | flops 2000000000 | bytes 14141440 | tf_op jit(solution)/shard_map/first/pallas_call | solution.py:404
  12.2 2.1 %collective-permute-start.2 = (f32[96,128]{1,0:T(8,128)S(1)}, f32[96,128]{1,0:T(8,128)S(1)}, u32[]{:S(2)}, u32[]{:S(2)}) collective-permute-start(f32[96,128]{1,0:T(8,128)S(1)} %get-tuple-element.44), channel_id=1, source_target_pairs={{0,1},{1,0},{2,3},{3,2},{4,5},{5,4},{6,7},{7,6},{8,9},{9,8},{10,11... | collective-permute-start | bytes 147464 | tf_op jit(solution)/shard_map/ppermute | solution.py:426
  14.2 2.1 %collective-permute-done.2.refs_0_ = f32[96,128]{1,0:T(8,128)S(1)} collective-permute-done((f32[96,128]{1,0:T(8,128)S(1)}, f32[96,128]{1,0:T(8,128)S(1)}, u32[]{:S(2)}, u32[]{:S(2)}) %collective-permute-start.2) | collective-permute-done | bytes 49184 | tf_op jit(solution)/shard_map/ppermute | solution.py:426
  16.4 0.1 middle.1
  16.5 0.6 %collective-permute-start.3 = (f32[48,1152]{1,0:T(8,128)S(1)}, f32[48,1152]{1,0:T(8,128)S(1)}, u32[]{:S(2)}, u32[]{:S(2)}) collective-permute-start(f32[48,1152]{1,0:T(8,128)S(1)} %get-tuple-element.49), channel_id=1, source_target_pairs={{0,2},{2,0},{4,6},{6,4},{8,10},{10,8},{12,14},{14,12},{16,18},{18,... | collective-permute-start | bytes 663560 | tf_op jit(solution)/shard_map/ppermute | solution.py:426
  17.1 4.5 %collective-permute-start.4 = (f32[48,1152]{1,0:T(8,128)S(1)}, f32[48,1152]{1,0:T(8,128)S(1)}, u32[]{:S(2)}, u32[]{:S(2)}) collective-permute-start(f32[48,1152]{1,0:T(8,128)S(1)} %get-tuple-element.50), channel_id=1, source_target_pairs={{2,4},{4,2},{6,8},{8,6},{10,12},{12,10},{14,16},{16,14},{18,20},{2... | collective-permute-start | bytes 663560 | tf_op jit(solution)/shard_map/ppermute | solution.py:426
  21.5 0.0 collective-permute-done.3.over_even_ref
  21.6 5.2 %collective-permute-done.4.over_odd_ref = f32[48,1152]{1,0:T(8,128)S(1)} collective-permute-done((f32[48,1152]{1,0:T(8,128)S(1)}, f32[48,1152]{1,0:T(8,128)S(1)}, u32[]{:S(2)}, u32[]{:S(2)}) %collective-permute-start.4) | collective-permute-done | bytes 221216 | tf_op jit(solution)/shard_map/ppermute | solution.py:426
  26.8 4.3 %second.1 = (f32[9960,128]{1,0:T(8,128)S(1)}, f32[3320,128]{1,0:T(8,128)S(1)}, f32[48,1024]{1,0:T(8,128)S(1)}, f32[48,1024]{1,0:T(8,128)S(1)}, f32[48,1024]{1,0:T(8,128)S(1)}, /*index=5*/f32[48,128]{1,0:T(8,128)S(1)}) custom-call(f32[9960,128]{1,0:T(8,128)S(1)} %get-tuple-element.39.dual_in, f32[3320,128]{1,0:T(8,128)S(1)} %get-tuple-element.34.sign_in, ...), custom_call_target="tpu_custom_call" | custom-call | flops 2000000000 | bytes 15912448 | tf_op jit(solution)/shard_map/second/pallas_call | solution.py:404
  31.1 4.4 %collective-permute-start.5 = (f32[48,1024]{1,0:T(8,128)S(1)}, f32[48,1024]{1,0:T(8,128)S(1)}, u32[]{:S(2)}, u32[]{:S(2)}) collective-permute-start(f32[48,1024]{1,0:T(8,128)S(1)} %get-tuple-element.54), channel_id=1, source_target_pairs={{0,2},{2,4},{4,6},{6,8},{8,10},{10,12},{12,14},{14,16},{16,18},{18... | collective-permute-start | bytes 589832 | tf_op jit(solution)/shard_map/ppermute | solution.py:432
  35.5 3.1 %collective-permute-start.6 = (f32[48,128]{1,0:T(8,128)S(1)}, f32[48,128]{1,0:T(8,128)S(1)}, u32[]{:S(2)}, u32[]{:S(2)}) collective-permute-start(f32[48,128]{1,0:T(8,128)S(1)} %get-tuple-element.55), channel_id=1, source_target_pairs={{0,1},{2,3},{4,5},{6,7},{8,9},{10,11},{12,13},{14,15},{16,17},{18,... | collective-permute-start | bytes 73736 | tf_op jit(solution)/shard_map/ppermute | solution.py:432
  38.5 2.8 %store.1 = (f32[3,362,1,8,128]{4,3,2,1,0:T(8,128)}, f32[362,1,8,128]{3,2,1,0:T(8,128)}) custom-call(f32[9960,128]{1,0:T(8,128)S(1)} %get-tuple-element.58.dual_ref, f32[3320,128]{1,0:T(8,128)S(1)} %get-tuple-element.59.sign_in), custom_call_target="tpu_custom_call" | custom-call | flops 2000000000 | bytes 12730368 | tf_op jit(solution)/shard_map/store/pallas_call | solution.py:404
  41.3 0.0 collective-permute-done.6.y_ref
  41.3 0.0 collective-permute-done.5.x_ref
  41.4 0.8 %last.1 = (f32[360,128]{1,0:T(8,128)}, f32[360,128]{1,0:T(8,128)}) custom-call(f32[48,1024]{1,0:T(8,128)S(1)} %get-tuple-element.52.base_ref, f32[48,1024]{1,0:T(8,128)S(1)} %get-tuple-element.41.inverse_ref, f32[48,1024]{1,0:T(8,128)S(1)} %get-tuple-element.53.coef_ref, f32[48,1024]{1,0:T(8,128)S(1)} %collective-permute-done.5.x_ref, ...), custom_call_target="tpu_custom_call" | custom-call | flops 1000000 | bytes 1179648 | tf_op jit(solution)/shard_map/last/pallas_call | solution.py:404
  (1 shorter events, 0.0 us)
Async XLA Ops:
  0.6 8.2 %copy-start = (f32[45,1,8,128]{3,2,1,0:T(8,128)S(1)}, f32[45,1,8,128]{3,2,1,0:T(8,128)}, u32[]{:S(2)}) copy-start(f32[45,1,8,128]{3,2,1,0:T(8,128)} %param.12) | copy-start | bytes 552964
  0.6 8.2 %copy-start.2 = (s32[1,8,128]{2,1,0:T(8,128)S(1)}, s32[1,8,128]{2,1,0:T(8,128)}, u32[]{:S(2)}) copy-start(s32[1,8,128]{2,1,0:T(8,128)} %param.11) | copy-start | bytes 12292
  0.7 8.2 %copy-start.1 = (f32[45,1,8,128]{3,2,1,0:T(8,128)S(1)}, f32[45,1,8,128]{3,2,1,0:T(8,128)}, u32[]{:S(2)}) copy-start(f32[45,1,8,128]{3,2,1,0:T(8,128)} %param.8) | copy-start | bytes 552964
  0.7 8.2 %collective-permute-start = (f32[45,1,8,128]{3,2,1,0:T(8,128)}, f32[45,1,8,128]{3,2,1,0:T(8,128)S(1)}, u32[]{:S(2)}, u32[]{:S(2)}) collective-permute-start(f32[45,1,8,128]{3,2,1,0:T(8,128)} %param.13), channel_id=1, source_target_pairs={{2,0},{4,2},{6,4},{8,6},{10,8},{12,10},{14,12},{16,14},{18,16},{20... | collective-permute-start | bytes 552968 | tf_op jit(solution)/shard_map/ppermute | solution.py:432
  3.7 5.2 %collective-permute-start.1 = (f32[45,128]{1,0:T(8,128)S(1)}, f32[45,128]{1,0:T(8,128)S(1)}, u32[]{:S(2)}, u32[]{:S(2)}) collective-permute-start(f32[45,128]{1,0:T(8,128)S(1)} %bitcast.20), channel_id=1, source_target_pairs={{1,0},{3,2},{5,4},{7,6},{9,8},{11,10},{13,12},{15,14},{17,16},{19,... | collective-permute-start | bytes 69128 | tf_op jit(solution)/shard_map/ppermute | solution.py:432
  12.2 4.2 %collective-permute-start.2 = (f32[96,128]{1,0:T(8,128)S(1)}, f32[96,128]{1,0:T(8,128)S(1)}, u32[]{:S(2)}, u32[]{:S(2)}) collective-permute-start(f32[96,128]{1,0:T(8,128)S(1)} %get-tuple-element.44), channel_id=1, source_target_pairs={{0,1},{1,0},{2,3},{3,2},{4,5},{5,4},{6,7},{7,6},{8,9},{9,8},{10,11... | collective-permute-start | bytes 147464 | tf_op jit(solution)/shard_map/ppermute | solution.py:426
  16.5 5.1 %collective-permute-start.3 = (f32[48,1152]{1,0:T(8,128)S(1)}, f32[48,1152]{1,0:T(8,128)S(1)}, u32[]{:S(2)}, u32[]{:S(2)}) collective-permute-start(f32[48,1152]{1,0:T(8,128)S(1)} %get-tuple-element.49), channel_id=1, source_target_pairs={{0,2},{2,0},{4,6},{6,4},{8,10},{10,8},{12,14},{14,12},{16,18},{18,... | collective-permute-start | bytes 663560 | tf_op jit(solution)/shard_map/ppermute | solution.py:426
  17.1 9.7 %collective-permute-start.4 = (f32[48,1152]{1,0:T(8,128)S(1)}, f32[48,1152]{1,0:T(8,128)S(1)}, u32[]{:S(2)}, u32[]{:S(2)}) collective-permute-start(f32[48,1152]{1,0:T(8,128)S(1)} %get-tuple-element.50), channel_id=1, source_target_pairs={{2,4},{4,2},{6,8},{8,6},{10,12},{12,10},{14,16},{16,14},{18,20},{2... | collective-permute-start | bytes 663560 | tf_op jit(solution)/shard_map/ppermute | solution.py:426
  31.1 10.3 %collective-permute-start.5 = (f32[48,1024]{1,0:T(8,128)S(1)}, f32[48,1024]{1,0:T(8,128)S(1)}, u32[]{:S(2)}, u32[]{:S(2)}) collective-permute-start(f32[48,1024]{1,0:T(8,128)S(1)} %get-tuple-element.54), channel_id=1, source_target_pairs={{0,2},{2,4},{4,6},{6,8},{8,10},{10,12},{12,14},{14,16},{16,18},{18... | collective-permute-start | bytes 589832 | tf_op jit(solution)/shard_map/ppermute | solution.py:432
  35.5 5.9 %collective-permute-start.6 = (f32[48,128]{1,0:T(8,128)S(1)}, f32[48,128]{1,0:T(8,128)S(1)}, u32[]{:S(2)}, u32[]{:S(2)}) collective-permute-start(f32[48,128]{1,0:T(8,128)S(1)} %get-tuple-element.55), channel_id=1, source_target_pairs={{0,1},{2,3},{4,5},{6,7},{8,9},{10,11},{12,13},{14,15},{16,17},{18,... | collective-permute-start | bytes 73736 | tf_op jit(solution)/shard_map/ppermute | solution.py:432

commit v3 on v2

--- a/solution.py
+++ b/solution.py
@@ -271,19 +271,27 @@
 
 
 def from_partners(axis, over_even, over_odd):
+    if over_odd is None:
+        over_odd = jnp.zeros_like(over_even)
     odd = jnp.broadcast_to(is_odd(axis), over_even.shape)
     return jnp.where(odd, over_even, over_odd), jnp.where(odd, over_odd, over_even)
 
 
-def first_kernel(s, dual_in, sign_in, cat_ref, adjoint_ref, e_ref, ex_ref, ey_ref, coef_ref, signal_ref,
-                 mask_ref, response_ref, dual_ref, base_ref, inverse_ref, coef_out, target_ref,
-                 x_ref, v_ref, y_ref, *refs):
+def received_at(axis, refs):
+    return from_partners(axis, refs[0][...], refs[1][...] if len(refs) > 1 else None)
+
+
+def first_kernel(s, dual_in, sign_in, cat_ref, adjoint_ref, e_ref, ex_ref, coef_ref, signal_ref,
+                 mask_ref, response_ref, *refs):
+    pairs_y = len(pair_lists(lax.axis_size("gy")))
+    received, refs = refs[:pairs_y], refs[pairs_y:]
+    dual_ref, base_ref, inverse_ref, coef_out, target_ref, x_ref, y_ref, *send_refs = refs[:-8]
     e_cat, diff = refs[-8:-6]
-    send_refs = refs[:-8]
     keep_x, keep_y = last_flags()
     here = planes_of(e_ref, s.count, s.rows, s.padded)
     there = planes_of(ex_ref, s.count, s.rows, s.padded)
-    edge_row = jnp.concatenate([ey_ref[...], jnp.zeros((s.padded - s.count, LANES), F32)], 0)
+    _, edge_row = received_at("gy", received)
+    edge_row = jnp.concatenate([edge_row, jnp.zeros((s.padded - s.count, LANES), F32)], 0)
     e_cat[2 * s.padded : s.low_row, :] = jnp.zeros((s.low_row - 2 * s.padded, s.width + LANES), BF16)
     put_cat(e_cat, jnp.concatenate(
         [(there - here) * (STEP_DUAL * keep_x),
@@ -305,30 +313,16 @@
     coef_out[...] = coef
     target_ref[...] = target
     x_ref[...] = from_x
-    v_ref[...] = ahead
     y_ref[...] = from_y
-    sends = to_partners(
-        "gy", jnp.concatenate([from_y, from_y], 0),
-        jnp.concatenate([ahead[:, 0:LANES], from_x[:, 0:LANES]], 0))
-    for send_ref, send in zip(send_refs, sends):
-        send_ref[...] = send
-
-
-def middle_kernel(s, base_in, inverse_ref, x_ref, v_ref, *refs):
-    *received, base_ref, even_ref, odd_ref, side_ref = refs
-    over_even = received[0][...]
-    over_odd = received[1][...] if len(received) > 1 else jnp.zeros_like(over_even)
-    below, above = from_partners("gy", over_even, over_odd)
-    base_ref[...] = base_in[...]
-    base_ref[:, 0:LANES] -= STEP_PRIMAL * below[0 : s.padded]
-    side_ref[...] = above[0 : s.padded]
-    ahead = v_ref[...]
-    row_index = lax.broadcasted_iota(jnp.int32, (s.padded, LANES), 0)
-    change = (2.0 * STEP_PRIMAL) * below[0 : s.padded] * inverse_ref[:, 0:LANES]
-    change = jnp.where(row_index < s.count, change, 0.0)
-    down = jnp.concatenate([ahead[:, 0:LANES] - change, ahead[:, LANES:], change], 1)
-    up = jnp.concatenate([x_ref[...], above[s.padded :]], 1)
-    even_ref[...], odd_ref[...] = to_partners("gx", up, down)
+    messages = (
+        to_partners("gx", from_x, ahead) + to_partners("gy", from_y, ahead[:, 0:LANES])[:pairs_y]
+        + to_partners("gy", from_y, from_x[:, 0:LANES])[:pairs_y])
+    for send_ref, message in zip(send_refs, messages):
+        send_ref[...] = message
+
+
+def add_first_row(planes, row):
+    return jnp.concatenate([planes[:, 0:LANES] + row, planes[:, LANES:]], 1)
 
 
 def ahead_of(s, message, own, response):
@@ -339,19 +333,21 @@
 
 
 def second_kernel(s, dual_in, sign_in, cat_ref, adjoint_ref, base_ref, inverse_ref, coef_ref, target_ref,
-                  x_ref, y_ref, over_even_ref, over_odd_ref, side_ref, response_ref,
-                  dual_ref, sign_ref, base_out, coef_out, x_out, y_out,
-                  e_cat, change, *splits):
+                  x_ref, y_ref, response_ref, *refs):
+    *received, dual_ref, sign_ref, base_out, coef_out, x_out, y_out = refs[:-8]
+    e_cat, change, *splits = refs[-8:]
+    pairs_y = (len(received) - 2) // 2
     keep_x, keep_y = last_flags()
-    below, above = from_partners("gx", over_even_ref[...], over_odd_ref[...])
+    below, above = received_at("gx", received[:2])
+    below_y, above_y = received_at("gy", received[2 : 2 + pairs_y])
+    below_d, above_d = received_at("gy", received[2 + pairs_y :])
     response = response_ref[...]
-    inverse = inverse_ref[...]
     coef = coef_ref[...]
-    updated = (base_ref[...] - STEP_PRIMAL * below[:, 0 : s.width]) * inverse
+    updated = (base_ref[...] - STEP_PRIMAL * add_first_row(below, below_y)) * inverse_ref[...]
     here = 2.0 * updated - coef
     wide = jnp.concatenate([response] * s.rows, 1)
-    there = ahead_of(s, above[:, 0 : s.width], x_ref[...], wide)
-    edge_row = ahead_of(s, side_ref[...], y_ref[...] + below[:, s.width :], response)
+    there = ahead_of(s, above, add_first_row(x_ref[...], below_d), wide)
+    edge_row = ahead_of(s, above_y, y_ref[...] + above_d, response)
     e_cat[2 * s.padded : s.low_row, :] = jnp.zeros((s.low_row - 2 * s.padded, 4 * s.width), BF16)
     edge = lane_edge()[0:1]
     planes = [here[:, row * LANES : (row + 1) * LANES] for row in range(s.rows)]
@@ -386,9 +382,10 @@
         copy.wait()
 
 
-def last_kernel(s, base_ref, inverse_ref, coef_ref, x_ref, y_ref, coef_out, extra_out):
-    total = jnp.concatenate(
-        [x_ref[:, 0:LANES] + y_ref[...], x_ref[:, LANES:]], 1)
+def last_kernel(s, base_ref, inverse_ref, coef_ref, x_ref, *refs):
+    *received, coef_out, extra_out = refs
+    below_y, _ = received_at("gy", received)
+    total = add_first_row(x_ref[...], below_y)
     updated = (base_ref[...] - STEP_PRIMAL * total) * inverse_ref[...]
     extra = 2.0 * updated - coef_ref[...]
     for row in range(s.rows):
@@ -426,6 +423,20 @@
     return [lax.ppermute(send, axis, pairs) for send, pairs in zip(sends, lists)]
 
 
+def diagonal_exchange(sends):
+    count_x, count_y = lax.axis_size("gx"), lax.axis_size("gy")
+    received = []
+    for send, pairs in zip(sends, pair_lists(count_y)):
+        flat = []
+        for low, high in pairs:
+            if low < high:
+                for x in range(1, count_x):
+                    ends = (x * count_y + low, (x - 1) * count_y + high)
+                    flat += [ends, ends[::-1]]
+        received.append(lax.ppermute(send, ("gx", "gy"), flat))
+    return received
+
+
 def shift(value, axis, steps):
     count = lax.axis_size(axis)
     pairs = [(i, i + steps) for i in range(count) if 0 <= i + steps < count]
@@ -448,7 +459,8 @@
     plane = f32(padded, width)
 
     after_x = shift(extrapolated, "gx", -1)
-    after_y = shift(extrapolated[:, 0, 0], "gy", -1)
+    pairs_y = len(pair_lists(lax.axis_size("gy")))
+    after_y = exchange("gy", [extrapolated[:, 0, 0]] * pairs_y)
     in_hbm = lambda a: pltpu.with_memory_space_constraint(a, pltpu.HBM)
     line = f32(padded, lanes)
     duals, sign, own, cat, adjoint, column = call(
@@ -460,29 +472,23 @@
          pltpu.VMEM((LANES, round_up(dirs, LANES)), F32), pltpu.VMEM((s.depth, width), BF16),
          pltpu.VMEM((dirs, width), F32), pltpu.SemaphoreType.DMA((4 * rows + 3,))],
         "load", 2_000_000_000, in_specs=[hbm] * 5)
-    pairs_y = len(pair_lists(lax.axis_size("gy")))
-    duals, base, inverse, coef, target, from_x, ahead, from_y, *sends = call(
+    duals, base, inverse, coef, target, from_x, from_y, *sends = call(
         functools.partial(first_kernel, s),
-        (dual,) + (plane,) * 6 + (line,) + (f32(2 * padded, lanes),) * pairs_y,
-        (duals, sign, cat, adjoint, own, flat(after_x), after_y, flat(coefficients), flat(signal),
-         mask[0], column),
+        (dual,) + (plane,) * 5 + (line,) + (plane,) * 2 + (line,) * (2 * pairs_y),
+        [duals, sign, cat, adjoint, own, flat(after_x), flat(coefficients), flat(signal),
+         mask[0], column] + after_y,
         [pltpu.VMEM((s.depth, width + LANES), BF16), pltpu.VMEM((dirs, width + LANES), F32)] + splits,
         "first", 2_000_000_000)
-    message = f32(padded, width + lanes)
-    base, to_even, to_odd, side = call(
-        functools.partial(middle_kernel, s),
-        (plane, message, message, line),
-        [base, inverse, from_x, ahead] + exchange("gy", sends), [], "middle", 1_000_000)
-    over_even, over_odd = exchange("gx", [to_even, to_odd])
+    received = exchange("gx", sends[:2])
+    received += exchange("gy", sends[2 : 2 + pairs_y]) + diagonal_exchange(sends[2 + pairs_y :])
     duals, sign, base, coef, from_x, from_y = call(
         functools.partial(second_kernel, s),
         (dual, signs, plane, plane, plane, line),
-        (duals, sign, cat, adjoint, base, inverse, coef, target, from_x, from_y, over_even, over_odd,
-         side, column),
+        [duals, sign, cat, adjoint, base, inverse, coef, target, from_x, from_y, column] + received,
         [pltpu.VMEM((s.depth, 4 * width), BF16), pltpu.VMEM((dirs, 4 * width), F32)] + splits,
         "second", 2_000_000_000)
     below_x = shift(from_x, "gx", 1)
-    below_y = shift(from_y, "gy", 1)
+    below_y = exchange("gy", [from_y] * pairs_y)
     grad_out, sign_out = call(
         functools.partial(store_kernel, s),
         (f32(*dual_grad.shape), f32(*dual_sign.shape)), (duals, sign),
@@ -490,7 +496,7 @@
     coef_out, extra_out = call(
         functools.partial(last_kernel, s),
         (f32(count * rows, lanes), f32(count * rows, lanes)),
-        (base, inverse, coef, below_x, below_y), [], "last", 1_000_000)
+        [base, inverse, coef, below_x] + below_y, [], "last", 1_000_000)
     return (coef_out.reshape(signal.shape), extra_out.reshape(signal.shape), grad_out, sign_out)
 
 

time: 42.4 us -> 36.6 us (0.86)
  the two profiles are of different devices: /device:TPU:1 before, /device:TPU:24 now
where the time goes in v3:
time: 36.6 us; the launch traced here: 36.4 us
  Pallas kernels  14.4 us (39%)
  starting transfers between devices  14.2 us (39%)
  waiting for transfers between devices  6.07 us (17%)
  local copies, waits for them, and re-layouts  0.96 us (3%)
  between operations  0.79 us (2%)
    pallas_call x5, Pallas kernels, call(): pl.pallas_call(kernel, out_shape=outs, in_specs=in_specs or [vmem] * len(...  14.4 us
    ppermute x5, starting transfers between devices, exchange(): lax.ppermute(send, axis, pairs)  5.52 us
    ppermute x2, starting transfers between devices, shift(): return lax.ppermute(value, axis, pairs)  4.81 us
    ppermute x1, starting transfers between devices, diagonal_exchange(): received.append(lax.ppermute(send, ('gx', 'gy'), flat))  3.91 us
    ppermute x1, waiting for transfers between devices, diagonal_exchange(): received.append(lax.ppermute(send, ('gx', 'gy'), flat))  3 us
    ppermute x2, waiting for transfers between devices, shift(): return lax.ppermute(value, axis, pairs)  2.07 us
    ppermute x5, waiting for transfers between devices, exchange(): lax.ppermute(send, axis, pairs)  1 us
    slice x1, local copies, waits for them, and re-layouts, per_device(): after_y = exchange('gy', [extrapolated[:, 0, 0]] * pairs_y)  0.95 us
  transfers between devices with their start and end apart: 8, of which 3 were waited for; matrix products, arithmetic and copies ran while one was open for 3% of the time, Pallas kernels for 16%

profile of v3, /device:TPU:24, one launch (start us, length us, event | category | flops | bytes accessed | tf_op | source)
XLA Modules:
  0.0 36.4 jit_solution(7643568160484126450)
XLA Ops:
  0.6 0.0 copy-start
  0.6 0.0 copy-start.2
  0.7 0.0 copy-start.1
  0.7 2.9 %collective-permute-start = (f32[45,1,8,128]{3,2,1,0:T(8,128)}, f32[45,1,8,128]{3,2,1,0:T(8,128)S(1)}, u32[]{:S(2)}, u32[]{:S(2)}) collective-permute-start(f32[45,1,8,128]{3,2,1,0:T(8,128)} %param.13), channel_id=1, source_target_pairs={{2,0},{4,2},{6,4},{8,6},{10,8},{12,10},{14,12},{16,14},{18,16},{20... | collective-permute-start | bytes 552968 | tf_op jit(solution)/shard_map/ppermute | solution.py:443
  3.6 0.9 %slice.3 = f32[45,1,1,128]{3,2,1,0:T(1,128)S(1)} slice(f32[45,1,8,128]{3,2,1,0:T(8,128)} %param.13), slice={[0:45], [0:1], [0:1], [0:128]} | slice | bytes 46080 | tf_op jit(solution)/shard_map/slice | solution.py:463
  4.5 1.6 %collective-permute-start.1 = (f32[45,128]{1,0:T(8,128)S(1)}, f32[45,128]{1,0:T(8,128)S(1)}, u32[]{:S(2)}, u32[]{:S(2)}) collective-permute-start(f32[45,128]{1,0:T(8,128)S(1)} %bitcast.20), channel_id=1, source_target_pairs={{0,1},{1,0},{2,3},{3,2},{4,5},{5,4},{6,7},{7,6},{8,9},{9,8},{10,11... | collective-permute-start | bytes 69128 | tf_op jit(solution)/shard_map/ppermute | solution.py:423
  6.1 3.2 %load.1 = (f32[9960,128]{1,0:T(8,128)S(1)}, f32[3320,128]{1,0:T(8,128)S(1)}, f32[360,128]{1,0:T(8,128)S(1)}, bf16[368,176]{1,0:T(8,128)(2,1)S(1)}, bf16[96,368]{1,0:T(8,128)(2,1)S(1)}, /*index=5*/f32[48,128]{1,0:T(8,128)S(1)}) custom-call(f32[360,128]{1,0:T(8,128)} %bitcast.21, f32[45,362]{1,0:T(8,128)} %bitcast.24, f32[1,45]{1,0:T(1,128)} %bitcast.25, ...), custom_call_target="tpu_custom_call" | custom-call | flops 2000000000 | bytes 13389116 | tf_op jit(solution)/shard_map/load/pallas_call | solution.py:401
  9.2 0.0 collective-permute-done.1.refs_0_
  9.3 0.0 collective-permute-done
  9.3 0.0 copy-done
  9.3 0.0 copy-done.2
  9.3 0.0 copy-done.1
  9.3 3.3 %first.1 = (f32[9960,128]{1,0:T(8,128)S(1)}, f32[48,1024]{1,0:T(8,128)S(1)}, f32[48,1024]{1,0:T(8,128)S(1)}, f32[48,1024]{1,0:T(8,128)S(1)}, f32[48,1024]{1,0:T(...) custom-call(f32[9960,128]{1,0:T(8,128)S(1)} %get-tuple-element.31.du, ...), custom_call_target="tpu_custom_call" | custom-call | flops 2000000000 | bytes 14338048 | tf_op jit(solution)/shard_map/first/pallas_call | solution.py:401
  12.6 0.1 collective-permute-start.2
  12.7 2.6 %collective-permute-start.3 = (f32[48,1024]{1,0:T(8,128)S(1)}, f32[48,1024]{1,0:T(8,128)S(1)}, u32[]{:S(2)}, u32[]{:S(2)}) collective-permute-start(f32[48,1024]{1,0:T(8,128)S(1)} %get-tuple-element.45), channel_id=1, source_target_pairs={{2,4},{4,2},{6,8},{8,6},{10,12},{12,10},{14,16},{16,14},{18,20},{2... | collective-permute-start | bytes 589832 | tf_op jit(solution)/shard_map/ppermute | solution.py:423
  15.2 1.2 %collective-permute-start.4 = (f32[48,128]{1,0:T(8,128)S(1)}, f32[48,128]{1,0:T(8,128)S(1)}, u32[]{:S(2)}, u32[]{:S(2)}) collective-permute-start(f32[48,128]{1,0:T(8,128)S(1)} %get-tuple-element.46), channel_id=1, source_target_pairs={{0,1},{1,0},{2,3},{3,2},{4,5},{5,4},{6,7},{7,6},{8,9},{9,8},{10,11... | collective-permute-start | bytes 73736 | tf_op jit(solution)/shard_map/ppermute | solution.py:423
  16.5 3.9 %collective-permute-start.5 = (f32[48,128]{1,0:T(8,128)S(1)}, f32[48,128]{1,0:T(8,128)S(1)}, u32[]{:S(2)}, u32[]{:S(2)}) collective-permute-start(f32[48,128]{1,0:T(8,128)S(1)} %get-tuple-element.47), channel_id=1, source_target_pairs={{2,1},{1,2},{4,3},{3,4},{6,5},{5,6},{8,7},{7,8},{10,9},{9,10},{12,... | collective-permute-start | bytes 73736 | tf_op jit(solution)/shard_map/ppermute | solution.py:436
  20.4 0.0 collective-permute-done.4.refs_2_
  20.4 3.0 %collective-permute-done.5.refs_3_ = f32[48,128]{1,0:T(8,128)S(1)} collective-permute-done((f32[48,128]{1,0:T(8,128)S(1)}, f32[48,128]{1,0:T(8,128)S(1)}, u32[]{:S(2)}, u32[]{:S(2)}) %collective-permute-start.5) | collective-permute-done | bytes 24608 | tf_op jit(solution)/shard_map/ppermute | solution.py:436
  23.4 0.0 collective-permute-done.2.refs_0_
  23.4 0.0 collective-permute-done.3.refs_1_
  23.4 4.3 %second.1 = (f32[9960,128]{1,0:T(8,128)S(1)}, f32[3320,128]{1,0:T(8,128)S(1)}, f32[48,1024]{1,0:T(8,128)S(1)}, f32[48,1024]{1,0:T(8,128)S(1)}, f32[48,1024]{1,0:T(8,128)S(1)}, /*index=5*/f32[48,128]{1,0:T(8,128)S(1)}) custom-call(f32[9960,128]{1,0:T(8,128)S(1)} %get-tuple-element.37.dual_in, f32[3320,128]{1,0:T(8,128)S(1)} %get-tuple-element.32.sign_in, ...), custom_call_target="tpu_custom_call" | custom-call | flops 2000000000 | bytes 15887872 | tf_op jit(solution)/shard_map/second/pallas_call | solution.py:401
  27.7 1.9 %collective-permute-start.6 = (f32[48,1024]{1,0:T(8,128)S(1)}, f32[48,1024]{1,0:T(8,128)S(1)}, u32[]{:S(2)}, u32[]{:S(2)}) collective-permute-start(f32[48,1024]{1,0:T(8,128)S(1)} %get-tuple-element.50), channel_id=1, source_target_pairs={{0,2},{2,4},{4,6},{6,8},{8,10},{10,12},{12,14},{14,16},{16,18},{18... | collective-permute-start | bytes 589832 | tf_op jit(solution)/shard_map/ppermute | solution.py:443
  29.6 0.1 collective-permute-start.7
  29.7 2.8 %store.1 = (f32[3,362,1,8,128]{4,3,2,1,0:T(8,128)}, f32[362,1,8,128]{3,2,1,0:T(8,128)}) custom-call(f32[9960,128]{1,0:T(8,128)S(1)} %get-tuple-element.54.dual_ref, f32[3320,128]{1,0:T(8,128)S(1)} %get-tuple-element.55.sign_in), custom_call_target="tpu_custom_call" | custom-call | flops 2000000000 | bytes 12730368 | tf_op jit(solution)/shard_map/store/pallas_call | solution.py:401
  32.5 1.0 %collective-permute-done.7.refs_0_ = f32[48,128]{1,0:T(8,128)S(1)} collective-permute-done((f32[48,128]{1,0:T(8,128)S(1)}, f32[48,128]{1,0:T(8,128)S(1)}, u32[]{:S(2)}, u32[]{:S(2)}) %collective-permute-start.7) | collective-permute-done | bytes 24608 | tf_op jit(solution)/shard_map/ppermute | solution.py:423
  33.5 2.1 %collective-permute-done.6.x_ref = f32[48,1024]{1,0:T(8,128)S(1)} collective-permute-done((f32[48,1024]{1,0:T(8,128)S(1)}, f32[48,1024]{1,0:T(8,128)S(1)}, u32[]{:S(2)}, u32[]{:S(2)}) %collective-permute-start.6) | collective-permute-done | bytes 196640 | tf_op jit(solution)/shard_map/ppermute | solution.py:443
  35.6 0.8 %last.1 = (f32[360,128]{1,0:T(8,128)}, f32[360,128]{1,0:T(8,128)}) custom-call(f32[48,1024]{1,0:T(8,128)S(1)} %get-tuple-element.48.base_ref, f32[48,1024]{1,0:T(8,128)S(1)} %get-tuple-element.39.inverse_ref, f32[48,1024]{1,0:T(8,128)S(1)} %get-tuple-element.49.coef_ref, f32[48,1024]{1,0:T(8,128)S(1)} %collective-permute-done.6.x_ref, ...), custom_call_target="tpu_custom_call" | custom-call | flops 1000000 | bytes 1179648 | tf_op jit(solution)/shard_map/last/pallas_call | solution.py:401
  (1 shorter events, 0.0 us)
Async XLA Ops:
  0.6 8.6 %copy-start = (f32[45,1,8,128]{3,2,1,0:T(8,128)S(1)}, f32[45,1,8,128]{3,2,1,0:T(8,128)}, u32[]{:S(2)}) copy-start(f32[45,1,8,128]{3,2,1,0:T(8,128)} %param.12) | copy-start | bytes 552964
  0.6 8.6 %copy-start.2 = (s32[1,8,128]{2,1,0:T(8,128)S(1)}, s32[1,8,128]{2,1,0:T(8,128)}, u32[]{:S(2)}) copy-start(s32[1,8,128]{2,1,0:T(8,128)} %param.11) | copy-start | bytes 12292
  0.7 8.6 %copy-start.1 = (f32[45,1,8,128]{3,2,1,0:T(8,128)S(1)}, f32[45,1,8,128]{3,2,1,0:T(8,128)}, u32[]{:S(2)}) copy-start(f32[45,1,8,128]{3,2,1,0:T(8,128)} %param.8) | copy-start | bytes 552964
  0.7 8.6 %collective-permute-start = (f32[45,1,8,128]{3,2,1,0:T(8,128)}, f32[45,1,8,128]{3,2,1,0:T(8,128)S(1)}, u32[]{:S(2)}, u32[]{:S(2)}) collective-permute-start(f32[45,1,8,128]{3,2,1,0:T(8,128)} %param.13), channel_id=1, source_target_pairs={{2,0},{4,2},{6,4},{8,6},{10,8},{12,10},{14,12},{16,14},{18,16},{20... | collective-permute-start | bytes 552968 | tf_op jit(solution)/shard_map/ppermute | solution.py:443
  4.5 4.7 %collective-permute-start.1 = (f32[45,128]{1,0:T(8,128)S(1)}, f32[45,128]{1,0:T(8,128)S(1)}, u32[]{:S(2)}, u32[]{:S(2)}) collective-permute-start(f32[45,128]{1,0:T(8,128)S(1)} %bitcast.20), channel_id=1, source_target_pairs={{0,1},{1,0},{2,3},{3,2},{4,5},{5,4},{6,7},{7,6},{8,9},{9,8},{10,11... | collective-permute-start | bytes 69128 | tf_op jit(solution)/shard_map/ppermute | solution.py:423
  12.6 10.8 %collective-permute-start.2 = (f32[48,1024]{1,0:T(8,128)S(1)}, f32[48,1024]{1,0:T(8,128)S(1)}, u32[]{:S(2)}, u32[]{:S(2)}) collective-permute-start(f32[48,1024]{1,0:T(8,128)S(1)} %get-tuple-element.44), channel_id=1, source_target_pairs={{0,2},{2,0},{4,6},{6,4},{8,10},{10,8},{12,14},{14,12},{16,18},{18,... | collective-permute-start | bytes 589832 | tf_op jit(solution)/shard_map/ppermute | solution.py:423
  12.7 10.7 %collective-permute-start.3 = (f32[48,1024]{1,0:T(8,128)S(1)}, f32[48,1024]{1,0:T(8,128)S(1)}, u32[]{:S(2)}, u32[]{:S(2)}) collective-permute-start(f32[48,1024]{1,0:T(8,128)S(1)} %get-tuple-element.45), channel_id=1, source_target_pairs={{2,4},{4,2},{6,8},{8,6},{10,12},{12,10},{14,16},{16,14},{18,20},{2... | collective-permute-start | bytes 589832 | tf_op jit(solution)/shard_map/ppermute | solution.py:423
  15.2 5.1 %collective-permute-start.4 = (f32[48,128]{1,0:T(8,128)S(1)}, f32[48,128]{1,0:T(8,128)S(1)}, u32[]{:S(2)}, u32[]{:S(2)}) collective-permute-start(f32[48,128]{1,0:T(8,128)S(1)} %get-tuple-element.46), channel_id=1, source_target_pairs={{0,1},{1,0},{2,3},{3,2},{4,5},{5,4},{6,7},{7,6},{8,9},{9,8},{10,11... | collective-permute-start | bytes 73736 | tf_op jit(solution)/shard_map/ppermute | solution.py:423
  16.5 6.9 %collective-permute-start.5 = (f32[48,128]{1,0:T(8,128)S(1)}, f32[48,128]{1,0:T(8,128)S(1)}, u32[]{:S(2)}, u32[]{:S(2)}) collective-permute-start(f32[48,128]{1,0:T(8,128)S(1)} %get-tuple-element.47), channel_id=1, source_target_pairs={{2,1},{1,2},{4,3},{3,4},{6,5},{5,6},{8,7},{7,8},{10,9},{9,10},{12,... | collective-permute-start | bytes 73736 | tf_op jit(solution)/shard_map/ppermute | solution.py:436
  27.7 7.9 %collective-permute-start.6 = (f32[48,1024]{1,0:T(8,128)S(1)}, f32[48,1024]{1,0:T(8,128)S(1)}, u32[]{:S(2)}, u32[]{:S(2)}) collective-permute-start(f32[48,1024]{1,0:T(8,128)S(1)} %get-tuple-element.50), channel_id=1, source_target_pairs={{0,2},{2,4},{4,6},{6,8},{8,10},{10,12},{12,14},{14,16},{16,18},{18... | collective-permute-start | bytes 589832 | tf_op jit(solution)/shard_map/ppermute | solution.py:443
  29.6 3.9 %collective-permute-start.7 = (f32[48,128]{1,0:T(8,128)S(1)}, f32[48,128]{1,0:T(8,128)S(1)}, u32[]{:S(2)}, u32[]{:S(2)}) collective-permute-start(f32[48,128]{1,0:T(8,128)S(1)} %get-tuple-element.51), channel_id=1, source_target_pairs={{0,1},{1,0},{2,3},{3,2},{4,5},{5,4},{6,7},{7,6},{8,9},{9,8},{10,11... | collective-permute-start | bytes 73736 | tf_op jit(solution)/shard_map/ppermute | solution.py:423

commit v4 on v3

--- a/solution.py
+++ b/solution.py
@@ -7,6 +7,7 @@
 from jax.experimental.pallas import tpu as pltpu
 from jax.sharding import PartitionSpec as P
 
+
 STEP_PRIMAL = 0.25
 STEP_DUAL = 0.02
 TV_WEIGHT = 0.5
@@ -54,18 +55,11 @@
         out_ref[:, start : start + size] = matmul(left_ref[...], right_ref[:, start : start + size])
 
 
-def harmonics(adjoint_ref, high_ref, low_ref, start, size, padded):
-    first = matmul(adjoint_ref[...], high_ref[:, start : start + size])
-    second = matmul(adjoint_ref[0:padded, :], low_ref[:, start : start + size])
+def harmonics(adjoint_ref, value, padded):
+    high, low = split_two(value)
+    first = matmul(adjoint_ref[...], high)
+    second = matmul(adjoint_ref[0:padded, :], low)
     return first[0:padded] + first[padded : 2 * padded] + second
-
-
-def all_harmonics(adjoint_ref, high_ref, low_ref, width, padded):
-    parts = [
-        harmonics(adjoint_ref, high_ref, low_ref, start, min(256, width - start), padded)
-        for start in range(0, width, 256)
-    ]
-    return jnp.concatenate(parts, 1)
 
 
 def last_flags():
@@ -192,9 +186,8 @@
         copy_of(0, row).wait()
 
 
-def dual_pass(s, dual_in, sign_in, dual_out, sign_out, change, highs):
+def dual_pass(s, dual_in, sign_in, dual_out, sign_out, change, back_ref):
     edge = lane_edge()
-    back_high, back_low, x_high, x_low, y_high, y_low = highs
     full = sign_out is not None
     signs = sign_out if full else sign_in
     dual_out[s.start(1, -1) : s.start(1, 0), :] = jnp.zeros((s.padded_dirs, LANES), F32)
@@ -225,9 +218,7 @@
             inner_z = dual_out[s.at(2, row, index), :] * edge
             back = signs[s.at(0, row, index), :] - (inner_z - previous_lane(inner_z))
             back = back - (dual_out[s.at(1, row, index), :] - dual_out[s.at(1, row - 1, index), :])
-            back_high[here, s.lanes(row)], back_low[here, s.lanes(row)] = split_two(back)
-            x_high[here, s.lanes(row)], x_low[here, s.lanes(row)] = split_two(
-                dual_out[s.at(0, row, index), :])
+            back_ref[here, s.lanes(row)] = back
         return carry
 
     def step(row, carry):
@@ -240,16 +231,21 @@
         lax.fori_loop(0, s.rows - 1, step, 0)
         shrink_row(s.rows - 1)
     lax.fori_loop(0, s.rows, split_row, 0)
-    for index in range(s.groups):
-        here = slice(index * GROUP, (index + 1) * GROUP)
-        y_high[here, :], y_low[here, :] = split_two(dual_out[s.at(1, s.rows - 1, index), :])
-
-
-def all_adjoints(s, adjoint_ref, splits, keep_x, keep_y):
-    back_high, back_low, x_high, x_low, y_high, y_low = splits
-    from_back = all_harmonics(adjoint_ref, back_high, back_low, s.width, s.padded)
-    from_x = all_harmonics(adjoint_ref, x_high, x_low, s.width, s.padded)
-    from_y = all_harmonics(adjoint_ref, y_high, y_low, LANES, s.padded)
+
+
+def all_adjoints(s, adjoint_ref, back_ref, dual_ref, keep_x, keep_y):
+    def plane(part, row):
+        return dual_ref[pl.ds(s.start(part, row), s.padded_dirs), :]
+
+    from_back, from_x = [], []
+    for row in range(0, s.rows, 2):
+        rows = range(row, min(row + 2, s.rows))
+        value = back_ref[:, row * LANES : (row + len(rows)) * LANES]
+        from_back.append(harmonics(adjoint_ref, value, s.padded))
+        value = jnp.concatenate([plane(0, each) for each in rows], 1)
+        from_x.append(harmonics(adjoint_ref, value, s.padded))
+    from_back, from_x = jnp.concatenate(from_back, 1), jnp.concatenate(from_x, 1)
+    from_y = harmonics(adjoint_ref, plane(1, s.rows - 1), s.padded)
     last = from_back[:, s.width - LANES :] + (1.0 - keep_y) * from_y
     total = jnp.concatenate([from_back[:, : s.width - LANES], last], 1) - keep_x * from_x
     return total, from_x, from_y
@@ -285,8 +281,8 @@
                  mask_ref, response_ref, *refs):
     pairs_y = len(pair_lists(lax.axis_size("gy")))
     received, refs = refs[:pairs_y], refs[pairs_y:]
-    dual_ref, base_ref, inverse_ref, coef_out, target_ref, x_ref, y_ref, *send_refs = refs[:-8]
-    e_cat, diff = refs[-8:-6]
+    dual_ref, base_ref, inverse_ref, coef_out, target_ref, x_ref, y_ref, *send_refs = refs[:-3]
+    e_cat, diff, back_ref = refs[-3:]
     keep_x, keep_y = last_flags()
     here = planes_of(e_ref, s.count, s.rows, s.padded)
     there = planes_of(ex_ref, s.count, s.rows, s.padded)
@@ -297,8 +293,8 @@
         [(there - here) * (STEP_DUAL * keep_x),
          (edge_row - here[:, s.width - LANES :]) * (STEP_DUAL * keep_y)], 1), s.low_row)
     wide_matmul(cat_ref, e_cat, diff, s.width + LANES)
-    dual_pass(s, dual_in, sign_in, dual_ref, None, diff, refs[-6:])
-    total, from_x, from_y = all_adjoints(s, adjoint_ref, refs[-6:], keep_x, keep_y)
+    dual_pass(s, dual_in, sign_in, dual_ref, None, diff, back_ref)
+    total, from_x, from_y = all_adjoints(s, adjoint_ref, back_ref, dual_ref, keep_x, keep_y)
     mask, response = weights(s, mask_ref, response_ref)
     weight = mask * response
     coef = planes_of(coef_ref, s.count, s.rows, s.padded)
@@ -334,8 +330,8 @@
 
 def second_kernel(s, dual_in, sign_in, cat_ref, adjoint_ref, base_ref, inverse_ref, coef_ref, target_ref,
                   x_ref, y_ref, response_ref, *refs):
-    *received, dual_ref, sign_ref, base_out, coef_out, x_out, y_out = refs[:-8]
-    e_cat, change, *splits = refs[-8:]
+    *received, dual_ref, sign_ref, base_out, coef_out, x_out, y_out = refs[:-3]
+    e_cat, change, back_ref = refs[-3:]
     pairs_y = (len(received) - 2) // 2
     keep_x, keep_y = last_flags()
     below, above = received_at("gx", received[:2])
@@ -358,8 +354,8 @@
     put_cat(e_cat, STEP_DUAL * jnp.concatenate(
         [(there - here) * keep_x, along_y, along_z, here], 1), s.low_row)
     wide_matmul(cat_ref, e_cat, change, 4 * s.width)
-    dual_pass(s, dual_in, sign_in, dual_ref, sign_ref, change, splits)
-    total, from_x, from_y = all_adjoints(s, adjoint_ref, splits, keep_x, keep_y)
+    dual_pass(s, dual_in, sign_in, dual_ref, sign_ref, change, back_ref)
+    total, from_x, from_y = all_adjoints(s, adjoint_ref, back_ref, dual_ref, keep_x, keep_y)
     base_out[...] = updated + target_ref[...] - STEP_PRIMAL * total
     coef_out[...] = updated
     x_out[...] = from_x
@@ -394,7 +390,7 @@
         extra_out[pl.ds(row, s.count, stride=s.rows), :] = extra[0 : s.count, at]
 
 
-def call(kernel, outs, ins, scratch, name, flops, in_specs=None, out_specs=None, aliases=None):
+def call(kernel, outs, ins, scratch, flops, in_specs=None, out_specs=None, aliases=None):
     vmem = pl.BlockSpec(memory_space=pltpu.VMEM)
     count = len(outs) if isinstance(outs, (tuple, list)) else 1
     size = lambda arrays: sum(a.size * a.dtype.itemsize for a in jax.tree.leaves(arrays))
@@ -408,7 +404,6 @@
         compiler_params=pltpu.CompilerParams(vmem_limit_bytes=VMEM_LIMIT),
         cost_estimate=pl.CostEstimate(
             flops=flops, bytes_accessed=size(outs) + size(list(ins)), transcendentals=0),
-        name=name,
     )(*ins)
 
 
@@ -453,7 +448,7 @@
     vmem = pl.BlockSpec(memory_space=pltpu.VMEM)
     hbm = pl.BlockSpec(memory_space=pltpu.HBM)
     dirs, padded, width = s.padded_dirs, s.padded, s.width
-    splits = [pltpu.VMEM((dirs, width), BF16)] * 4 + [pltpu.VMEM((dirs, LANES), BF16)] * 2
+    back = [pltpu.VMEM((dirs, width), F32)]
     dual = f32(3 * s.part_rows, lanes)
     signs = f32(s.part_rows, lanes)
     plane = f32(padded, width)
@@ -471,32 +466,33 @@
         [pltpu.VMEM((count, s.directions), F32), pltpu.VMEM((1, count), F32),
          pltpu.VMEM((LANES, round_up(dirs, LANES)), F32), pltpu.VMEM((s.depth, width), BF16),
          pltpu.VMEM((dirs, width), F32), pltpu.SemaphoreType.DMA((4 * rows + 3,))],
-        "load", 2_000_000_000, in_specs=[hbm] * 5)
+        2_000_000_000, in_specs=[hbm] * 5)
     duals, base, inverse, coef, target, from_x, from_y, *sends = call(
         functools.partial(first_kernel, s),
         (dual,) + (plane,) * 5 + (line,) + (plane,) * 2 + (line,) * (2 * pairs_y),
         [duals, sign, cat, adjoint, own, flat(after_x), flat(coefficients), flat(signal),
          mask[0], column] + after_y,
-        [pltpu.VMEM((s.depth, width + LANES), BF16), pltpu.VMEM((dirs, width + LANES), F32)] + splits,
-        "first", 2_000_000_000)
+        [pltpu.VMEM((s.depth, width + LANES), BF16), pltpu.VMEM((dirs, width + LANES), F32)] + back,
+        2_000_000_000)
     received = exchange("gx", sends[:2])
-    received += exchange("gy", sends[2 : 2 + pairs_y]) + diagonal_exchange(sends[2 + pairs_y :])
+    received += exchange("gy", sends[2 : 2 + pairs_y])
+    received += diagonal_exchange(sends[2 + pairs_y :])
     duals, sign, base, coef, from_x, from_y = call(
         functools.partial(second_kernel, s),
         (dual, signs, plane, plane, plane, line),
         [duals, sign, cat, adjoint, base, inverse, coef, target, from_x, from_y, column] + received,
-        [pltpu.VMEM((s.depth, 4 * width), BF16), pltpu.VMEM((dirs, 4 * width), F32)] + splits,
-        "second", 2_000_000_000)
+        [pltpu.VMEM((s.depth, 4 * width), BF16), pltpu.VMEM((dirs, 4 * width), F32)] + back,
+        2_000_000_000)
     below_x = shift(from_x, "gx", 1)
     below_y = exchange("gy", [from_y] * pairs_y)
     grad_out, sign_out = call(
         functools.partial(store_kernel, s),
         (f32(*dual_grad.shape), f32(*dual_sign.shape)), (duals, sign),
-        [pltpu.SemaphoreType.DMA((4 * rows,))], "store", 2_000_000_000, out_specs=[hbm, hbm])
+        [pltpu.SemaphoreType.DMA((4 * rows,))], 2_000_000_000, out_specs=[hbm, hbm])
     coef_out, extra_out = call(
         functools.partial(last_kernel, s),
         (f32(count * rows, lanes), f32(count * rows, lanes)),
-        [base, inverse, coef, below_x] + below_y, [], "last", 1_000_000)
+        [base, inverse, coef, below_x] + below_y, [], 1_000_000)
     return (coef_out.reshape(signal.shape), extra_out.reshape(signal.shape), grad_out, sign_out)
 
 

time: 36.6 us -> 36.3 us (level)
  the two profiles are of different devices: /device:TPU:24 before, /device:TPU:8 now
where the time goes in v4:
time: 36.3 us; the launch traced here: 36.1 us
  starting transfers between devices  14.2 us (39%)
  Pallas kernels  14 us (39%)
  waiting for transfers between devices  6.08 us (17%)
  local copies, waits for them, and re-layouts  0.96 us (3%)
  between operations  0.79 us (2%)
    pallas_call x5, Pallas kernels, call(): pl.pallas_call(kernel, out_shape=outs, in_specs=in_specs or [vmem] * len(...  14 us
    ppermute x5, starting transfers between devices, exchange(): lax.ppermute(send, axis, pairs)  5.51 us
    ppermute x2, starting transfers between devices, shift(): return lax.ppermute(value, axis, pairs)  4.81 us
    ppermute x1, starting transfers between devices, diagonal_exchange(): received.append(lax.ppermute(send, ('gx', 'gy'), flat))  3.91 us
    ppermute x1, waiting for transfers between devices, diagonal_exchange(): received.append(lax.ppermute(send, ('gx', 'gy'), flat))  3 us
    ppermute x2, waiting for transfers between devices, shift(): return lax.ppermute(value, axis, pairs)  2.07 us
    ppermute x5, waiting for transfers between devices, exchange(): lax.ppermute(send, axis, pairs)  1.01 us
    slice x1, local copies, waits for them, and re-layouts, per_device(): after_y = exchange('gy', [extrapolated[:, 0, 0]] * pairs_y)  0.95 us
  transfers between devices with their start and end apart: 8, of which 3 were waited for; matrix products, arithmetic and copies ran while one was open for 3% of the time, Pallas kernels for 16%

profile of v4, /device:TPU:8, one launch (start us, length us, event | category | flops | bytes accessed | tf_op | source)
XLA Modules:
  0.0 36.1 jit_solution(12068472147413207608)
XLA Ops:
  0.6 0.0 copy-start
  0.6 0.0 copy-start.2
  0.7 0.0 copy-start.1
  0.7 2.9 %collective-permute-start = (f32[45,1,8,128]{3,2,1,0:T(8,128)}, f32[45,1,8,128]{3,2,1,0:T(8,128)S(1)}, u32[]{:S(2)}, u32[]{:S(2)}) collective-permute-start(f32[45,1,8,128]{3,2,1,0:T(8,128)} %param.13), channel_id=1, source_target_pairs={{2,0},{4,2},{6,4},{8,6},{10,8},{12,10},{14,12},{16,14},{18,16},{20... | collective-permute-start | bytes 552968 | tf_op jit(solution)/shard_map/ppermute | solution.py:438
  3.6 0.9 %slice.3 = f32[45,1,1,128]{3,2,1,0:T(1,128)S(1)} slice(f32[45,1,8,128]{3,2,1,0:T(8,128)} %param.13), slice={[0:45], [0:1], [0:1], [0:128]} | slice | bytes 46080 | tf_op jit(solution)/shard_map/slice | solution.py:458
  4.5 1.6 %collective-permute-start.1 = (f32[45,128]{1,0:T(8,128)S(1)}, f32[45,128]{1,0:T(8,128)S(1)}, u32[]{:S(2)}, u32[]{:S(2)}) collective-permute-start(f32[45,128]{1,0:T(8,128)S(1)} %bitcast.20), channel_id=1, source_target_pairs={{0,1},{1,0},{2,3},{3,2},{4,5},{5,4},{6,7},{7,6},{8,9},{9,8},{10,11... | collective-permute-start | bytes 69128 | tf_op jit(solution)/shard_map/ppermute | solution.py:418
  6.1 3.2 %shard_map.111 = (f32[9960,128]{1,0:T(8,128)S(1)}, f32[3320,128]{1,0:T(8,128)S(1)}, f32[360,128]{1,0:T(8,128)S(1)}, bf16[368,176]{1,0:T(8,128)(2,1)S(1)}, bf16[9...) custom-call(f32[360,128]{1,0:T(8,128)} %bitcast.21, f32[45,362]{1,0:T(8,128)} %bitcast.24, f32[1,45]{1,0:T(1,128)} %bitcast.25, ...), custom_call_target="tpu_custom_call" | custom-call | flops 2000000000 | bytes 13389116 | tf_op jit(solution)/shard_map/pallas_call | solution.py:397
  9.2 0.0 collective-permute-done.1.refs_0_
  9.3 0.0 collective-permute-done
  9.3 0.0 copy-done
  9.3 0.0 copy-done.2
  9.3 0.0 copy-done.1
  9.3 3.2 %shard_map.112 = (f32[9960,128]{1,0:T(8,128)S(1)}, f32[48,1024]{1,0:T(8,128)S(1)}, f32[48,1024]{1,0:T(8,128)S(1)}, f32[48,1024]{1,0:T(8,128)S(1)}, f32[48,1024]{...) custom-call(f32[9960,128]{1,0:T(8,128)S(1)} %get-tuple-element.31.du, ...), custom_call_target="tpu_custom_call" | custom-call | flops 2000000000 | bytes 14338048 | tf_op jit(solution)/shard_map/pallas_call | solution.py:397
  12.5 0.1 collective-permute-start.2
  12.5 2.6 %collective-permute-start.3 = (f32[48,1024]{1,0:T(8,128)S(1)}, f32[48,1024]{1,0:T(8,128)S(1)}, u32[]{:S(2)}, u32[]{:S(2)}) collective-permute-start(f32[48,1024]{1,0:T(8,128)S(1)} %get-tuple-element.45), channel_id=1, source_target_pairs={{2,4},{4,2},{6,8},{8,6},{10,12},{12,10},{14,16},{16,14},{18,20},{2... | collective-permute-start | bytes 589832 | tf_op jit(solution)/shard_map/ppermute | solution.py:418
  15.1 1.2 %collective-permute-start.4 = (f32[48,128]{1,0:T(8,128)S(1)}, f32[48,128]{1,0:T(8,128)S(1)}, u32[]{:S(2)}, u32[]{:S(2)}) collective-permute-start(f32[48,128]{1,0:T(8,128)S(1)} %get-tuple-element.46), channel_id=1, source_target_pairs={{0,1},{1,0},{2,3},{3,2},{4,5},{5,4},{6,7},{7,6},{8,9},{9,8},{10,11... | collective-permute-start | bytes 73736 | tf_op jit(solution)/shard_map/ppermute | solution.py:418
  16.3 3.9 %collective-permute-start.5 = (f32[48,128]{1,0:T(8,128)S(1)}, f32[48,128]{1,0:T(8,128)S(1)}, u32[]{:S(2)}, u32[]{:S(2)}) collective-permute-start(f32[48,128]{1,0:T(8,128)S(1)} %get-tuple-element.47), channel_id=1, source_target_pairs={{2,1},{1,2},{4,3},{3,4},{6,5},{5,6},{8,7},{7,8},{10,9},{9,10},{12,... | collective-permute-start | bytes 73736 | tf_op jit(solution)/shard_map/ppermute | solution.py:431
  20.2 0.0 collective-permute-done.4.refs_2_
  20.3 3.0 %collective-permute-done.5.refs_3_ = f32[48,128]{1,0:T(8,128)S(1)} collective-permute-done((f32[48,128]{1,0:T(8,128)S(1)}, f32[48,128]{1,0:T(8,128)S(1)}, u32[]{:S(2)}, u32[]{:S(2)}) %collective-permute-start.5) | collective-permute-done | bytes 24608 | tf_op jit(solution)/shard_map/ppermute | solution.py:431
  23.3 0.0 collective-permute-done.2.refs_0_
  23.3 0.0 collective-permute-done.3.refs_1_
  23.3 4.1 %shard_map.113 = (f32[9960,128]{1,0:T(8,128)S(1)}, f32[3320,128]{1,0:T(8,128)S(1)}, f32[48,1024]{1,0:T(8,128)S(1)}, f32[48,1024]{1,0:T(8,128)S(1)}, f32[48,1024]{1,0:T(8,128)S(1)}, /*index=5*/f32[48,128]{1,0:T(8,128)S(1)}) custom-call(f32[9960,128]{1,0:T(8,128)S(1)} %get-tuple-element.37.dual_in, f32[3320,128]{1,0:T(8,128)S(1)} %get-tuple-element.32.sign_in, ...), custom_call_target="tpu_custom_call" | custom-call | flops 2000000000 | bytes 15887872 | tf_op jit(solution)/shard_map/pallas_call | solution.py:397
  27.3 1.9 %collective-permute-start.6 = (f32[48,1024]{1,0:T(8,128)S(1)}, f32[48,1024]{1,0:T(8,128)S(1)}, u32[]{:S(2)}, u32[]{:S(2)}) collective-permute-start(f32[48,1024]{1,0:T(8,128)S(1)} %get-tuple-element.50), channel_id=1, source_target_pairs={{0,2},{2,4},{4,6},{6,8},{8,10},{10,12},{12,14},{14,16},{16,18},{18... | collective-permute-start | bytes 589832 | tf_op jit(solution)/shard_map/ppermute | solution.py:438
  29.3 0.1 collective-permute-start.7
  29.4 2.8 %shard_map.115 = (f32[3,362,1,8,128]{4,3,2,1,0:T(8,128)}, f32[362,1,8,128]{3,2,1,0:T(8,128)}) custom-call(f32[9960,128]{1,0:T(8,128)S(1)} %get-tuple-element.54.dual_ref, f32[3320,128]{1,0:T(8,128)S(1)} %get-tuple-element.55.sign_in), custom_call_target="tpu_custom_call" | custom-call | flops 2000000000 | bytes 12730368 | tf_op jit(solution)/shard_map/pallas_call | solution.py:397
  32.2 1.0 %collective-permute-done.7.refs_0_ = f32[48,128]{1,0:T(8,128)S(1)} collective-permute-done((f32[48,128]{1,0:T(8,128)S(1)}, f32[48,128]{1,0:T(8,128)S(1)}, u32[]{:S(2)}, u32[]{:S(2)}) %collective-permute-start.7) | collective-permute-done | bytes 24608 | tf_op jit(solution)/shard_map/ppermute | solution.py:418
  33.2 2.1 %collective-permute-done.6.x_ref = f32[48,1024]{1,0:T(8,128)S(1)} collective-permute-done((f32[48,1024]{1,0:T(8,128)S(1)}, f32[48,1024]{1,0:T(8,128)S(1)}, u32[]{:S(2)}, u32[]{:S(2)}) %collective-permute-start.6) | collective-permute-done | bytes 196640 | tf_op jit(solution)/shard_map/ppermute | solution.py:438
  35.2 0.8 %shard_map.114 = (f32[360,128]{1,0:T(8,128)}, f32[360,128]{1,0:T(8,128)}) custom-call(f32[48,1024]{1,0:T(8,128)S(1)} %get-tuple-element.48.base_ref, f32[48,1024]{1,0:T(8,128)S(1)} %get-tuple-element.39.inverse_ref, f32[48,1024]{1,0:T(8,128)S(1)} %get-tuple-element.49.coef_ref, f32[48,1024]{1,0:T(8,128)S(1)} %collective-permute-done.6.x_ref, ...), custom_call_target="tpu_custom_call" | custom-call | flops 1000000 | bytes 1179648 | tf_op jit(solution)/shard_map/pallas_call | solution.py:397
  (1 shorter events, 0.0 us)
Async XLA Ops:
  0.6 8.6 %copy-start = (f32[45,1,8,128]{3,2,1,0:T(8,128)S(1)}, f32[45,1,8,128]{3,2,1,0:T(8,128)}, u32[]{:S(2)}) copy-start(f32[45,1,8,128]{3,2,1,0:T(8,128)} %param.12) | copy-start | bytes 552964
  0.6 8.6 %copy-start.2 = (s32[1,8,128]{2,1,0:T(8,128)S(1)}, s32[1,8,128]{2,1,0:T(8,128)}, u32[]{:S(2)}) copy-start(s32[1,8,128]{2,1,0:T(8,128)} %param.11) | copy-start | bytes 12292
  0.7 8.6 %copy-start.1 = (f32[45,1,8,128]{3,2,1,0:T(8,128)S(1)}, f32[45,1,8,128]{3,2,1,0:T(8,128)}, u32[]{:S(2)}) copy-start(f32[45,1,8,128]{3,2,1,0:T(8,128)} %param.8) | copy-start | bytes 552964
  0.7 8.6 %collective-permute-start = (f32[45,1,8,128]{3,2,1,0:T(8,128)}, f32[45,1,8,128]{3,2,1,0:T(8,128)S(1)}, u32[]{:S(2)}, u32[]{:S(2)}) collective-permute-start(f32[45,1,8,128]{3,2,1,0:T(8,128)} %param.13), channel_id=1, source_target_pairs={{2,0},{4,2},{6,4},{8,6},{10,8},{12,10},{14,12},{16,14},{18,16},{20... | collective-permute-start | bytes 552968 | tf_op jit(solution)/shard_map/ppermute | solution.py:438
  4.5 4.7 %collective-permute-start.1 = (f32[45,128]{1,0:T(8,128)S(1)}, f32[45,128]{1,0:T(8,128)S(1)}, u32[]{:S(2)}, u32[]{:S(2)}) collective-permute-start(f32[45,128]{1,0:T(8,128)S(1)} %bitcast.20), channel_id=1, source_target_pairs={{0,1},{1,0},{2,3},{3,2},{4,5},{5,4},{6,7},{7,6},{8,9},{9,8},{10,11... | collective-permute-start | bytes 69128 | tf_op jit(solution)/shard_map/ppermute | solution.py:418
  12.5 10.8 %collective-permute-start.2 = (f32[48,1024]{1,0:T(8,128)S(1)}, f32[48,1024]{1,0:T(8,128)S(1)}, u32[]{:S(2)}, u32[]{:S(2)}) collective-permute-start(f32[48,1024]{1,0:T(8,128)S(1)} %get-tuple-element.44), channel_id=1, source_target_pairs={{0,2},{2,0},{4,6},{6,4},{8,10},{10,8},{12,14},{14,12},{16,18},{18,... | collective-permute-start | bytes 589832 | tf_op jit(solution)/shard_map/ppermute | solution.py:418
  12.5 10.7 %collective-permute-start.3 = (f32[48,1024]{1,0:T(8,128)S(1)}, f32[48,1024]{1,0:T(8,128)S(1)}, u32[]{:S(2)}, u32[]{:S(2)}) collective-permute-start(f32[48,1024]{1,0:T(8,128)S(1)} %get-tuple-element.45), channel_id=1, source_target_pairs={{2,4},{4,2},{6,8},{8,6},{10,12},{12,10},{14,16},{16,14},{18,20},{2... | collective-permute-start | bytes 589832 | tf_op jit(solution)/shard_map/ppermute | solution.py:418
  15.1 5.1 %collective-permute-start.4 = (f32[48,128]{1,0:T(8,128)S(1)}, f32[48,128]{1,0:T(8,128)S(1)}, u32[]{:S(2)}, u32[]{:S(2)}) collective-permute-start(f32[48,128]{1,0:T(8,128)S(1)} %get-tuple-element.46), channel_id=1, source_target_pairs={{0,1},{1,0},{2,3},{3,2},{4,5},{5,4},{6,7},{7,6},{8,9},{9,8},{10,11... | collective-permute-start | bytes 73736 | tf_op jit(solution)/shard_map/ppermute | solution.py:418
  16.3 6.9 %collective-permute-start.5 = (f32[48,128]{1,0:T(8,128)S(1)}, f32[48,128]{1,0:T(8,128)S(1)}, u32[]{:S(2)}, u32[]{:S(2)}) collective-permute-start(f32[48,128]{1,0:T(8,128)S(1)} %get-tuple-element.47), channel_id=1, source_target_pairs={{2,1},{1,2},{4,3},{3,4},{6,5},{5,6},{8,7},{7,8},{10,9},{9,10},{12,... | collective-permute-start | bytes 73736 | tf_op jit(solution)/shard_map/ppermute | solution.py:431
  27.3 7.9 %collective-permute-start.6 = (f32[48,1024]{1,0:T(8,128)S(1)}, f32[48,1024]{1,0:T(8,128)S(1)}, u32[]{:S(2)}, u32[]{:S(2)}) collective-permute-start(f32[48,1024]{1,0:T(8,128)S(1)} %get-tuple-element.50), channel_id=1, source_target_pairs={{0,2},{2,4},{4,6},{6,8},{8,10},{10,12},{12,14},{14,16},{16,18},{18... | collective-permute-start | bytes 589832 | tf_op jit(solution)/shard_map/ppermute | solution.py:438
  29.3 3.9 %collective-permute-start.7 = (f32[48,128]{1,0:T(8,128)S(1)}, f32[48,128]{1,0:T(8,128)S(1)}, u32[]{:S(2)}, u32[]{:S(2)}) collective-permute-start(f32[48,128]{1,0:T(8,128)S(1)} %get-tuple-element.51), channel_id=1, source_target_pairs={{0,1},{1,0},{2,3},{3,2},{4,5},{5,4},{6,7},{7,6},{8,9},{9,8},{10,11... | collective-permute-start | bytes 73736 | tf_op jit(solution)/shard_map/ppermute | solution.py:418

commit v5 on v4

--- a/solution.py
+++ b/solution.py
@@ -105,6 +105,8 @@
         return part * self.part_rows + (row + 1) * self.padded_dirs
 
     def at(self, part, row, index):
+        if isinstance(row, int):
+            return slice(self.start(part, row) + index * GROUP, self.start(part, row) + (index + 1) * GROUP)
         return pl.ds(pl.multiple_of(self.start(part, row) + index * GROUP, 8), GROUP)
 
     def lanes(self, row):
@@ -186,66 +188,69 @@
         copy_of(0, row).wait()
 
 
-def dual_pass(s, dual_in, sign_in, dual_out, sign_out, change, back_ref):
-    edge = lane_edge()
+def dual_and_adjoints(s, dual_in, sign_in, dual_out, sign_out, cat_ref, e_cat, change, back_ref,
+                      adjoint_ref, keep_x, keep_y):
     full = sign_out is not None
     signs = sign_out if full else sign_in
-    dual_out[s.start(1, -1) : s.start(1, 0), :] = jnp.zeros((s.padded_dirs, LANES), F32)
-
-    def part_lanes(part, row):
-        return pl.ds(pl.multiple_of(part * s.width + row * LANES, LANES), LANES)
+    edge = lane_edge()
+    last_row = s.rows - 1
+    pairs = [range(row, min(row + 2, s.rows)) for row in range(0, s.rows, 2)]
+
+    def lanes_of(part, row, count=1):
+        return slice(part * s.width + row * LANES, part * s.width + (row + count) * LANES)
+
+    def differences(rows):
+        parts = [lanes_of(part, rows[0], len(rows)) for part in (range(4) if full else range(1))]
+        if not full and last_row in rows:
+            parts.append(lanes_of(1, 0))
+        for at in parts:
+            change[:, at] = matmul(cat_ref[...], e_cat[:, at])
 
     def shrink_row(row):
         for index in range(s.groups):
             here = slice(index * GROUP, (index + 1) * GROUP)
-            step_x = dual_in[s.at(0, row, index), :] + change[here, part_lanes(0, row)]
+            step_x = dual_in[s.at(0, row, index), :] + change[here, lanes_of(0, row)]
             step_y, step_z = dual_in[s.at(1, row, index), :], dual_in[s.at(2, row, index), :]
             if full:
-                step_y = step_y + change[here, part_lanes(1, row)]
-                step_z = step_z + change[here, part_lanes(2, row)]
+                step_y = step_y + change[here, lanes_of(1, row)]
+                step_z = step_z + change[here, lanes_of(2, row)]
                 sign_out[s.at(0, row, index), :] = jnp.minimum(
-                    0.0, sign_in[s.at(0, row, index), :] + change[here, part_lanes(3, row)])
-            elif isinstance(row, int):
-                step_y = step_y + change[here, part_lanes(1, 0)]
+                    0.0, sign_in[s.at(0, row, index), :] + change[here, lanes_of(3, row)])
+            elif row == last_row:
+                step_y = step_y + change[here, lanes_of(1, 0)]
             new_x, new_y, new_z = shrunk(step_x, step_y, step_z)
             dual_out[s.at(0, row, index), :] = new_x
             dual_out[s.at(1, row, index), :] = new_y
             dual_out[s.at(2, row, index), :] = new_z
 
-    def split_row(row, carry):
+    def back_row(row):
         for index in range(s.groups):
             here = slice(index * GROUP, (index + 1) * GROUP)
             inner_z = dual_out[s.at(2, row, index), :] * edge
             back = signs[s.at(0, row, index), :] - (inner_z - previous_lane(inner_z))
-            back = back - (dual_out[s.at(1, row, index), :] - dual_out[s.at(1, row - 1, index), :])
-            back_ref[here, s.lanes(row)] = back
-        return carry
-
-    def step(row, carry):
-        shrink_row(row)
-        return carry
-
-    if full:
-        lax.fori_loop(0, s.rows, step, 0)
-    else:
-        lax.fori_loop(0, s.rows - 1, step, 0)
-        shrink_row(s.rows - 1)
-    lax.fori_loop(0, s.rows, split_row, 0)
-
-
-def all_adjoints(s, adjoint_ref, back_ref, dual_ref, keep_x, keep_y):
+            back = back - dual_out[s.at(1, row, index), :]
+            if row:
+                back = back + dual_out[s.at(1, row - 1, index), :]
+            back_ref[here, lanes_of(0, row)] = back
+
     def plane(part, row):
-        return dual_ref[pl.ds(s.start(part, row), s.padded_dirs), :]
+        return dual_out[s.start(part, row) : s.start(part, row) + s.padded_dirs, :]
 
     from_back, from_x = [], []
-    for row in range(0, s.rows, 2):
-        rows = range(row, min(row + 2, s.rows))
-        value = back_ref[:, row * LANES : (row + len(rows)) * LANES]
-        from_back.append(harmonics(adjoint_ref, value, s.padded))
-        value = jnp.concatenate([plane(0, each) for each in rows], 1)
-        from_x.append(harmonics(adjoint_ref, value, s.padded))
+    differences(pairs[0])
+    for number, rows in enumerate(pairs):
+        if number + 1 < len(pairs):
+            differences(pairs[number + 1])
+        for row in rows:
+            shrink_row(row)
+        for row in rows:
+            back_row(row)
+        from_x.append(harmonics(
+            adjoint_ref, jnp.concatenate([plane(0, row) for row in rows], 1), s.padded))
+        from_back.append(harmonics(
+            adjoint_ref, back_ref[:, lanes_of(0, rows[0], len(rows))], s.padded))
     from_back, from_x = jnp.concatenate(from_back, 1), jnp.concatenate(from_x, 1)
-    from_y = harmonics(adjoint_ref, plane(1, s.rows - 1), s.padded)
+    from_y = harmonics(adjoint_ref, plane(1, last_row), s.padded)
     last = from_back[:, s.width - LANES :] + (1.0 - keep_y) * from_y
     total = jnp.concatenate([from_back[:, : s.width - LANES], last], 1) - keep_x * from_x
     return total, from_x, from_y
@@ -292,9 +297,9 @@
     put_cat(e_cat, jnp.concatenate(
         [(there - here) * (STEP_DUAL * keep_x),
          (edge_row - here[:, s.width - LANES :]) * (STEP_DUAL * keep_y)], 1), s.low_row)
-    wide_matmul(cat_ref, e_cat, diff, s.width + LANES)
-    dual_pass(s, dual_in, sign_in, dual_ref, None, diff, back_ref)
-    total, from_x, from_y = all_adjoints(s, adjoint_ref, back_ref, dual_ref, keep_x, keep_y)
+    total, from_x, from_y = dual_and_adjoints(
+        s, dual_in, sign_in, dual_ref, None, cat_ref, e_cat, diff, back_ref, adjoint_ref,
+        keep_x, keep_y)
     mask, response = weights(s, mask_ref, response_ref)
     weight = mask * response
     coef = planes_of(coef_ref, s.count, s.rows, s.padded)
@@ -353,9 +358,9 @@
     along_z = jnp.concatenate([(next_lane(plane) - plane) * edge for plane in planes], 1)
     put_cat(e_cat, STEP_DUAL * jnp.concatenate(
         [(there - here) * keep_x, along_y, along_z, here], 1), s.low_row)
-    wide_matmul(cat_ref, e_cat, change, 4 * s.width)
-    dual_pass(s, dual_in, sign_in, dual_ref, sign_ref, change, back_ref)
-    total, from_x, from_y = all_adjoints(s, adjoint_ref, back_ref, dual_ref, keep_x, keep_y)
+    total, from_x, from_y = dual_and_adjoints(
+        s, dual_in, sign_in, dual_ref, sign_ref, cat_ref, e_cat, change, back_ref, adjoint_ref,
+        keep_x, keep_y)
     base_out[...] = updated + target_ref[...] - STEP_PRIMAL * total
     coef_out[...] = updated
     x_out[...] = from_x

time: 36.3 us -> 33.8 us (0.931)
  the two profiles are of different devices: /device:TPU:8 before, /device:TPU:24 now
where the time goes in v5:
time: 33.8 us; the launch traced here: 33.6 us
  starting transfers between devices  14.2 us (42%)
  Pallas kernels  11.6 us (34%)
  waiting for transfers between devices  6.07 us (18%)
  local copies, waits for them, and re-layouts  0.96 us (3%)
  between operations  0.78 us (2%)
    pallas_call x5, Pallas kernels, call(): pl.pallas_call(kernel, out_shape=outs, in_specs=in_specs or [vmem] * len(...  11.6 us
    ppermute x5, starting transfers between devices, exchange(): lax.ppermute(send, axis, pairs)  5.52 us
    ppermute x2, starting transfers between devices, shift(): return lax.ppermute(value, axis, pairs)  4.81 us
    ppermute x1, starting transfers between devices, diagonal_exchange(): received.append(lax.ppermute(send, ('gx', 'gy'), flat))  3.91 us
    ppermute x1, waiting for transfers between devices, diagonal_exchange(): received.append(lax.ppermute(send, ('gx', 'gy'), flat))  3 us
    ppermute x2, waiting for transfers between devices, shift(): return lax.ppermute(value, axis, pairs)  2.07 us
    ppermute x5, waiting for transfers between devices, exchange(): lax.ppermute(send, axis, pairs)  1 us
    slice x1, local copies, waits for them, and re-layouts, per_device(): after_y = exchange('gy', [extrapolated[:, 0, 0]] * pairs_y)  0.95 us
  transfers between devices with their start and end apart: 8, of which 3 were waited for; matrix products, arithmetic and copies ran while one was open for 3% of the time, Pallas kernels for 18%

profile of v5, /device:TPU:24, one launch (start us, length us, event | category | flops | bytes accessed | tf_op | source)
XLA Modules:
  0.0 33.6 jit_solution(8837918605754572539)
XLA Ops:
  0.6 0.0 copy-start
  0.6 0.0 copy-start.2
  0.7 0.0 copy-start.1
  0.7 2.9 %collective-permute-start = (f32[45,1,8,128]{3,2,1,0:T(8,128)}, f32[45,1,8,128]{3,2,1,0:T(8,128)S(1)}, u32[]{:S(2)}, u32[]{:S(2)}) collective-permute-start(f32[45,1,8,128]{3,2,1,0:T(8,128)} %param.13), channel_id=1, source_target_pairs={{2,0},{4,2},{6,4},{8,6},{10,8},{12,10},{14,12},{16,14},{18,16},{20... | collective-permute-start | bytes 552968 | tf_op jit(solution)/shard_map/ppermute | solution.py:443
  3.6 0.9 %slice.3 = f32[45,1,1,128]{3,2,1,0:T(1,128)S(1)} slice(f32[45,1,8,128]{3,2,1,0:T(8,128)} %param.13), slice={[0:45], [0:1], [0:1], [0:128]} | slice | bytes 46080 | tf_op jit(solution)/shard_map/slice | solution.py:463
  4.5 1.6 %collective-permute-start.1 = (f32[45,128]{1,0:T(8,128)S(1)}, f32[45,128]{1,0:T(8,128)S(1)}, u32[]{:S(2)}, u32[]{:S(2)}) collective-permute-start(f32[45,128]{1,0:T(8,128)S(1)} %bitcast.20), channel_id=1, source_target_pairs={{0,1},{1,0},{2,3},{3,2},{4,5},{5,4},{6,7},{7,6},{8,9},{9,8},{10,11... | collective-permute-start | bytes 69128 | tf_op jit(solution)/shard_map/ppermute | solution.py:423
  6.1 3.2 %shard_map.111 = (f32[9960,128]{1,0:T(8,128)S(1)}, f32[3320,128]{1,0:T(8,128)S(1)}, f32[360,128]{1,0:T(8,128)S(1)}, bf16[368,176]{1,0:T(8,128)(2,1)S(1)}, bf16[9...) custom-call(f32[360,128]{1,0:T(8,128)} %bitcast.21, f32[45,362]{1,0:T(8,128)} %bitcast.24, f32[1,45]{1,0:T(1,128)} %bitcast.25, ...), custom_call_target="tpu_custom_call" | custom-call | flops 2000000000 | bytes 13389116 | tf_op jit(solution)/shard_map/pallas_call | solution.py:402
  9.2 0.0 collective-permute-done.1.refs_0_
  9.3 0.0 collective-permute-done
  9.3 0.0 copy-done
  9.3 0.0 copy-done.2
  9.3 0.0 copy-done.1
  9.3 2.1 %shard_map.112 = (f32[9960,128]{1,0:T(8,128)S(1)}, f32[48,1024]{1,0:T(8,128)S(1)}, f32[48,1024]{1,0:T(8,128)S(1)}, f32[48,1024]{1,0:T(8,128)S(1)}, f32[48,1024]{...) custom-call(f32[9960,128]{1,0:T(8,128)S(1)} %get-tuple-element.31.du, ...), custom_call_target="tpu_custom_call" | custom-call | flops 2000000000 | bytes 14338048 | tf_op jit(solution)/shard_map/pallas_call | solution.py:402
  11.4 0.1 collective-permute-start.2
  11.5 2.6 %collective-permute-start.3 = (f32[48,1024]{1,0:T(8,128)S(1)}, f32[48,1024]{1,0:T(8,128)S(1)}, u32[]{:S(2)}, u32[]{:S(2)}) collective-permute-start(f32[48,1024]{1,0:T(8,128)S(1)} %get-tuple-element.45), channel_id=1, source_target_pairs={{2,4},{4,2},{6,8},{8,6},{10,12},{12,10},{14,16},{16,14},{18,20},{2... | collective-permute-start | bytes 589832 | tf_op jit(solution)/shard_map/ppermute | solution.py:423
  14.0 1.2 %collective-permute-start.4 = (f32[48,128]{1,0:T(8,128)S(1)}, f32[48,128]{1,0:T(8,128)S(1)}, u32[]{:S(2)}, u32[]{:S(2)}) collective-permute-start(f32[48,128]{1,0:T(8,128)S(1)} %get-tuple-element.46), channel_id=1, source_target_pairs={{0,1},{1,0},{2,3},{3,2},{4,5},{5,4},{6,7},{7,6},{8,9},{9,8},{10,11... | collective-permute-start | bytes 73736 | tf_op jit(solution)/shard_map/ppermute | solution.py:423
  15.2 3.9 %collective-permute-start.5 = (f32[48,128]{1,0:T(8,128)S(1)}, f32[48,128]{1,0:T(8,128)S(1)}, u32[]{:S(2)}, u32[]{:S(2)}) collective-permute-start(f32[48,128]{1,0:T(8,128)S(1)} %get-tuple-element.47), channel_id=1, source_target_pairs={{2,1},{1,2},{4,3},{3,4},{6,5},{5,6},{8,7},{7,8},{10,9},{9,10},{12,... | collective-permute-start | bytes 73736 | tf_op jit(solution)/shard_map/ppermute | solution.py:436
  19.2 0.0 collective-permute-done.4.refs_2_
  19.2 3.0 %collective-permute-done.5.refs_3_ = f32[48,128]{1,0:T(8,128)S(1)} collective-permute-done((f32[48,128]{1,0:T(8,128)S(1)}, f32[48,128]{1,0:T(8,128)S(1)}, u32[]{:S(2)}, u32[]{:S(2)}) %collective-permute-start.5) | collective-permute-done | bytes 24608 | tf_op jit(solution)/shard_map/ppermute | solution.py:436
  22.2 0.0 collective-permute-done.2.refs_0_
  22.2 0.0 collective-permute-done.3.refs_1_
  22.2 2.7 %shard_map.113 = (f32[9960,128]{1,0:T(8,128)S(1)}, f32[3320,128]{1,0:T(8,128)S(1)}, f32[48,1024]{1,0:T(8,128)S(1)}, f32[48,1024]{1,0:T(8,128)S(1)}, f32[48,1024]{1,0:T(8,128)S(1)}, /*index=5*/f32[48,128]{1,0:T(8,128)S(1)}) custom-call(f32[9960,128]{1,0:T(8,128)S(1)} %get-tuple-element.37.dual_in, f32[3320,128]{1,0:T(8,128)S(1)} %get-tuple-element.32.sign_in, ...), custom_call_target="tpu_custom_call" | custom-call | flops 2000000000 | bytes 15887872 | tf_op jit(solution)/shard_map/pallas_call | solution.py:402
  24.9 1.9 %collective-permute-start.6 = (f32[48,1024]{1,0:T(8,128)S(1)}, f32[48,1024]{1,0:T(8,128)S(1)}, u32[]{:S(2)}, u32[]{:S(2)}) collective-permute-start(f32[48,1024]{1,0:T(8,128)S(1)} %get-tuple-element.50), channel_id=1, source_target_pairs={{0,2},{2,4},{4,6},{6,8},{8,10},{10,12},{12,14},{14,16},{16,18},{18... | collective-permute-start | bytes 589832 | tf_op jit(solution)/shard_map/ppermute | solution.py:443
  26.8 0.1 collective-permute-start.7
  26.9 2.8 %shard_map.115 = (f32[3,362,1,8,128]{4,3,2,1,0:T(8,128)}, f32[362,1,8,128]{3,2,1,0:T(8,128)}) custom-call(f32[9960,128]{1,0:T(8,128)S(1)} %get-tuple-element.54.dual_ref, f32[3320,128]{1,0:T(8,128)S(1)} %get-tuple-element.55.sign_in), custom_call_target="tpu_custom_call" | custom-call | flops 2000000000 | bytes 12730368 | tf_op jit(solution)/shard_map/pallas_call | solution.py:402
  29.7 1.0 %collective-permute-done.7.refs_0_ = f32[48,128]{1,0:T(8,128)S(1)} collective-permute-done((f32[48,128]{1,0:T(8,128)S(1)}, f32[48,128]{1,0:T(8,128)S(1)}, u32[]{:S(2)}, u32[]{:S(2)}) %collective-permute-start.7) | collective-permute-done | bytes 24608 | tf_op jit(solution)/shard_map/ppermute | solution.py:423
  30.7 2.1 %collective-permute-done.6.x_ref = f32[48,1024]{1,0:T(8,128)S(1)} collective-permute-done((f32[48,1024]{1,0:T(8,128)S(1)}, f32[48,1024]{1,0:T(8,128)S(1)}, u32[]{:S(2)}, u32[]{:S(2)}) %collective-permute-start.6) | collective-permute-done | bytes 196640 | tf_op jit(solution)/shard_map/ppermute | solution.py:443
  32.8 0.8 %shard_map.114 = (f32[360,128]{1,0:T(8,128)}, f32[360,128]{1,0:T(8,128)}) custom-call(f32[48,1024]{1,0:T(8,128)S(1)} %get-tuple-element.48.base_ref, f32[48,1024]{1,0:T(8,128)S(1)} %get-tuple-element.39.inverse_ref, f32[48,1024]{1,0:T(8,128)S(1)} %get-tuple-element.49.coef_ref, f32[48,1024]{1,0:T(8,128)S(1)} %collective-permute-done.6.x_ref, ...), custom_call_target="tpu_custom_call" | custom-call | flops 1000000 | bytes 1179648 | tf_op jit(solution)/shard_map/pallas_call | solution.py:402
  (1 shorter events, 0.0 us)
Async XLA Ops:
  0.6 8.6 %copy-start = (f32[45,1,8,128]{3,2,1,0:T(8,128)S(1)}, f32[45,1,8,128]{3,2,1,0:T(8,128)}, u32[]{:S(2)}) copy-start(f32[45,1,8,128]{3,2,1,0:T(8,128)} %param.12) | copy-start | bytes 552964
  0.6 8.6 %copy-start.2 = (s32[1,8,128]{2,1,0:T(8,128)S(1)}, s32[1,8,128]{2,1,0:T(8,128)}, u32[]{:S(2)}) copy-start(s32[1,8,128]{2,1,0:T(8,128)} %param.11) | copy-start | bytes 12292
  0.7 8.6 %copy-start.1 = (f32[45,1,8,128]{3,2,1,0:T(8,128)S(1)}, f32[45,1,8,128]{3,2,1,0:T(8,128)}, u32[]{:S(2)}) copy-start(f32[45,1,8,128]{3,2,1,0:T(8,128)} %param.8) | copy-start | bytes 552964
  0.7 8.6 %collective-permute-start = (f32[45,1,8,128]{3,2,1,0:T(8,128)}, f32[45,1,8,128]{3,2,1,0:T(8,128)S(1)}, u32[]{:S(2)}, u32[]{:S(2)}) collective-permute-start(f32[45,1,8,128]{3,2,1,0:T(8,128)} %param.13), channel_id=1, source_target_pairs={{2,0},{4,2},{6,4},{8,6},{10,8},{12,10},{14,12},{16,14},{18,16},{20... | collective-permute-start | bytes 552968 | tf_op jit(solution)/shard_map/ppermute | solution.py:443
  4.5 4.7 %collective-permute-start.1 = (f32[45,128]{1,0:T(8,128)S(1)}, f32[45,128]{1,0:T(8,128)S(1)}, u32[]{:S(2)}, u32[]{:S(2)}) collective-permute-start(f32[45,128]{1,0:T(8,128)S(1)} %bitcast.20), channel_id=1, source_target_pairs={{0,1},{1,0},{2,3},{3,2},{4,5},{5,4},{6,7},{7,6},{8,9},{9,8},{10,11... | collective-permute-start | bytes 69128 | tf_op jit(solution)/shard_map/ppermute | solution.py:423
  11.4 10.8 %collective-permute-start.2 = (f32[48,1024]{1,0:T(8,128)S(1)}, f32[48,1024]{1,0:T(8,128)S(1)}, u32[]{:S(2)}, u32[]{:S(2)}) collective-permute-start(f32[48,1024]{1,0:T(8,128)S(1)} %get-tuple-element.44), channel_id=1, source_target_pairs={{0,2},{2,0},{4,6},{6,4},{8,10},{10,8},{12,14},{14,12},{16,18},{18,... | collective-permute-start | bytes 589832 | tf_op jit(solution)/shard_map/ppermute | solution.py:423
  11.5 10.7 %collective-permute-start.3 = (f32[48,1024]{1,0:T(8,128)S(1)}, f32[48,1024]{1,0:T(8,128)S(1)}, u32[]{:S(2)}, u32[]{:S(2)}) collective-permute-start(f32[48,1024]{1,0:T(8,128)S(1)} %get-tuple-element.45), channel_id=1, source_target_pairs={{2,4},{4,2},{6,8},{8,6},{10,12},{12,10},{14,16},{16,14},{18,20},{2... | collective-permute-start | bytes 589832 | tf_op jit(solution)/shard_map/ppermute | solution.py:423
  14.0 5.1 %collective-permute-start.4 = (f32[48,128]{1,0:T(8,128)S(1)}, f32[48,128]{1,0:T(8,128)S(1)}, u32[]{:S(2)}, u32[]{:S(2)}) collective-permute-start(f32[48,128]{1,0:T(8,128)S(1)} %get-tuple-element.46), channel_id=1, source_target_pairs={{0,1},{1,0},{2,3},{3,2},{4,5},{5,4},{6,7},{7,6},{8,9},{9,8},{10,11... | collective-permute-start | bytes 73736 | tf_op jit(solution)/shard_map/ppermute | solution.py:423
  15.2 6.9 %collective-permute-start.5 = (f32[48,128]{1,0:T(8,128)S(1)}, f32[48,128]{1,0:T(8,128)S(1)}, u32[]{:S(2)}, u32[]{:S(2)}) collective-permute-start(f32[48,128]{1,0:T(8,128)S(1)} %get-tuple-element.47), channel_id=1, source_target_pairs={{2,1},{1,2},{4,3},{3,4},{6,5},{5,6},{8,7},{7,8},{10,9},{9,10},{12,... | collective-permute-start | bytes 73736 | tf_op jit(solution)/shard_map/ppermute | solution.py:436
  24.9 7.9 %collective-permute-start.6 = (f32[48,1024]{1,0:T(8,128)S(1)}, f32[48,1024]{1,0:T(8,128)S(1)}, u32[]{:S(2)}, u32[]{:S(2)}) collective-permute-start(f32[48,1024]{1,0:T(8,128)S(1)} %get-tuple-element.50), channel_id=1, source_target_pairs={{0,2},{2,4},{4,6},{6,8},{8,10},{10,12},{12,14},{14,16},{16,18},{18... | collective-permute-start | bytes 589832 | tf_op jit(solution)/shard_map/ppermute | solution.py:443
  26.8 3.9 %collective-permute-start.7 = (f32[48,128]{1,0:T(8,128)S(1)}, f32[48,128]{1,0:T(8,128)S(1)}, u32[]{:S(2)}, u32[]{:S(2)}) collective-permute-start(f32[48,128]{1,0:T(8,128)S(1)} %get-tuple-element.51), channel_id=1, source_target_pairs={{0,1},{1,0},{2,3},{3,2},{4,5},{5,4},{6,7},{7,6},{8,9},{9,8},{10,11... | collective-permute-start | bytes 73736 | tf_op jit(solution)/shard_map/ppermute | solution.py:423

commit v6 on v5

--- a/solution.py
+++ b/solution.py
@@ -188,13 +188,38 @@
         copy_of(0, row).wait()
 
 
+def row_pairs(s):
+    return [range(row, min(row + 2, s.rows)) for row in range(0, s.rows, 2)]
+
+
+def back_rows(s, rows, signs, dual_ref, back_ref):
+    edge = lane_edge()
+    for row in rows:
+        for index in range(s.groups):
+            here = slice(index * GROUP, (index + 1) * GROUP)
+            inner_z = dual_ref[s.at(2, row, index), :] * edge
+            back = signs[s.at(0, row, index), :] - (inner_z - previous_lane(inner_z))
+            back = back - dual_ref[s.at(1, row, index), :]
+            if row:
+                back = back + dual_ref[s.at(1, row - 1, index), :]
+            back_ref[here, row * LANES : (row + 1) * LANES] = back
+
+
+def back_harmonics(s, rows, adjoint_ref, back_ref):
+    at = slice(rows[0] * LANES, (rows[-1] + 1) * LANES)
+    return harmonics(adjoint_ref, back_ref[:, at], s.padded)
+
+
+def whole_adjoint(s, from_back, from_x, from_y, keep_x, keep_y):
+    last = from_back[:, s.width - LANES :] + (1.0 - keep_y) * from_y
+    return jnp.concatenate([from_back[:, : s.width - LANES], last], 1) - keep_x * from_x
+
+
 def dual_and_adjoints(s, dual_in, sign_in, dual_out, sign_out, cat_ref, e_cat, change, back_ref,
-                      adjoint_ref, keep_x, keep_y):
+                      adjoint_ref):
     full = sign_out is not None
-    signs = sign_out if full else sign_in
-    edge = lane_edge()
     last_row = s.rows - 1
-    pairs = [range(row, min(row + 2, s.rows)) for row in range(0, s.rows, 2)]
+    pairs = row_pairs(s)
 
     def lanes_of(part, row, count=1):
         return slice(part * s.width + row * LANES, part * s.width + (row + count) * LANES)
@@ -223,16 +248,6 @@
             dual_out[s.at(1, row, index), :] = new_y
             dual_out[s.at(2, row, index), :] = new_z
 
-    def back_row(row):
-        for index in range(s.groups):
-            here = slice(index * GROUP, (index + 1) * GROUP)
-            inner_z = dual_out[s.at(2, row, index), :] * edge
-            back = signs[s.at(0, row, index), :] - (inner_z - previous_lane(inner_z))
-            back = back - dual_out[s.at(1, row, index), :]
-            if row:
-                back = back + dual_out[s.at(1, row - 1, index), :]
-            back_ref[here, lanes_of(0, row)] = back
-
     def plane(part, row):
         return dual_out[s.start(part, row) : s.start(part, row) + s.padded_dirs, :]
 
@@ -243,17 +258,15 @@
             differences(pairs[number + 1])
         for row in rows:
             shrink_row(row)
-        for row in rows:
-            back_row(row)
+        if not full:
+            back_rows(s, rows, sign_in, dual_out, back_ref)
         from_x.append(harmonics(
             adjoint_ref, jnp.concatenate([plane(0, row) for row in rows], 1), s.padded))
-        from_back.append(harmonics(
-            adjoint_ref, back_ref[:, lanes_of(0, rows[0], len(rows))], s.padded))
-    from_back, from_x = jnp.concatenate(from_back, 1), jnp.concatenate(from_x, 1)
+        if not full:
+            from_back.append(back_harmonics(s, rows, adjoint_ref, back_ref))
     from_y = harmonics(adjoint_ref, plane(1, last_row), s.padded)
-    last = from_back[:, s.width - LANES :] + (1.0 - keep_y) * from_y
-    total = jnp.concatenate([from_back[:, : s.width - LANES], last], 1) - keep_x * from_x
-    return total, from_x, from_y
+    from_back = None if full else jnp.concatenate(from_back, 1)
+    return from_back, jnp.concatenate(from_x, 1), from_y
 
 
 def weights(s, mask_ref, response_ref):
@@ -297,9 +310,9 @@
     put_cat(e_cat, jnp.concatenate(
         [(there - here) * (STEP_DUAL * keep_x),
          (edge_row - here[:, s.width - LANES :]) * (STEP_DUAL * keep_y)], 1), s.low_row)
-    total, from_x, from_y = dual_and_adjoints(
-        s, dual_in, sign_in, dual_ref, None, cat_ref, e_cat, diff, back_ref, adjoint_ref,
-        keep_x, keep_y)
+    from_back, from_x, from_y = dual_and_adjoints(
+        s, dual_in, sign_in, dual_ref, None, cat_ref, e_cat, diff, back_ref, adjoint_ref)
+    total = whole_adjoint(s, from_back, from_x, from_y, keep_x, keep_y)
     mask, response = weights(s, mask_ref, response_ref)
     weight = mask * response
     coef = planes_of(coef_ref, s.count, s.rows, s.padded)
@@ -333,10 +346,9 @@
     return jnp.where(row_index < s.count, message - (2.0 * STEP_PRIMAL) * inverse * own, 0.0)
 
 
-def second_kernel(s, dual_in, sign_in, cat_ref, adjoint_ref, base_ref, inverse_ref, coef_ref, target_ref,
+def second_kernel(s, dual_in, sign_in, cat_ref, adjoint_ref, base_ref, inverse_ref, coef_ref,
                   x_ref, y_ref, response_ref, *refs):
-    *received, dual_ref, sign_ref, base_out, coef_out, x_out, y_out = refs[:-3]
-    e_cat, change, back_ref = refs[-3:]
+    *received, dual_ref, sign_ref, coef_out, x_out, y_out, e_cat, change = refs
     pairs_y = (len(received) - 2) // 2
     keep_x, keep_y = last_flags()
     below, above = received_at("gx", received[:2])
@@ -358,16 +370,15 @@
     along_z = jnp.concatenate([(next_lane(plane) - plane) * edge for plane in planes], 1)
     put_cat(e_cat, STEP_DUAL * jnp.concatenate(
         [(there - here) * keep_x, along_y, along_z, here], 1), s.low_row)
-    total, from_x, from_y = dual_and_adjoints(
-        s, dual_in, sign_in, dual_ref, sign_ref, cat_ref, e_cat, change, back_ref, adjoint_ref,
-        keep_x, keep_y)
-    base_out[...] = updated + target_ref[...] - STEP_PRIMAL * total
+    _, from_x, from_y = dual_and_adjoints(
+        s, dual_in, sign_in, dual_ref, sign_ref, cat_ref, e_cat, change, None, adjoint_ref)
     coef_out[...] = updated
     x_out[...] = from_x
     y_out[...] = from_y
 
 
-def store_kernel(s, dual_ref, sign_in, grad_ref, sign_ref, sems):
+def close_kernel(s, dual_ref, sign_in, adjoint_ref, coef_ref, target_ref, x_ref, y_ref,
+                 base_ref, grad_ref, sign_ref, back_ref, sems):
     copies = []
     for row in range(s.rows):
         for part in range(3):
@@ -379,6 +390,14 @@
             sems.at[3 * s.rows + row]))
     for copy in copies:
         copy.start()
+    keep_x, keep_y = last_flags()
+    from_back = []
+    for rows in row_pairs(s):
+        back_rows(s, rows, sign_in, dual_ref, back_ref)
+        from_back.append(back_harmonics(s, rows, adjoint_ref, back_ref))
+    total = whole_adjoint(
+        s, jnp.concatenate(from_back, 1), x_ref[...], y_ref[...], keep_x, keep_y)
+    base_ref[...] = coef_ref[...] + target_ref[...] - STEP_PRIMAL * total
     for copy in copies:
         copy.wait()
 
@@ -482,18 +501,20 @@
     received = exchange("gx", sends[:2])
     received += exchange("gy", sends[2 : 2 + pairs_y])
     received += diagonal_exchange(sends[2 + pairs_y :])
-    duals, sign, base, coef, from_x, from_y = call(
+    duals, sign, coef, from_x, from_y = call(
         functools.partial(second_kernel, s),
-        (dual, signs, plane, plane, plane, line),
-        [duals, sign, cat, adjoint, base, inverse, coef, target, from_x, from_y, column] + received,
-        [pltpu.VMEM((s.depth, 4 * width), BF16), pltpu.VMEM((dirs, 4 * width), F32)] + back,
+        (dual, signs, plane, plane, line),
+        [duals, sign, cat, adjoint, base, inverse, coef, from_x, from_y, column] + received,
+        [pltpu.VMEM((s.depth, 4 * width), BF16), pltpu.VMEM((dirs, 4 * width), F32)],
         2_000_000_000)
     below_x = shift(from_x, "gx", 1)
     below_y = exchange("gy", [from_y] * pairs_y)
-    grad_out, sign_out = call(
-        functools.partial(store_kernel, s),
-        (f32(*dual_grad.shape), f32(*dual_sign.shape)), (duals, sign),
-        [pltpu.SemaphoreType.DMA((4 * rows,))], 2_000_000_000, out_specs=[hbm, hbm])
+    base, grad_out, sign_out = call(
+        functools.partial(close_kernel, s),
+        (plane, f32(*dual_grad.shape), f32(*dual_sign.shape)),
+        [duals, sign, adjoint, coef, target, from_x, from_y],
+        back + [pltpu.SemaphoreType.DMA((4 * rows,))], 2_000_000_000,
+        out_specs=[vmem, hbm, hbm])
     coef_out, extra_out = call(
         functools.partial(last_kernel, s),
         (f32(count * rows, lanes), f32(count * rows, lanes)),

time: 33.8 us -> 33.2 us (0.982)
  waiting for transfers between devices: 6.07 us -> 5.36 us
    ppermute x5, waiting for transfers between devices: 1 us -> 0.29 us  [exchange(): lax.ppermute(send, axis, pairs)]
  transfers between devices with their start and end apart: 8 -> 8, of which waited for: 3 -> 3; matrix products, arithmetic and copies ran while one was open for 3% -> 3% of each run, Pallas kernels for 18% -> 20%
where the time goes in v6:
time: 33.2 us; the launch traced here: 33 us
  starting transfers between devices  14.2 us (43%)
  Pallas kernels  11.6 us (35%)
  waiting for transfers between devices  5.36 us (16%)
  local copies, waits for them, and re-layouts  0.96 us (3%)
  between operations  0.79 us (2%)
    pallas_call x5, Pallas kernels, call(): pl.pallas_call(kernel, out_shape=outs, in_specs=in_specs or [vmem] * len(...  11.6 us
    ppermute x5, starting transfers between devices, exchange(): lax.ppermute(send, axis, pairs)  5.51 us
    ppermute x2, starting transfers between devices, shift(): return lax.ppermute(value, axis, pairs)  4.81 us
    ppermute x1, starting transfers between devices, diagonal_exchange(): received.append(lax.ppermute(send, ('gx', 'gy'), flat))  3.91 us
    ppermute x1, waiting for transfers between devices, diagonal_exchange(): received.append(lax.ppermute(send, ('gx', 'gy'), flat))  3 us
    ppermute x2, waiting for transfers between devices, shift(): return lax.ppermute(value, axis, pairs)  2.07 us
    slice x1, local copies, waits for them, and re-layouts, per_device(): after_y = exchange('gy', [extrapolated[:, 0, 0]] * pairs_y)  0.95 us
  transfers between devices with their start and end apart: 8, of which 3 were waited for; matrix products, arithmetic and copies ran while one was open for 3% of the time, Pallas kernels for 20%

profile of v6, /device:TPU:24, one launch (start us, length us, event | category | flops | bytes accessed | tf_op | source)
XLA Modules:
  0.0 33.0 jit_solution(6106344353945465651)
XLA Ops:
  0.6 0.0 copy-start
  0.6 0.0 copy-start.2
  0.7 0.0 copy-start.1
  0.7 2.9 %collective-permute-start = (f32[45,1,8,128]{3,2,1,0:T(8,128)}, f32[45,1,8,128]{3,2,1,0:T(8,128)S(1)}, u32[]{:S(2)}, u32[]{:S(2)}) collective-permute-start(f32[45,1,8,128]{3,2,1,0:T(8,128)} %param.13), channel_id=1, source_target_pairs={{2,0},{4,2},{6,4},{8,6},{10,8},{12,10},{14,12},{16,14},{18,16},{20... | collective-permute-start | bytes 552968 | tf_op jit(solution)/shard_map/ppermute | solution.py:462
  3.6 0.9 %slice.3 = f32[45,1,1,128]{3,2,1,0:T(1,128)S(1)} slice(f32[45,1,8,128]{3,2,1,0:T(8,128)} %param.13), slice={[0:45], [0:1], [0:1], [0:128]} | slice | bytes 46080 | tf_op jit(solution)/shard_map/slice | solution.py:482
  4.5 1.6 %collective-permute-start.1 = (f32[45,128]{1,0:T(8,128)S(1)}, f32[45,128]{1,0:T(8,128)S(1)}, u32[]{:S(2)}, u32[]{:S(2)}) collective-permute-start(f32[45,128]{1,0:T(8,128)S(1)} %bitcast.20), channel_id=1, source_target_pairs={{0,1},{1,0},{2,3},{3,2},{4,5},{5,4},{6,7},{7,6},{8,9},{9,8},{10,11... | collective-permute-start | bytes 69128 | tf_op jit(solution)/shard_map/ppermute | solution.py:442
  6.1 3.2 %shard_map.111 = (f32[9960,128]{1,0:T(8,128)S(1)}, f32[3320,128]{1,0:T(8,128)S(1)}, f32[360,128]{1,0:T(8,128)S(1)}, bf16[368,176]{1,0:T(8,128)(2,1)S(1)}, bf16[9...) custom-call(f32[360,128]{1,0:T(8,128)} %bitcast.21, f32[45,362]{1,0:T(8,128)} %bitcast.24, f32[1,45]{1,0:T(1,128)} %bitcast.25, ...), custom_call_target="tpu_custom_call" | custom-call | flops 2000000000 | bytes 13389116 | tf_op jit(solution)/shard_map/pallas_call | solution.py:421
  9.2 0.0 collective-permute-done.1.refs_0_
  9.3 0.0 collective-permute-done
  9.3 0.0 copy-done
  9.3 0.0 copy-done.2
  9.3 0.0 copy-done.1
  9.3 2.1 %shard_map.112 = (f32[9960,128]{1,0:T(8,128)S(1)}, f32[48,1024]{1,0:T(8,128)S(1)}, f32[48,1024]{1,0:T(8,128)S(1)}, f32[48,1024]{1,0:T(8,128)S(1)}, f32[48,1024]{...) custom-call(f32[9960,128]{1,0:T(8,128)S(1)} %get-tuple-element.31.du, ...), custom_call_target="tpu_custom_call" | custom-call | flops 2000000000 | bytes 14338048 | tf_op jit(solution)/shard_map/pallas_call | solution.py:421
  11.4 0.1 collective-permute-start.2
  11.5 2.6 %collective-permute-start.3 = (f32[48,1024]{1,0:T(8,128)S(1)}, f32[48,1024]{1,0:T(8,128)S(1)}, u32[]{:S(2)}, u32[]{:S(2)}) collective-permute-start(f32[48,1024]{1,0:T(8,128)S(1)} %get-tuple-element.44), channel_id=1, source_target_pairs={{2,4},{4,2},{6,8},{8,6},{10,12},{12,10},{14,16},{16,14},{18,20},{2... | collective-permute-start | bytes 589832 | tf_op jit(solution)/shard_map/ppermute | solution.py:442
  14.0 1.2 %collective-permute-start.4 = (f32[48,128]{1,0:T(8,128)S(1)}, f32[48,128]{1,0:T(8,128)S(1)}, u32[]{:S(2)}, u32[]{:S(2)}) collective-permute-start(f32[48,128]{1,0:T(8,128)S(1)} %get-tuple-element.45), channel_id=1, source_target_pairs={{0,1},{1,0},{2,3},{3,2},{4,5},{5,4},{6,7},{7,6},{8,9},{9,8},{10,11... | collective-permute-start | bytes 73736 | tf_op jit(solution)/shard_map/ppermute | solution.py:442
  15.2 3.9 %collective-permute-start.5 = (f32[48,128]{1,0:T(8,128)S(1)}, f32[48,128]{1,0:T(8,128)S(1)}, u32[]{:S(2)}, u32[]{:S(2)}) collective-permute-start(f32[48,128]{1,0:T(8,128)S(1)} %get-tuple-element.46), channel_id=1, source_target_pairs={{2,1},{1,2},{4,3},{3,4},{6,5},{5,6},{8,7},{7,8},{10,9},{9,10},{12,... | collective-permute-start | bytes 73736 | tf_op jit(solution)/shard_map/ppermute | solution.py:455
  19.2 0.0 collective-permute-done.4.refs_2_
  19.2 3.0 %collective-permute-done.5.refs_3_ = f32[48,128]{1,0:T(8,128)S(1)} collective-permute-done((f32[48,128]{1,0:T(8,128)S(1)}, f32[48,128]{1,0:T(8,128)S(1)}, u32[]{:S(2)}, u32[]{:S(2)}) %collective-permute-start.5) | collective-permute-done | bytes 24608 | tf_op jit(solution)/shard_map/ppermute | solution.py:455
  22.2 0.0 collective-permute-done.2.refs_0_
  22.2 0.0 collective-permute-done.3.refs_1_
  22.2 2.0 %shard_map.113 = (f32[9960,128]{1,0:T(8,128)S(1)}, f32[3320,128]{1,0:T(8,128)S(1)}, f32[48,1024]{1,0:T(8,128)S(1)}, f32[48,1024]{1,0:T(8,128)S(1)}, f32[48,128]{1,0:T(8,128)S(1)}) custom-call(f32[9960,128]{1,0:T(8,128)S(1)} %get-tuple-element.37.dual_in, f32[3320,128]{1,0:T(8,128)S(1)} %get-tuple-element.32.sign_in, ...), custom_call_target="tpu_custom_call" | custom-call | flops 2000000000 | bytes 15494656 | tf_op jit(solution)/shard_map/pallas_call | solution.py:421
  24.2 1.9 %collective-permute-start.6 = (f32[48,1024]{1,0:T(8,128)S(1)}, f32[48,1024]{1,0:T(8,128)S(1)}, u32[]{:S(2)}, u32[]{:S(2)}) collective-permute-start(f32[48,1024]{1,0:T(8,128)S(1)} %get-tuple-element.51.x_ref), channel_id=1, source_target_pairs={{0,2},{2,4},{4,6},{6,8},{8,10},{10,12},{12,14},{14,16},{16,18},{18... | collective-permute-start | bytes 589832 | tf_op jit(solution)/shard_map/ppermute | solution.py:462
  26.2 0.1 collective-permute-start.7
  26.3 3.5 %shard_map.114 = (f32[48,1024]{1,0:T(8,128)S(1)}, f32[3,362,1,8,128]{4,3,2,1,0:T(8,128)}, f32[362,1,8,128]{3,2,1,0:T(8,128)}) custom-call(f32[9960,128]{1,0:T(8,128)S(1)} %get-tuple-element.47.dual_ref, f32[3320,128]{1,0:T(8,128)S(1)} %get-tuple-element.48.sign_in, bf16[96,368]{1,0:T(8,128)(2,1)S(1)} %get-tuple-element.34.adjoint_ref, ...), custom_call_target="tpu_custom_call" | custom-call | flops 2000000000 | bytes 13612032 | tf_op jit(solution)/shard_map/pallas_call | solution.py:421
  29.8 0.3 collective-permute-done.7.refs_0_
  30.0 2.1 %collective-permute-done.6.x_ref = f32[48,1024]{1,0:T(8,128)S(1)} collective-permute-done((f32[48,1024]{1,0:T(8,128)S(1)}, f32[48,1024]{1,0:T(8,128)S(1)}, u32[]{:S(2)}, u32[]{:S(2)}) %collective-permute-start.6) | collective-permute-done | bytes 196640 | tf_op jit(solution)/shard_map/ppermute | solution.py:462
  32.1 0.8 %shard_map.115 = (f32[360,128]{1,0:T(8,128)}, f32[360,128]{1,0:T(8,128)}) custom-call(f32[48,1024]{1,0:T(8,128)S(1)} %get-tuple-element.53.base_ref, f32[48,1024]{1,0:T(8,128)S(1)} %get-tuple-element.39.inverse_ref, f32[48,1024]{1,0:T(8,128)S(1)} %get-tuple-element.49.coef_ref, f32[48,1024]{1,0:T(8,128)S(1)} %collective-permute-done.6.x_ref, ...), custom_call_target="tpu_custom_call" | custom-call | flops 1000000 | bytes 1179648 | tf_op jit(solution)/shard_map/pallas_call | solution.py:421
  (1 shorter events, 0.0 us)
Async XLA Ops:
  0.6 8.6 %copy-start = (f32[45,1,8,128]{3,2,1,0:T(8,128)S(1)}, f32[45,1,8,128]{3,2,1,0:T(8,128)}, u32[]{:S(2)}) copy-start(f32[45,1,8,128]{3,2,1,0:T(8,128)} %param.12) | copy-start | bytes 552964
  0.6 8.6 %copy-start.2 = (s32[1,8,128]{2,1,0:T(8,128)S(1)}, s32[1,8,128]{2,1,0:T(8,128)}, u32[]{:S(2)}) copy-start(s32[1,8,128]{2,1,0:T(8,128)} %param.11) | copy-start | bytes 12292
  0.7 8.6 %copy-start.1 = (f32[45,1,8,128]{3,2,1,0:T(8,128)S(1)}, f32[45,1,8,128]{3,2,1,0:T(8,128)}, u32[]{:S(2)}) copy-start(f32[45,1,8,128]{3,2,1,0:T(8,128)} %param.8) | copy-start | bytes 552964
  0.7 8.6 %collective-permute-start = (f32[45,1,8,128]{3,2,1,0:T(8,128)}, f32[45,1,8,128]{3,2,1,0:T(8,128)S(1)}, u32[]{:S(2)}, u32[]{:S(2)}) collective-permute-start(f32[45,1,8,128]{3,2,1,0:T(8,128)} %param.13), channel_id=1, source_target_pairs={{2,0},{4,2},{6,4},{8,6},{10,8},{12,10},{14,12},{16,14},{18,16},{20... | collective-permute-start | bytes 552968 | tf_op jit(solution)/shard_map/ppermute | solution.py:462
  4.5 4.7 %collective-permute-start.1 = (f32[45,128]{1,0:T(8,128)S(1)}, f32[45,128]{1,0:T(8,128)S(1)}, u32[]{:S(2)}, u32[]{:S(2)}) collective-permute-start(f32[45,128]{1,0:T(8,128)S(1)} %bitcast.20), channel_id=1, source_target_pairs={{0,1},{1,0},{2,3},{3,2},{4,5},{5,4},{6,7},{7,6},{8,9},{9,8},{10,11... | collective-permute-start | bytes 69128 | tf_op jit(solution)/shard_map/ppermute | solution.py:442
  11.4 10.8 %collective-permute-start.2 = (f32[48,1024]{1,0:T(8,128)S(1)}, f32[48,1024]{1,0:T(8,128)S(1)}, u32[]{:S(2)}, u32[]{:S(2)}) collective-permute-start(f32[48,1024]{1,0:T(8,128)S(1)} %get-tuple-element.43), channel_id=1, source_target_pairs={{0,2},{2,0},{4,6},{6,4},{8,10},{10,8},{12,14},{14,12},{16,18},{18,... | collective-permute-start | bytes 589832 | tf_op jit(solution)/shard_map/ppermute | solution.py:442
  11.5 10.7 %collective-permute-start.3 = (f32[48,1024]{1,0:T(8,128)S(1)}, f32[48,1024]{1,0:T(8,128)S(1)}, u32[]{:S(2)}, u32[]{:S(2)}) collective-permute-start(f32[48,1024]{1,0:T(8,128)S(1)} %get-tuple-element.44), channel_id=1, source_target_pairs={{2,4},{4,2},{6,8},{8,6},{10,12},{12,10},{14,16},{16,14},{18,20},{2... | collective-permute-start | bytes 589832 | tf_op jit(solution)/shard_map/ppermute | solution.py:442
  14.0 5.1 %collective-permute-start.4 = (f32[48,128]{1,0:T(8,128)S(1)}, f32[48,128]{1,0:T(8,128)S(1)}, u32[]{:S(2)}, u32[]{:S(2)}) collective-permute-start(f32[48,128]{1,0:T(8,128)S(1)} %get-tuple-element.45), channel_id=1, source_target_pairs={{0,1},{1,0},{2,3},{3,2},{4,5},{5,4},{6,7},{7,6},{8,9},{9,8},{10,11... | collective-permute-start | bytes 73736 | tf_op jit(solution)/shard_map/ppermute | solution.py:442
  15.2 6.9 %collective-permute-start.5 = (f32[48,128]{1,0:T(8,128)S(1)}, f32[48,128]{1,0:T(8,128)S(1)}, u32[]{:S(2)}, u32[]{:S(2)}) collective-permute-start(f32[48,128]{1,0:T(8,128)S(1)} %get-tuple-element.46), channel_id=1, source_target_pairs={{2,1},{1,2},{4,3},{3,4},{6,5},{5,6},{8,7},{7,8},{10,9},{9,10},{12,... | collective-permute-start | bytes 73736 | tf_op jit(solution)/shard_map/ppermute | solution.py:455
  24.2 7.9 %collective-permute-start.6 = (f32[48,1024]{1,0:T(8,128)S(1)}, f32[48,1024]{1,0:T(8,128)S(1)}, u32[]{:S(2)}, u32[]{:S(2)}) collective-permute-start(f32[48,1024]{1,0:T(8,128)S(1)} %get-tuple-element.51.x_ref), channel_id=1, source_target_pairs={{0,2},{2,4},{4,6},{6,8},{8,10},{10,12},{12,14},{14,16},{16,18},{18... | collective-permute-start | bytes 589832 | tf_op jit(solution)/shard_map/ppermute | solution.py:462
  26.2 3.9 %collective-permute-start.7 = (f32[48,128]{1,0:T(8,128)S(1)}, f32[48,128]{1,0:T(8,128)S(1)}, u32[]{:S(2)}, u32[]{:S(2)}) collective-permute-start(f32[48,128]{1,0:T(8,128)S(1)} %get-tuple-element.52.y_ref), channel_id=1, source_target_pairs={{0,1},{1,0},{2,3},{3,2},{4,5},{5,4},{6,7},{7,6},{8,9},{9,8},{10,11... | collective-permute-start | bytes 73736 | tf_op jit(solution)/shard_map/ppermute | solution.py:442
